TPU v7x, 32 devices: a whole 2x2x4 slice. The times are simulated.
32 devices in a mesh: emb: 32 (over z, y, x, core).
Axes of the slice: x: 2, y: 2, z: 4, core: 2. Of those that a mesh axis runs over, the one named last changes fastest.
Arguments:
- token_ids: int32 [32768], P('emb')
- hot_ids: int32 [2048], replicated
- x_in: bfloat16 [32768, 1024], P('emb')
- d_out: bfloat16 [32768, 1024], P('emb')
- emb_table: bfloat16 [4, 50304, 1024], P(None, 'emb')
- hot_table: bfloat16 [4, 2048, 1024], replicated
- w_up: bfloat16 [4, 1024, 4096], replicated
- w_down: bfloat16 [4, 4096, 1024], replicated
- w_gate: bfloat16 [4, 1024, 1024], replicated
- w_proj: bfloat16 [4, 1024, 1024], replicated
Outputs:
- output 1: bfloat16 [32768, 1024], P('emb')
- output 2: float32 [4, 50304, 1024], P(None, 'emb')
- output 3: float32 [4, 2048, 1024], replicated
All inputs are finite; a program needn't handle non-finite values.
Results may differ from a plain program's by a relative error of at most 0.0156594.
Values are sent between devices in bfloat16 or wider.
A program may use at most 1 GiB of HBM per device.

v0:
```python
import functools

import jax
import jax.numpy as jnp
from jax import lax
from jax.experimental import pallas as pl
from jax.experimental.pallas import tpu as pltpu
from jax.sharding import PartitionSpec as P


NORM_EPS = 1e-6
FREQ_HOT = 112
FREQ_COLD = 16
FREQ = FREQ_HOT + FREQ_COLD
COLD_MAX = 256
GELU_A = 0.7978845608028654
GELU_B = GELU_A * 0.044715
VMEM = 66_000_000
ROWS = 256
LEVELS = (16, 20, 24, 28, 32, 40, 48, 64, 80, 96, 128, 160, 192, 256)
BF = jnp.bfloat16
F32 = jnp.float32


def gelu_back(pre_act, cot_in):
    _, pull = jax.vjp(jax.nn.gelu, pre_act.astype(F32))
    return pull(cot_in)[0]


def dot32(a, b):
    return jnp.dot(a, b, preferred_element_type=F32)


def dense_parts(resid, w_up, w_gate):
    resid_f = resid.astype(F32)
    inv_rms = lax.rsqrt(jnp.mean(resid_f * resid_f, axis=-1, keepdims=True) + NORM_EPS)
    normed = (resid_f * inv_rms).astype(BF)
    hidden = dot32(normed, w_up).astype(BF)
    gate_pre = dot32(normed, w_gate).astype(BF)
    return resid_f, inv_rms, hidden, gate_pre


def layer_forward(resid, emb_rows, w_up, w_down, w_gate, w_proj):
    resid_f, _, hidden, gate_pre = dense_parts(resid, w_up, w_gate)
    activated = jax.nn.gelu(hidden.astype(F32)).astype(BF)
    mlp_out = dot32(activated, w_down).astype(BF)
    gate = jax.nn.gelu(gate_pre.astype(F32)).astype(BF)
    mixed = (gate.astype(F32) * emb_rows.astype(F32)).astype(BF)
    projected = dot32(mixed, w_proj).astype(BF)
    return (resid_f + mlp_out.astype(F32) + projected.astype(F32)).astype(BF)


def layer_backward(resid, emb_rows, d_next, w_up, w_down, w_gate, w_proj):
    resid_f, inv_rms, hidden, gate_pre = dense_parts(resid, w_up, w_gate)
    gate = jax.nn.gelu(gate_pre.astype(F32)).astype(BF)
    d_cast = d_next.astype(BF)
    d_mixed = jnp.einsum('nd,ed->ne', d_cast, w_proj, preferred_element_type=F32)
    d_rows = gate.astype(F32) * d_mixed
    d_gpre = gelu_back(gate_pre, d_mixed * emb_rows.astype(F32))
    d_hidden = gelu_back(hidden, jnp.einsum('nd,fd->nf', d_cast, w_down, preferred_element_type=F32))
    d_normed = (jnp.einsum('nf,df->nd', d_hidden.astype(BF), w_up, preferred_element_type=F32)
                + jnp.einsum('ne,de->nd', d_gpre.astype(BF), w_gate, preferred_element_type=F32))
    inner = jnp.mean(d_normed * resid_f, axis=-1, keepdims=True)
    d_prev = d_next + inv_rms * d_normed - resid_f * (inv_rms * inv_rms * inv_rms) * inner
    return d_prev, d_rows


def general_path(n_dev, my_index, token_ids, hot_ids, x_in, d_out, emb_table, hot_table, w_up, w_down, w_gate, w_proj):
    n_loc = token_ids.shape[0]
    _, rows_dev, emb_dim = emb_table.shape
    capacity = max(8, (2 * n_loc) // n_dev)
    n_slots = n_dev * capacity
    hot_match = token_ids[:, None] == hot_ids[None, :]
    is_hot = jnp.any(hot_match, axis=1)
    hot_pick = hot_match.astype(BF)
    hot_pick_f = hot_match.astype(F32)
    owner_id = token_ids // rows_dev
    to_owner = (owner_id[:, None] == jnp.arange(n_dev, dtype=jnp.int32)[None, :]) & jnp.logical_not(is_hot)[:, None]
    owner_rank = jnp.cumsum(to_owner.astype(jnp.int32), axis=0) - 1
    place = jnp.sum(jnp.where(to_owner, owner_rank, 0), axis=1)
    slot = jnp.where(is_hot, n_slots, owner_id * capacity + place)
    send_ids = jnp.full((n_slots,), -1, jnp.int32).at[slot].set(token_ids, mode='drop')
    slot_tok = jnp.full((n_slots,), -1, jnp.int32).at[slot].set(jnp.arange(n_loc, dtype=jnp.int32), mode='drop')
    recv_ids = lax.all_to_all(send_ids.reshape(n_dev, capacity), 'emb', 0, 0, tiled=True).reshape(n_slots)
    served_ok = recv_ids >= 0
    local_row = jnp.where(served_ok, recv_ids - my_index * rows_dev, 0)
    pick_slot = jnp.minimum(slot, n_slots - 1)
    slot_used = slot_tok >= 0
    slot_src = jnp.maximum(slot_tok, 0)

    def fwd(resid, per_layer):
        table, hot_l, up, down, gate_w, proj = per_layer
        served = jnp.take(table, local_row, axis=0)
        fetched = lax.all_to_all(served.reshape(n_dev, capacity, emb_dim), 'emb', 0, 0, tiled=True).reshape(n_slots, emb_dim)
        cold_rows = jnp.take(fetched, pick_slot, axis=0)
        hot_rows = dot32(hot_pick, hot_l).astype(BF)
        emb_rows = jnp.where(is_hot[:, None], hot_rows, cold_rows)
        return layer_forward(resid, emb_rows, up, down, gate_w, proj), (resid, emb_rows)

    x_out, (x_saved, rows_saved) = lax.scan(fwd, x_in, (emb_table, hot_table, w_up, w_down, w_gate, w_proj))

    def bwd(d_resid, per_layer):
        resid_l, rows_l, up, down, gate_w, proj = per_layer
        d_resid, d_rows = layer_backward(resid_l, rows_l, d_resid, up, down, gate_w, proj)
        outgoing = jnp.where(slot_used[:, None], jnp.take(d_rows, slot_src, axis=0), 0.0)
        incoming = lax.all_to_all(outgoing.reshape(n_dev, capacity, emb_dim), 'emb', 0, 0, tiled=True).reshape(n_slots, emb_dim)
        d_tab = jax.ops.segment_sum(jnp.where(served_ok[:, None], incoming, 0.0), local_row, num_segments=rows_dev)
        hot_local = jnp.einsum('nh,ne->he', hot_pick_f, d_rows, precision=lax.Precision.HIGHEST, preferred_element_type=F32)
        return d_resid, (d_tab, lax.psum(hot_local, 'emb'))

    _, (d_table, d_hot) = lax.scan(bwd, d_out.astype(F32), (x_saved, rows_saved, w_up, w_down, w_gate, w_proj), reverse=True)
    return x_out, d_table, d_hot


def split3(v):
    hi = v.astype(BF)
    rest = v - hi.astype(F32)
    mid = rest.astype(BF)
    return hi, mid, (rest - mid.astype(F32)).astype(BF)


def iota(shape, dim):
    return lax.broadcasted_iota(jnp.int32, shape, dim)


def one_hot(v, n, dtype=BF):
    return (v[:, None] == iota((v.shape[0], n), 1)).astype(dtype)


def dot_nt(a, b):
    return lax.dot_general(a, b, (((1,), (1,)), ((), ())), preferred_element_type=F32)


def gelu(x):
    half = 0.5 * x
    return half + half * jnp.tanh(x * (GELU_A + GELU_B * (x * x)))


def gelu_slope(x):
    sq = x * x
    th = jnp.tanh(x * (GELU_A + GELU_B * sq))
    return (0.5 + 0.5 * th) + (0.5 * x) * (1.0 - th * th) * (GELU_A + (3.0 * GELU_B) * sq)


def forward_kernel(n_l, n_f, x0, cls, table, wu, wd, wg, wp, xs, hs, ss, xo, x_now, u_now, acc, q_now):
    layer, step = pl.program_id(0), pl.program_id(1)
    n_tok = x_now.shape[0]
    parts = [pl.ds(m, ROWS) for m in range(0, n_tok, ROWS)]

    @pl.when((layer == 0) & (step == 0))
    def _():
        x_now[...] = x0[...]

    @pl.when(step == 0)
    def _():
        for m in parts:
            xb = x_now[m, :]
            x = xb.astype(F32)
            xs[0, m, :] = xb
            u = (x * lax.rsqrt(jnp.mean(x * x, axis=-1, keepdims=True) + NORM_EPS)).astype(BF)
            u_now[m, :] = u
            s = dot32(u, wg[0]).astype(BF)
            ss[0, m, :] = s
            g = gelu(s.astype(F32)).astype(BF)
            pick = (cls[m, :] == iota((ROWS, table.shape[1]), 1)).astype(BF)
            e = dot32(pick, table[0]).astype(BF)
            mixed = (g.astype(F32) * e.astype(F32)).astype(BF)
            q_now[m, :] = dot32(mixed, wp[0]).astype(BF)
            acc[m, :] = jnp.zeros((ROWS, acc.shape[1]), F32)

    for m in parts:
        h = dot32(u_now[m, :], wu[0]).astype(BF)
        hs[0, m, :] = h
        act = gelu(h.astype(F32)).astype(BF)
        acc[m, :] += dot32(act, wd[0])

    @pl.when(step == n_f - 1)
    def _():
        for m in parts:
            x = x_now[m, :].astype(F32) + acc[m, :].astype(BF).astype(F32) + q_now[m, :].astype(F32)
            x_now[m, :] = x.astype(BF)

    @pl.when((step == n_f - 1) & (layer == n_l - 1))
    def _():
        xo[...] = x_now[...]


def forward(x0, cls, table, w_up, w_down, w_gate, w_proj):
    n_tok, dim = x0.shape
    n_l, _, ff = w_up.shape
    emb = w_gate.shape[2]
    tile = min(512, ff)
    n_f = ff // tile
    n_c = table.shape[1]
    flops = n_l * 2 * n_tok * dim * (2 * ff + 2 * emb + n_c)
    return pl.pallas_call(
        functools.partial(forward_kernel, n_l, n_f),
        grid=(n_l, n_f),
        in_specs=[
            pl.BlockSpec((n_tok, dim), lambda l, f: (0, 0)),
            pl.BlockSpec((n_tok, 1), lambda l, f: (0, 0)),
            pl.BlockSpec((1, n_c, emb), lambda l, f: (l, 0, 0)),
            pl.BlockSpec((1, dim, tile), lambda l, f: (l, 0, f)),
            pl.BlockSpec((1, tile, dim), lambda l, f: (l, f, 0)),
            pl.BlockSpec((1, dim, emb), lambda l, f: (l, 0, 0)),
            pl.BlockSpec((1, emb, dim), lambda l, f: (l, 0, 0)),
        ],
        out_specs=[
            pl.BlockSpec((1, n_tok, dim), lambda l, f: (l, 0, 0)),
            pl.BlockSpec((1, n_tok, tile), lambda l, f: (l, 0, f)),
            pl.BlockSpec((1, n_tok, emb), lambda l, f: (l, 0, 0)),
            pl.BlockSpec((n_tok, dim), lambda l, f: (0, 0)),
        ],
        out_shape=[
            jax.ShapeDtypeStruct((n_l, n_tok, dim), BF),
            jax.ShapeDtypeStruct((n_l, n_tok, ff), BF),
            jax.ShapeDtypeStruct((n_l, n_tok, emb), BF),
            jax.ShapeDtypeStruct((n_tok, dim), BF),
        ],
        scratch_shapes=[pltpu.VMEM((n_tok, dim), BF), pltpu.VMEM((n_tok, dim), BF),
                        pltpu.VMEM((n_tok, dim), F32), pltpu.VMEM((n_tok, dim), BF)],
        compiler_params=pltpu.CompilerParams(vmem_limit_bytes=VMEM, dimension_semantics=("arbitrary", "arbitrary")),
        cost_estimate=pl.CostEstimate(flops=flops, bytes_accessed=n_l * 40_000_000, transcendentals=0),
        name="forward",
    )(x0, cls, table, w_up, w_down, w_gate, w_proj)


def backward_kernel(n_l, n_f, last_full, r_in, cls, cls_t, table, xs, hs, ss, wu, wd, wg, wp, sums, r, c_now, acc, three):
    step = pl.program_id(0)
    index, f = step // n_f, step % n_f
    n_tok = c_now.shape[0]
    parts = [pl.ds(m, ROWS) for m in range(0, n_tok, ROWS)]
    goes_on = True if last_full else index < n_l - 1

    @pl.when(step == 0)
    def _():
        r[...] = r_in[...].astype(F32)

    @pl.when(f == 0)
    def _():
        for m in parts:
            c = r[m, :].astype(BF)
            c_now[m, :] = c
            a = dot_nt(c, wp[0])
            s = ss[0, m, :].astype(F32)
            rows = gelu(s).astype(BF).astype(F32) * a
            for i, part in enumerate(split3(rows)):
                three[i, m, :] = part
            pick = (cls[m, :] == iota((ROWS, table.shape[1]), 1)).astype(BF)
            e = dot32(pick, table[0])
            ds = (gelu_slope(s) * (a * e)).astype(BF)
            acc[m, :] = dot_nt(ds, wg[0])
        pick_t = (cls_t[...] == iota((table.shape[1], n_tok), 0)).astype(BF)
        sums[0] = dot32(pick_t, three[0]) + (dot32(pick_t, three[1]) + dot32(pick_t, three[2]))

    @pl.when(goes_on)
    def _():
        for m in parts:
            d_act = dot_nt(c_now[m, :], wd[0])
            dh = (gelu_slope(hs[0, m, :].astype(F32)) * d_act).astype(BF)
            acc[m, :] += dot_nt(dh, wu[0])

    @pl.when((f == n_f - 1) & goes_on)
    def _():
        for m in parts:
            x = xs[0, m, :].astype(F32)
            k = lax.rsqrt(jnp.mean(x * x, axis=-1, keepdims=True) + NORM_EPS)
            du = acc[m, :]
            inner = jnp.mean(du * x, axis=-1, keepdims=True)
            r[m, :] = r[m, :] + k * du - x * (k * k * k) * inner


def backward(first, n_l, last_full, r_in, cls, cls_t, table, xs, hs, ss, w_up, w_down, w_gate, w_proj):
    n_tok, dim = r_in.shape
    ff = w_up.shape[2]
    emb = w_gate.shape[2]
    tile = min(512, ff)
    n_f = ff // tile
    n_c = table.shape[1]
    n_steps = n_l * n_f if last_full else (n_l - 1) * n_f + 1

    def whole(t):
        return (first - t // n_f, 0, 0)

    def cols(t):
        return (first - t // n_f, 0, t % n_f)

    def rows(t):
        return (first - t // n_f, t % n_f, 0)

    once = pl.Buffered(1)
    return pl.pallas_call(
        functools.partial(backward_kernel, n_l, n_f, last_full),
        grid=(n_steps,),
        in_specs=[
            pl.BlockSpec((n_tok, dim), lambda t: (0, 0), pipeline_mode=once),
            pl.BlockSpec((n_tok, 1), lambda t: (0, 0), pipeline_mode=once),
            pl.BlockSpec((1, n_tok), lambda t: (0, 0), pipeline_mode=once),
            pl.BlockSpec((1, n_c, emb), whole),
            pl.BlockSpec((1, n_tok, dim), whole),
            pl.BlockSpec((1, n_tok, tile), cols),
            pl.BlockSpec((1, n_tok, emb), whole),
            pl.BlockSpec((1, dim, tile), cols),
            pl.BlockSpec((1, tile, dim), rows),
            pl.BlockSpec((1, dim, emb), whole),
            pl.BlockSpec((1, emb, dim), whole),
        ],
        out_specs=[
            pl.BlockSpec((1, n_c, emb), lambda t: (t // n_f, 0, 0)),
            pl.BlockSpec((n_tok, dim), lambda t: (0, 0)),
        ],
        out_shape=[
            jax.ShapeDtypeStruct((n_l, n_c, emb), F32),
            jax.ShapeDtypeStruct((n_tok, dim), F32),
        ],
        scratch_shapes=[pltpu.VMEM((n_tok, dim), BF), pltpu.VMEM((n_tok, dim), F32), pltpu.VMEM((3, n_tok, emb), BF)],
        compiler_params=pltpu.CompilerParams(vmem_limit_bytes=VMEM, dimension_semantics=("arbitrary",)),
        cost_estimate=pl.CostEstimate(flops=n_l * 2 * n_tok * dim * (2 * ff + 2 * emb + 4 * n_c),
                                      bytes_accessed=n_l * 40_000_000, transcendentals=0),
        name="backward",
    )(r_in, cls, cls_t, table, xs, hs, ss, w_up, w_down, w_gate, w_proj)


def count_kernel(ids, out):
    n_hi = out.shape[0]
    n_tok = ids.shape[1]
    out[...] = jnp.zeros(out.shape, F32)

    @pl.loop(0, ids.shape[0])
    def _(i):
        row = ids[pl.ds(i, 1), :]
        hi = ((row >> 8) == iota((n_hi, n_tok), 0)).astype(BF)
        lo = ((row & 255) == iota((256, n_tok), 0)).astype(BF)
        out[...] += dot_nt(hi, lo)


def count_ids(ids, n_hi):
    return pl.pallas_call(count_kernel, out_shape=jax.ShapeDtypeStruct((n_hi, 256), F32),
                          compiler_params=pltpu.CompilerParams(vmem_limit_bytes=VMEM), name="count_ids")(ids)


def pack_kernel(row_of, table, out, sem):
    @pl.loop(0, out.shape[0])
    def _(k):
        pltpu.make_async_copy(table.at[row_of[k]], out.at[k], sem).start()

    pltpu.make_async_copy(table.at[pl.ds(0, out.shape[0])], out, sem).wait()


def pack_rows(row_of, table):
    n = row_of.shape[0]
    return pl.pallas_call(
        pack_kernel,
        grid_spec=pltpu.PrefetchScalarGridSpec(
            num_scalar_prefetch=1, grid=(1,),
            in_specs=[pl.BlockSpec(memory_space=pl.ANY)],
            out_specs=pl.BlockSpec((n,) + table.shape[1:], lambda i, *_: (0, 0, 0)),
            scratch_shapes=[pltpu.SemaphoreType.DMA(())]),
        out_shape=jax.ShapeDtypeStruct((n,) + table.shape[1:], table.dtype),
        compiler_params=pltpu.CompilerParams(vmem_limit_bytes=VMEM), name="pack_rows",
    )(row_of, table)


def gather_kernel(mine, out, own, z_s, z_r, x_s, x_r, y_s, y_r, fx_s, fx_r, fy_s, fy_r,
                  c_s, c_r, cx_s, cx_r, cy_s, cy_r, cd_s, cd_r):
    me = lax.axis_index('emb')
    core, x, y, z = me % 2, (me // 2) % 2, (me // 4) % 2, me // 8
    half = mine.shape[0] // 2
    first, second = pl.ds(0, half), pl.ds(half, half)

    def dev(z, y, x, core):
        return z * 8 + y * 4 + x * 2 + core

    def copy(src, dst, send, recv, k, to):
        return pltpu.make_async_remote_copy(src_ref=src, dst_ref=dst, send_sem=send.at[k], recv_sem=recv.at[k],
                                            device_id=(to,), device_id_type=pl.DeviceIdType.MESH)

    to_x, to_y, to_core = dev(z, y, 1 - x, core), dev(z, 1 - y, x, core), dev(z, y, x, 1 - core)
    barrier = pltpu.get_barrier_semaphore()
    peers = [dev((z + k) % 4, y, x, core) for k in range(1, 4)] + [to_x, to_y, to_core]
    for peer in peers:
        pl.semaphore_signal(barrier, inc=1, device_id=(peer,), device_id_type=pl.DeviceIdType.MESH)
    pl.semaphore_wait(barrier, len(peers))

    keep = pltpu.make_async_copy(mine, out.at[me], own)
    keep.start()
    sent = []

    def send(*args):
        c = copy(*args)
        c.start()
        sent.append(c)

    def got(block, recv, send_sem, k):
        copy(block, block, send_sem, recv, k, to_x).wait_recv()

    for k in range(1, 4):
        send(mine, out.at[me], z_s, z_r, k, dev((z + k) % 4, y, x, core))

    def column(k):
        at = dev((z - k + 4) % 4, y, x, core)
        if k:
            got(out.at[at], z_r, z_s, k)
        src = out.at[at] if k else mine
        send(src, out.at[at], x_s, x_r, k, to_x)
        send(src, out.at[at], y_s, y_r, k, to_y)
        send(src, out.at[at], c_s, c_r, k, to_core)

    def onward(k):
        zk = (z - k + 4) % 4
        bx, by = dev(zk, y, 1 - x, core), dev(zk, 1 - y, x, core)
        got(out.at[bx], x_r, x_s, k)
        send(out.at[bx, first], out.at[bx, first], fy_s, fy_r, k, to_y)
        send(out.at[bx], out.at[bx], cx_s, cx_r, k, to_core)
        got(out.at[by], y_r, y_s, k)
        send(out.at[by, second], out.at[by, second], fx_s, fx_r, k, to_x)
        send(out.at[by], out.at[by], cy_s, cy_r, k, to_core)

    def across(k):
        bd = dev((z - k + 4) % 4, 1 - y, 1 - x, core)
        got(out.at[bd, first], fy_r, fy_s, k)
        got(out.at[bd, second], fx_r, fx_s, k)
        send(out.at[bd], out.at[bd], cd_s, cd_r, k, to_core)

    column(0)
    column(1)
    onward(0)
    column(2)
    onward(1)
    column(3)
    onward(2)
    across(0)
    onward(3)
    across(1)
    across(2)
    across(3)
    for k in range(4):
        zk = (z - k + 4) % 4
        got(out.at[dev(zk, y, x, 1 - core)], c_r, c_s, k)
        got(out.at[dev(zk, y, 1 - x, 1 - core)], cx_r, cx_s, k)
        got(out.at[dev(zk, 1 - y, x, 1 - core)], cy_r, cy_s, k)
        got(out.at[dev(zk, 1 - y, 1 - x, 1 - core)], cd_r, cd_s, k)
    for c in sent:
        c.wait_send()
    keep.wait()


def gather_all(mine, n_dev):
    n = mine.shape[0]
    return pl.pallas_call(
        gather_kernel,
        in_specs=[pl.BlockSpec(memory_space=pltpu.VMEM)],
        out_specs=pl.BlockSpec(memory_space=pl.ANY),
        out_shape=jax.ShapeDtypeStruct((n_dev,) + mine.shape, mine.dtype),
        scratch_shapes=[pltpu.SemaphoreType.DMA(())] + [pltpu.SemaphoreType.DMA((4,))] * 18,
        compiler_params=pltpu.CompilerParams(collective_id=0, has_side_effects=True, vmem_limit_bytes=VMEM),
        cost_estimate=pl.CostEstimate(flops=80_000_000_000, bytes_accessed=n_dev * n * 4096, transcendentals=0),
        name="gather_all",
    )(mine)


def hot_kernel(n_dev, raw, freq, code, into, out):
    n_r = raw.shape[1]
    n = n_r * n_dev
    row = iota((n, n), 0)
    order = (iota((n, n), 1) == (row % n_dev) * n_r + row // n_dev).astype(BF)
    sel = (code[0] == iota((n, freq.shape[1]), 1)).astype(BF)
    got = [dot32(order, p) for p in split3(raw[...].reshape(n, raw.shape[2]))]
    more = [dot32(sel, p) for p in split3(freq[0])]
    out[0] = (got[0] + (got[1] + got[2])) + (more[0] + (more[1] + more[2]))


def hot_out(first, n_l, gathered, freq, code, into):
    n_dev, _, emb = gathered.shape
    n_r = 8
    width = n_r * n_dev
    blocks = into.shape[1] // width
    return pl.pallas_call(
        functools.partial(hot_kernel, n_dev),
        grid=(n_l, blocks),
        in_specs=[
            pl.BlockSpec((n_dev, n_r, emb), lambda i, b: (0, i * blocks + b, 0)),
            pl.BlockSpec((1, freq.shape[1], emb), lambda i, b: (i, 0, 0)),
            pl.BlockSpec((1, width, 1), lambda i, b: (b, 0, 0)),
            pl.BlockSpec(memory_space=pl.ANY),
        ],
        out_specs=pl.BlockSpec((1, width, emb), lambda i, b: (first - i, b, 0)),
        out_shape=jax.ShapeDtypeStruct(into.shape, F32),
        input_output_aliases={3: 0},
        compiler_params=pltpu.CompilerParams(vmem_limit_bytes=VMEM, dimension_semantics=("arbitrary", "arbitrary")),
        cost_estimate=pl.CostEstimate(flops=20_000_000_000, bytes_accessed=n_l * 16_000_000, transcendentals=0),
        name="hot_out",
    )(gathered, freq, code.reshape(blocks, width, 1), into)


def empty_kernel(out):
    pass


def empty(shape):
    return pl.pallas_call(empty_kernel, out_specs=pl.BlockSpec(memory_space=pl.ANY),
                          out_shape=jax.ShapeDtypeStruct(shape, F32), name="empty")()


def table_kernel(at0, starts, row_of, *refs):
    srcs, out = refs[:-1], refs[-1]
    block = pl.program_id(0)
    n_rows = out.shape[0]
    out[...] = jnp.zeros(out.shape, F32)

    @pl.loop(starts[block], starts[block + 1])
    def _(k):
        at = row_of[k] - block * n_rows
        for l, src in enumerate(srcs):
            out[at, pl.ds(l, 1), :] = src[0, pl.ds(at0 + k, 1), :]


def table_out(rows_dev, at0, starts, row_of, srcs, n_blocks):
    n_l = len(srcs)
    _, n_c, emb = srcs[0][0].shape
    n_rows = rows_dev // n_blocks

    def spec(i):
        return pl.BlockSpec((1, n_c, emb), lambda b, *_: (i, 0, 0))

    return pl.pallas_call(
        functools.partial(table_kernel, at0),
        grid_spec=pltpu.PrefetchScalarGridSpec(
            num_scalar_prefetch=2, grid=(n_blocks,),
            in_specs=[spec(i) for _, i in srcs],
            out_specs=pl.BlockSpec((n_rows, n_l, emb), lambda b, *_: (b, 0, 0))),
        out_shape=jax.ShapeDtypeStruct((rows_dev, n_l, emb), F32),
        compiler_params=pltpu.CompilerParams(vmem_limit_bytes=VMEM, dimension_semantics=("arbitrary",)),
        cost_estimate=pl.CostEstimate(flops=12_000_000_000, bytes_accessed=rows_dev * n_l * emb * 4, transcendentals=0),
        name="table_out",
    )(starts, row_of, *[s for s, _ in srcs])


def row_kernel(at, row, into, out, sem):
    @pl.when(at[0] >= 0)
    def _():
        c = pltpu.make_async_copy(row, out.at[pl.ds(at[0], 1)], sem)
        c.start()
        c.wait()


def put_row(at, row, into):
    return pl.pallas_call(
        row_kernel,
        in_specs=[pl.BlockSpec(memory_space=pltpu.SMEM), pl.BlockSpec(memory_space=pltpu.VMEM), pl.BlockSpec(memory_space=pl.ANY)],
        out_specs=pl.BlockSpec(memory_space=pl.ANY),
        out_shape=jax.ShapeDtypeStruct(into.shape, F32),
        scratch_shapes=[pltpu.SemaphoreType.DMA(())],
        input_output_aliases={2: 0}, name="put_row",
    )(at, row, into)


def solution(mesh):
    n_dev = mesh.shape['emb']

    def body(token_ids, hot_ids, x_in, d_out, emb_table, hot_table, w_up, w_down, w_gate, w_proj):
        n_loc = token_ids.shape[0]
        layers, rows_dev, emb_dim = emb_table.shape
        n_hot = hot_ids.shape[0]
        places = n_loc // n_dev
        hot_dev = n_hot // n_dev
        vocab = rows_dev * n_dev
        n_hi = -(-vocab // 2048) * 8
        me = lax.axis_index('emb')
        per_dev = FREQ // n_dev
        hot_at, cold_at = FREQ, FREQ + hot_dev

        def swap(v):
            return lax.all_to_all(v, 'emb', 0, 0, tiled=True)

        def exchange(v):
            return swap(v.reshape(n_dev, places, -1)).reshape(n_loc, -1)

        count = count_ids(swap(jnp.broadcast_to(token_ids[None, :], (n_dev, n_loc))), n_hi)
        tok_hi = one_hot(token_ids >> 8, n_hi)
        tok_lo = one_hot(token_ids & 255, 256)
        hot_hi = one_hot(hot_ids >> 8, n_hi)
        hot_lo = one_hot(hot_ids & 255, 256)
        slot_no = jnp.arange(n_hot, dtype=jnp.int32)
        q_map = dot32(hot_hi.T, hot_lo * (slot_no // n_dev + 1).astype(BF)[:, None]).astype(BF)
        r_map = dot32(hot_hi.T, hot_lo * (slot_no % n_dev).astype(BF)[:, None]).astype(BF)
        levels = jnp.array(LEVELS, F32)
        upper = (iota((256, 256), 0) < iota((256, 256), 1)).astype(BF)

        def number(mask, most):
            kept = jnp.where(mask, count, 0.0)
            n_over = jnp.sum((kept[:, :, None] >= levels).astype(F32), axis=(0, 1))
            level = jnp.min(jnp.where(n_over <= most, levels, 1e9))
            flag = kept >= level
            per_row = jnp.sum(flag.astype(F32), axis=1)
            before = jnp.sum(jnp.where(iota((n_hi, n_hi), 0) > iota((n_hi, n_hi), 1), per_row[None, :], 0.0), axis=1)
            return jnp.where(flag, dot32(flag.astype(BF), upper) + before[:, None] + 1.0, 0.0)

        is_hot_map = q_map > 0
        hot_no = number(is_hot_map, FREQ_HOT)
        cold_no = number(jnp.logical_not(is_hot_map), FREQ_COLD)
        freq_map = jnp.where(hot_no > 0, hot_no, jnp.where(cold_no > 0, FREQ_HOT + cold_no, 0.0)).astype(BF)
        id_map = iota((n_hi, 256), 0) * 256 + iota((n_hi, 256), 1)
        cold_id = jnp.sum(jnp.where(cold_no.astype(jnp.int32)[None] == iota((FREQ_COLD, 1, 1), 0) + 1, id_map[None] + 1, 0), axis=(1, 2)) - 1

        def look(hi, lo, *maps):
            got = dot32(hi, jnp.concatenate(maps, axis=1))
            return [jnp.sum(got[:, i * 256:(i + 1) * 256] * lo.astype(F32), axis=1).astype(jnp.int32) for i in range(len(maps))]

        tok_f, tok_q, tok_r = look(tok_hi, tok_lo, freq_map, q_map, r_map)
        (hot_f,) = look(hot_hi, hot_lo, freq_map)
        row_ids = me * rows_dev + jnp.arange(rows_dev, dtype=jnp.int32)
        row_f, row_q, row_n = look(one_hot(row_ids >> 8, n_hi), one_hot(row_ids & 255, 256),
                                   freq_map, q_map, (count > 0).astype(BF))

        rare = tok_f == 0
        owner = jnp.where(tok_q > 0, tok_r, token_ids // rows_dev)
        to_dev = (owner[:, None] == iota((n_loc, n_dev), 1)) & rare[:, None]
        marks = jnp.concatenate([to_dev.astype(BF), jnp.logical_not(rare).astype(BF)[:, None]], axis=1)
        earlier = (iota((n_loc, n_loc), 0) > iota((n_loc, n_loc), 1)).astype(BF)
        ranks = dot32(earlier, marks)
        sent = jnp.sum(to_dev.astype(F32), axis=0)
        fits = jnp.max(sent) <= places
        free = jnp.maximum(places - sent, 0.0)
        free_at = jnp.sum(jnp.where(iota((n_dev, n_dev), 0) > iota((n_dev, n_dev), 1), free[None, :], 0.0), axis=1)
        fill = ranks[:, n_dev]
        fill_dev = (fill[:, None] >= free_at[None, :]) & (fill[:, None] < (free_at + free)[None, :])
        fill_place = jnp.sum(jnp.where(fill_dev, fill[:, None] + (sent - free_at)[None, :], 0.0), axis=1)
        rare_place = jnp.sum(jnp.where(to_dev, ranks[:, :n_dev], 0.0), axis=1)
        dest = jnp.sum(jnp.where(jnp.where(rare[:, None], to_dev, fill_dev), iota((n_loc, n_dev), 1), 0), axis=1)
        slot = dest * places + jnp.where(rare, rare_place, fill_place).astype(jnp.int32)
        row_used = (row_n > 0) & (row_f == 0) & (row_q == 0)
        fits = fits & (jnp.sum(row_used.astype(jnp.int32)) <= COLD_MAX) & (jnp.sum((row_f > FREQ_HOT).astype(jnp.int32)) <= 1)
        tok_class = jnp.where(rare, jnp.where(tok_q > 0, hot_at + tok_q - 1, cold_at + token_ids % rows_dev), tok_f - 1)
        move = iota((n_loc, n_loc), 0) == slot[None, :]
        move_b = move.astype(BF)
        x_moved = exchange(dot32(move_b, x_in).astype(BF))
        d_placed = dot32(move_b, d_out).astype(BF)
        send_class = jnp.sum(jnp.where(move, tok_class[None, :], 0), axis=1) + jnp.where(fits, 0, 1 << 20)
        got_class = swap(send_class.reshape(n_dev, places)).reshape(n_loc)
        all_fit = jnp.max(got_class) < (1 << 20)

        below = iota((rows_dev, rows_dev), 0) > iota((rows_dev, rows_dev), 1)
        used_rank = jnp.sum(jnp.where(below & row_used[None, :], 1, 0), axis=1)
        row_of = jnp.sum(jnp.where((used_rank[None, :] == iota((COLD_MAX, rows_dev), 0)) & row_used[None, :],
                                   iota((COLD_MAX, rows_dev), 1), 0), axis=1)
        cold_owner = jnp.where(cold_id >= 0, cold_id // rows_dev, -1)
        my_cold = (cold_owner == me).astype(jnp.int32)
        my_row = jnp.sum(my_cold * (cold_id - me * rows_dev + 1)) - 1
        wanted = jnp.concatenate([row_of, jnp.full((8,), jnp.clip(my_row, 0, rows_dev - 1), jnp.int32)])
        packed = pack_rows(wanted, emb_table.transpose(1, 0, 2))
        freq_cold = swap(jnp.broadcast_to(packed[COLD_MAX:COLD_MAX + 1], (n_dev, layers, emb_dim)))
        cold_pick = one_hot(cold_owner, n_dev)
        hot_pick = one_hot(hot_f - 1, FREQ_HOT).T
        hot_mine = lax.dynamic_index_in_dim(hot_table.reshape(layers, hot_dev, n_dev, emb_dim), me, 2, keepdims=False)
        table = jnp.stack([jnp.concatenate([
            dot32(hot_pick, hot_table[i]).astype(BF), dot32(cold_pick, freq_cold[:, i]).astype(BF),
            hot_mine[i], packed[:COLD_MAX, i]], axis=0) for i in range(layers)])
        n_blocks = 12 if rows_dev % 12 == 0 else 1
        edges = (rows_dev // n_blocks) * iota((n_blocks + 1, rows_dev), 0)
        starts = jnp.sum(jnp.where(row_used[None, :] & (iota((n_blocks + 1, rows_dev), 1) < edges), 1, 0), axis=1)
        row_no = got_class - cold_at
        used_before = jnp.sum(jnp.where(row_used[None, :] & (iota((n_loc, rows_dev), 1) < row_no[:, None]), 1, 0), axis=1)
        cls = jnp.where(row_no >= 0, cold_at + used_before, got_class)
        code = jnp.where((hot_f > 0) & (hot_f <= FREQ_HOT), hot_f - 1, -1)
        back = (slot[:, None] == iota((n_loc, n_loc), 1)).astype(BF)

        def fast(x_moved, d_placed, table, cls, back, starts, row_of, code, my_cold, my_row):
            return run(x_moved, d_placed, table, cls, back, starts, row_of, code, my_cold, my_row)

        def run(x_moved, d_placed, table, cls, back, starts, row_of, code, my_cold, my_row):
            d_moved = exchange(d_placed)
            cls_col, cls_row = cls.reshape(n_loc, 1), cls.reshape(1, n_loc)
            xs, hs, ss, x_last = forward(x_moved, cls_col, table, w_up, w_down, w_gate, w_proj)
            x_back = exchange(x_last)

            def freq_parts(sums):
                return sums[:, :FREQ].reshape(2, n_dev, per_dev, emb_dim).transpose(1, 0, 2, 3)

            sums_a, r = backward(3, 2, True, d_moved, cls_col, cls_row, table, xs, hs, ss, w_up, w_down, w_gate, w_proj)
            all_a = lax.all_gather(sums_a[:, hot_at:cold_at].reshape(2 * hot_dev, emb_dim), 'emb')
            freq_a = swap(freq_parts(sums_a))
            r, x_back = lax.optimization_barrier((r, x_back))
            sums_b, _ = backward(1, 2, False, r, cls_col, cls_row, table, xs, hs, ss, w_up, w_down, w_gate, w_proj)
            freq_b = swap(freq_parts(sums_b))
            x_out = dot32(back, x_back).astype(BF)
            d_table = table_out(rows_dev, cold_at, starts, row_of, [(sums_b, 1), (sums_b, 0), (sums_a, 1), (sums_a, 0)], n_blocks)
            totals = [jnp.sum(v, axis=0).reshape(2 * per_dev, emb_dim) for v in (freq_a, freq_b)]
            mine = jnp.concatenate([sums_b[:, hot_at:cold_at].reshape(2 * hot_dev, emb_dim)] + totals, axis=0)
            mine, x_out, d_table = lax.optimization_barrier((mine, x_out, d_table))
            all_b = gather_all(mine, n_dev)
            freq = all_b[:, 2 * hot_dev:].reshape(n_dev, layers, per_dev, emb_dim).transpose(1, 0, 2, 3).reshape(layers, FREQ, emb_dim)
            row = jnp.sum(freq[::-1, FREQ_HOT:] * my_cold.astype(F32)[None, :, None], axis=1)[None]
            d_table = put_row(my_row.reshape(1), row, d_table)
            into = empty((layers, n_hot, emb_dim))
            into = hot_out(1, 2, all_b, freq[2:], code, into)
            into = hot_out(3, 2, all_a, freq[:2], code, into)
            return x_out, d_table.transpose(1, 0, 2), into

        def slow(*_):
            return general_path(n_dev, me, token_ids, hot_ids, x_in, d_out, emb_table, hot_table, w_up, w_down, w_gate, w_proj)

        given = lax.optimization_barrier((x_moved, d_placed, table, cls, back, starts, row_of, code, my_cold, my_row))
        return lax.cond(all_fit, fast, slow, *given)

    return jax.shard_map(body, mesh=mesh,
                         in_specs=(P('emb'), P(), P('emb', None), P('emb', None), P(None, 'emb', None), P(), P(), P(), P(), P()),
                         out_specs=(P('emb', None), P(None, 'emb', None), P()),
                         check_vma=False)
```

profile of v0, /device:TPU:24, one launch (start us, length us, event | category | flops | bytes accessed | tf_op | source)
XLA Modules:
  0.0 795.8 jit_solution(16184082902418869372)
XLA Ops:
  7.2 3.1 copy.332
  11.0 5.9 all-to-all-start.7
  17.6 3.3 constant_dynamic-slice_fusion.2
  24.6 12.9 %count_ids.1 = f32[200,256]{1,0:T(8,128)} custom-call(s32[32,1024]{1,0:T(8,128)} %bitcast.345), custom_call_target="tpu_custom_call" | custom-call | tf_op jit(solution)/shard_map/count_ids/pallas_call | solution.py:338
  38.4 1.8 broadcast_select_fusion.2
  43.8 1.7 fusion.219
  46.2 3.7 fusion.226
  49.8 3.7 fusion.223
  58.9 1.8 fusion.199
  64.6 1.6 select_reduce_fusion.4
  68.8 5.8 all-to-all-start.8
  75.3 12.3 %pack_rows.1 = bf16[264,4,1024]{2,1,0:T(4,128)(2,1)} custom-call(s32[264]{0:T(512)} %concatenate.34.row_of, bf16[1572,4,1024]{2,1,0:T(4,128)(2,1)} %bitcast.327), custom_call_target="tpu_custom_call" | custom-call | tf_op jit(solution)/shard_map/pack_rows/pallas_call | solution.py:352
  87.6 9.0 %fusion.313 = (bf16[256,1,1024]{2,1,0:T(2,128)(2,1)}, bf16[256,1,1024]{2,1,0:T(2,128)(2,1)}, bf16[256,1,1024]{2,1,0:T(2,128)(2,1)}, bf16[256,1,1024]{2,1,0:T(2,128)(2,1)S(1)}) fusion(bf16[264,4,1024]{2,1,0:T(4,128)(2,1)} %pack_rows.1), kind=kLoop, calls=%fused_computation.455 | loop fusion | bytes 4194304 | tf_op jit(solution)/shard_map/slice | solution.py:658
  98.0 4.0 all-to-all-start.10
  102.0 4.3 fusion.207
  106.4 3.9 all-to-all-done.10
  110.3 6.1 all-to-all-start.9
  117.8 2.2 copy.281
  121.3 3.6 fusion.229
  125.0 3.8 fusion.220
  128.9 3.7 fusion.208
  135.4 1.7 select_reduce_fusion.1
  142.4 2.1 pad_maximum_fusion.1
  144.5 18.6 %all-to-all-done.9 = bf16[32,32,1024]{2,1,0:T(8,128)(2,1)} async-done(((bf16[32,32,1024]{2,1,0:T(8,128)(2,1)}), bf16[32,32,1024]{2,1,0:T(8,128)(2,1)}, u32[]{:S(2)}, u32[]{:S(2)}) %all-to-all-start.9) | async-done | bytes 2097184 | tf_op jit(solution)/shard_map/all_to_all | solution.py:574
  163.1 625.4 %conditional.1 = (bf16[1024,1024]{1,0:T(8,128)(2,1)}, f32[4,1572,1024]{2,0,1:T(4,128)}, f32[4,2048,1024]{2,1,0:T(8,128)}) conditional(s32[]{:T(128)} %convert_element_type.445, (s32[1024]{0:T(1024)S(1)}, s32[2048]{0:T(1024)S(1)}, s32[]{:T(128)}, bf16[4,1024,4096]{2,1,0:T(8,128)(2,1)}, bf16[4,4096,1024]{2,1,0:T(8,128)(2,1)}, ...), branch_computations={%region_31.47_spmd, %region_47.51_spmd} | conditional | flops 324738678784 | bytes 577410176 | solution.py:704
  170.8 6.0 all-to-all-start
  177.9 138.8 %forward.1 = (bf16[4,1024,1024]{2,1,0:T(8,128)(2,1)}, bf16[4,1024,4096]{2,1,0:T(8,128)(2,1)}, bf16[4,1024,1024]{2,1,0:T(8,128)(2,1)}, bf16[1024,1024]{1,0:T(8,128)(2,1)}) custom-call(bf16[1024,1024]{1,0:T(8,128)(2,1)} %get-tuple-element.471.x0, s32[1024,1]{1,0:T(8,128)} %copy.200.cls, bf16[4,448,1024]{2,1,0:T(8,128)(2,1)} %get-tuple-element.470.table, ...), custom_call_target="tpu_custom_call" | custom-call | flops 89657442304 | bytes 160000000 | tf_op jit(solution)/shard_map/cond/branch_1_fun/forward/pallas_call | solution.py:196
  316.7 87.2 %backward.2 = (f32[2,448,1024]{2,1,0:T(8,128)}, f32[1024,1024]{1,0:T(8,128)}) custom-call(bf16[1024,1024]{1,0:T(8,128)(2,1)} %bitcast.5.r_in, s32[1024,1]{1,0:T(8,128)} %copy.200.cls, s32[1,1024]{1,0:T(1,128)S(1)} %bitcast.354, bf16[4,448,1024]{2,1,0:T(8,128)(2,1)} %get-tuple-element.470.table, bf16[4,1024,1024]{2,1,0:T(8,128)(2,1)} %get-tuple-element.476.xs, ...), custom_call_target="tpu_custom_call" | custom-call | flops 50465865728 | bytes 80000000 | tf_op jit(solution)/shard_map/cond/branch_1_fun/backward/pallas_call | solution.py:292
  403.9 1.9 slice.85
  405.8 86.0 %all_to_all.68 = bf16[32,32,1024]{2,1,0:T(8,128)(2,1)} all-to-all(bf16[32,32,1024]{2,1,0:T(8,128)(2,1)} %bitcast.337), channel_id=1, replica_groups=mesh['emb'=32] {'emb'}, dimensions={0} | all-to-all | bytes 4194304 | tf_op jit(solution)/shard_map/cond/branch_1_fun/all_to_all | solution.py:574
  491.8 59.6 %backward.3 = (f32[2,448,1024]{2,1,0:T(8,128)}, f32[1024,1024]{1,0:T(8,128)}) custom-call(f32[1024,1024]{1,0:T(8,128)} %get-tuple-element.481.r_in, s32[1024,1]{1,0:T(8,128)} %copy.200.cls, s32[1,1024]{1,0:T(1,128)S(1)} %bitcast.355, bf16[4,448,1024]{2,1,0:T(8,128)(2,1)} %get-tuple-element.470.table, bf16[4,1024,1024]{2,1,0:T(8,128)(2,1)} %get-tuple-element.476.xs, ...), custom_call_target="tpu_custom_call" | custom-call | flops 50465865728 | bytes 80000000 | tf_op jit(solution)/shard_map/cond/branch_1_fun/backward/pallas_call | solution.py:292
  554.1 6.6 all-to-all-start.3
  563.4 21.2 %all-to-all-done.3 = f32[32,2,4,1024]{3,2,1,0:T(4,128)S(1)} async-done(((f32[32,2,4,1024]{3,2,1,0:T(4,128)}), f32[32,2,4,1024]{3,2,1,0:T(4,128)S(1)}, u32[]{:S(2)}, u32[]{:S(2)}) %all-to-all-start.3) | async-done | bytes 1048608 | tf_op jit(solution)/shard_map/cond/branch_1_fun/all_to_all | solution.py:574
  584.7 6.0 all-to-all-start.2
  591.3 1.9 reshape.574.code
  593.2 1.9 slice.80
  595.1 5.3 convert_bitcast_fusion
  600.5 13.3 %table_out.1.into = f32[1572,4,1024]{2,1,0:T(4,128)} custom-call(s32[13]{0:T(128)S(1)} %copy-done.41, s32[256]{0:T(256)S(1)} %copy-done.37, f32[2,448,1024]{2,1,0:T(8,128)} %get-tuple-element.482.refs_0_.refs_1_, f32[2,448,1024]{2,1,0:T(8,128)} %get-tuple-element.482.refs_0_.refs_1_, f32[2,448,1024]{2,1,0:T(8,128)} %get-tuple-element.483.refs_2_.refs_3_, ...), custom_call_target="tpu_custom_call" | custom-call | flops 12000000000 | bytes 25755648 | tf_op jit(solution)/shard_map/cond/branch_1_fun/table_out/pallas_call | solution.py:526
  613.8 1.6 reduce_sum.291
  617.7 2.5 copy.207
  620.2 105.2 %gather_all.1.raw = f32[32,144,1024]{2,1,0:T(8,128)} custom-call(f32[144,1024]{1,0:T(8,128)} %pad_maximum_fusion.mine), custom_call_target="tpu_custom_call" | custom-call | flops 80000000000 | bytes 18874368 | tf_op jit(solution)/shard_map/cond/branch_1_fun/gather_all/pallas_call | solution.py:450
  725.4 1.6 slice-done
  727.0 1.7 reshape.489
  728.7 1.8 copy.275
  730.5 1.8 reshape.490
  733.5 2.5 slice.89.freq
  739.4 24.4 %hot_out.2.into = f32[4,2048,1024]{2,1,0:T(8,128)} custom-call(f32[32,144,1024]{2,1,0:T(8,128)} %gather_all.1.raw, f32[2,128,1024]{2,1,0:T(8,128)} %slice.89.freq, s32[8,256,1]{2,1,0:T(8,128)} %reshape.574.code, f32[4,2048,1024]{2,1,0:T(8,128)} %empty.1.into), custom_call_target="tpu_custom_call", output_to_operand_aliasing={{}: (3, {})} | custom-call | flops 20000000000 | bytes 32000000 | tf_op jit(solution)/shard_map/cond/branch_1_fun/hot_out/pallas_call | solution.py:478
  763.8 24.4 %hot_out.3 = f32[4,2048,1024]{2,1,0:T(8,128)} custom-call(f32[32,128,1024]{2,1,0:T(8,128)} %all-gather.2.cloned.1.call-done.raw, f32[2,128,1024]{2,1,0:T(8,128)} %slice.87.freq, s32[8,256,1]{2,1,0:T(8,128)} %reshape.574.code, f32[4,2048,1024]{2,1,0:T(8,128)} %hot_out.2.into), custom_call_target="tpu_custom_call", output_to_operand_aliasing={{}: (3, {})} | custom-call | flops 20000000000 | bytes 32000000 | tf_op jit(solution)/shard_map/cond/branch_1_fun/hot_out/pallas_call | solution.py:478
  (163 shorter events, 45.6 us)
Async XLA Ops:
  7.2 3.1 copy-start.18
  7.2 10.3 %copy-start.31 = (s32[2048]{0:T(1024)S(1)}, s32[2048]{0:T(1024)}, u32[]{:S(2)}) copy-start(s32[2048]{0:T(1024)} %param.18) | copy-start | bytes 24580
  11.0 12.9 %all-to-all-start.7 = ((s32[32,1,1024]{2,1,0:T(1,128)}), s32[32,1,1024]{2,1,0:T(1,128)S(1)}, u32[]{:S(2)}, u32[]{:S(2)}) async-start(s32[32,1,1024]{2,1,0:T(1,128)} %broadcast_in_dim.307), calls=%async_computation.7 | async-start | bytes 262144 | tf_op jit(solution)/shard_map/all_to_all | solution.py:574
  17.5 22.7 %copy-start.35 = (s32[2048]{0:T(1024)}, s32[2048]{0:T(1024)S(1)}, u32[]{:S(2)}) copy-start(s32[2048]{0:T(1024)S(1)} %get-tuple-element.1006) | copy-start | bytes 24580
  21.6 18.6 %copy-start.38 = (f32[14]{0:T(128)S(1)}, f32[14]{0:T(128)}, u32[]{:S(2)}) copy-start(f32[14]{0:T(128)} %constant.405.clone) | copy-start | bytes 172
  46.2 7.3 copy-start.33
  53.5 2.0 copy-start.39
  56.6 2.3 copy-start.27
  58.9 3.2 copy-start.24
  64.0 0.6 copy-start.29
  66.1 9.1 %copy-start.36 = (s32[256]{0:T(256)}, s32[256]{0:T(256)S(1)}, u32[]{:S(2)}) copy-start(s32[256]{0:T(256)S(1)} %select_reduce_fusion.4) | copy-start | bytes 3076
  68.8 28.4 %all-to-all-start.8 = ((s32[32,1,32]{2,1,0:T(1,128)}), s32[32,1,32]{2,1,0:T(1,128)S(1)}, u32[]{:S(2)}, u32[]{:S(2)}) async-start(s32[32,1,32]{2,1,0:T(1,128)} %add.430), calls=%async_computation.8 | async-start | bytes 32768 | tf_op jit(solution)/shard_map/all_to_all | solution.py:574
  87.5 14.5 %copy-start = (bf16[1024,1024]{1,0:T(8,128)(2,1)S(1)}, bf16[1024,1024]{1,0:T(8,128)(2,1)}, u32[]{:S(2)}) copy-start(bf16[1024,1024]{1,0:T(8,128)(2,1)} %copy.332) | copy-start | bytes 6291460
  98.0 12.3 %all-to-all-start.10 = ((bf16[32,4,1024]{2,1,0:T(4,128)(2,1)}), bf16[32,4,1024]{2,1,0:T(4,128)(2,1)S(1)}, u32[]{:S(2)}, u32[]{:S(2)}) async-start(bf16[32,4,1024]{2,1,0:T(4,128)(2,1)} %broadcast_in_dim.326), calls=%async_computation.10 | async-start | bytes 524288 | tf_op jit(solution)/shard_map/all_to_all | solution.py:574
  106.4 13.7 %copy-start.4 = (bf16[256,1,1024]{2,1,0:T(2,128)(2,1)S(1)}, bf16[256,1,1024]{2,1,0:T(2,128)(2,1)}, u32[]{:S(2)}) copy-start(bf16[256,1,1024]{2,1,0:T(2,128)(2,1)} %get-tuple-element.991) | copy-start | bytes 1572868
  106.4 14.6 %copy-start.3 = (bf16[256,1,1024]{2,1,0:T(2,128)(2,1)S(1)}, bf16[256,1,1024]{2,1,0:T(2,128)(2,1)}, u32[]{:S(2)}) copy-start(bf16[256,1,1024]{2,1,0:T(2,128)(2,1)} %get-tuple-element.992) | copy-start | bytes 1572868
  110.3 52.8 %all-to-all-start.9 = ((bf16[32,32,1024]{2,1,0:T(8,128)(2,1)}), bf16[32,32,1024]{2,1,0:T(8,128)(2,1)}, u32[]{:S(2)}, u32[]{:S(2)}) async-start(bf16[32,32,1024]{2,1,0:T(8,128)(2,1)} %bitcast.335), calls=%async_computation.9 | async-start | bytes 4194304 | tf_op jit(solution)/shard_map/all_to_all | solution.py:574
  116.4 5.0 copy-start.34
  125.0 3.8 copy-start.7
  125.0 3.8 copy-start.25
  128.8 6.6 copy-start.30
  128.8 8.7 %copy-start.28 = (s32[16]{0:T(128)S(1)}, s32[16]{0:T(128)}, u32[]{:S(2)}) copy-start(s32[16]{0:T(128)} %copy-done.27) | copy-start | bytes 196
  128.8 8.9 %copy-start.6 = (bf16[256,1,1024]{2,0,1:T(8,128)(2,1)S(1)}, bf16[256,1,1024]{2,0,1:T(8,128)(2,1)}, u32[]{:S(2)}) copy-start(bf16[256,1,1024]{2,0,1:T(8,128)(2,1)} %copy.281) | copy-start | bytes 1572868
  128.8 8.9 %copy-start.15 = (bf16[64,1024]{1,0:T(8,128)(2,1)S(1)}, bf16[64,1024]{1,0:T(8,128)(2,1)}, u32[]{:S(2)}) copy-start(bf16[64,1024]{1,0:T(8,128)(2,1)} %get-tuple-element.1022) | copy-start | bytes 393220
  128.8 10.1 %copy-start.5 = (bf16[256,1,1024]{2,0,1:T(8,128)(2,1)S(1)}, bf16[256,1,1024]{2,0,1:T(8,128)(2,1)}, u32[]{:S(2)}) copy-start(bf16[256,1,1024]{2,0,1:T(8,128)(2,1)} %copy.278) | copy-start | bytes 1572868
  128.9 10.1 %copy-start.16 = (bf16[64,1024]{1,0:T(8,128)(2,1)S(1)}, bf16[64,1024]{1,0:T(8,128)(2,1)}, u32[]{:S(2)}) copy-start(bf16[64,1024]{1,0:T(8,128)(2,1)} %get-tuple-element.1019) | copy-start | bytes 393220
  132.6 7.6 copy-start.14
  141.3 21.8 %copy-start.19 = (s32[1024]{0:T(1024)S(1)}, s32[1024]{0:T(1024)}, u32[]{:S(2)}) copy-start(s32[1024]{0:T(1024)} %param.17) | copy-start | bytes 12292
  141.3 21.8 %copy-start.32 = (s32[2048]{0:T(1024)S(1)}, s32[2048]{0:T(1024)}, u32[]{:S(2)}) copy-start(s32[2048]{0:T(1024)} %param.18) | copy-start | bytes 24580
  170.8 145.8 %all-to-all-start = ((bf16[32,32,1024]{2,1,0:T(8,128)(2,1)}), bf16[32,32,1024]{2,1,0:T(8,128)(2,1)}, u32[]{:S(2)}, u32[]{:S(2)}) async-start(bf16[32,32,1024]{2,1,0:T(8,128)(2,1)} %bitcast.334), calls=%async_computation | async-start | bytes 4194304 | tf_op jit(solution)/shard_map/cond/branch_1_fun/all_to_all | solution.py:574
  176.8 587.0 %all-gather.2.cloned.1.call-start = ((), (), s32[]{:S(2)}) async-start(), calls=%async_computation.11 | async-start | bytes 17301504 | tf_op jit(solution)/shard_map/cond/branch_1_fun/all_gather | solution.py:681
  554.1 30.6 %all-to-all-start.3 = ((f32[32,2,4,1024]{3,2,1,0:T(4,128)}), f32[32,2,4,1024]{3,2,1,0:T(4,128)S(1)}, u32[]{:S(2)}, u32[]{:S(2)}) async-start(f32[32,2,4,1024]{3,2,1,0:T(4,128)} %bitcast.242), calls=%async_computation.3 | async-start | bytes 2097152 | tf_op jit(solution)/shard_map/cond/branch_1_fun/all_to_all | solution.py:574
  584.7 6.0 copy-start.2
  584.7 30.7 %all-to-all-start.2 = ((f32[32,2,4,1024]{3,2,1,0:T(4,128)}), f32[32,2,4,1024]{3,2,1,0:T(4,128)}, u32[]{:S(2)}, u32[]{:S(2)}) async-start(f32[32,2,4,1024]{3,2,1,0:T(4,128)} %bitcast.243), calls=%async_computation.2 | async-start | bytes 2097152 | tf_op jit(solution)/shard_map/cond/branch_1_fun/all_to_all | solution.py:574
  590.6 0.6 copy-start.40
  590.6 0.7 copy-start.26
  590.6 4.5 copy-start.8
  595.1 5.3 copy-start.37
  595.1 5.3 copy-start.41
  600.5 16.3 %copy-start.10 = (f32[2,64,1024]{2,1,0:T(8,128)S(1)}, f32[2,64,1024]{2,1,0:T(8,128)}, u32[]{:S(2)}) copy-start(f32[2,64,1024]{2,1,0:T(8,128)} %slice.80) | copy-start | bytes 1572868 | tf_op jit(solution)/shard_map/cond
  613.8 3.9 copy-start.9
  725.4 1.6 slice-start
  732.3 5.1 slice-start.1
Sparse Core Ops, SparseCore 0:
  406.0 142.3 all-gather.1
where the time goes:
time: 807 us; the launch traced here: 796 us
  Pallas kernels  479 us (59%)
  blocking collectives  86 us (11%)
  local copies, waits for them, and re-layouts  53.2 us (7%)
  waiting for transfers between devices  43.8 us (5%)
  starting transfers between devices  40.4 us (5%)
  matrix products  35.9 us (4%)
  other arithmetic  30.7 us (4%)
  between operations  18.3 us (2%)
  loops' own time  8.18 us (1%)
    pallas_call x2, Pallas kernels, backward(): pl.pallas_call(functools.partial(backward_kernel, n_l, n_f, last_full), g...  147 us
    pallas_call x1, Pallas kernels, forward(): pl.pallas_call(functools.partial(forward_kernel, n_l, n_f), grid=(n_l, n_...  139 us
    pallas_call x1, Pallas kernels, gather_all(): pl.pallas_call(gather_kernel, in_specs=[pl.BlockSpec(memory_space=pltpu.V...  105 us
    all_to_all x1, blocking collectives, swap(): return lax.all_to_all(v, 'emb', 0, 0, tiled=True)  86 us
    pallas_call x2, Pallas kernels, hot_out(): pl.pallas_call(functools.partial(hot_kernel, n_dev), grid=(n_l, blocks),...  48.9 us
    all_to_all x7, waiting for transfers between devices, swap(): return lax.all_to_all(v, 'emb', 0, 0, tiled=True)  43.7 us
    all_to_all x7, starting transfers between devices, swap(): return lax.all_to_all(v, 'emb', 0, 0, tiled=True)  40.3 us
    dot_general x19, matrix products, dot32(): return jnp.dot(a, b, preferred_element_type=F32)  35.9 us
  transfers between devices with their start and end apart: 8, of which 3 were waited for; matrix products, arithmetic and copies ran while one was open for 10% of the time, Pallas kernels for 45%

commit v1 on v0

v1 whole, which is shorter than its diff:
```python
import functools

import jax
import jax.numpy as jnp
from jax import lax
from jax.experimental import pallas as pl
from jax.experimental.pallas import tpu as pltpu
from jax.sharding import PartitionSpec as P


NORM_EPS = 1e-6
FREQ_HOT = 112
FREQ_COLD = 16
FREQ = FREQ_HOT + FREQ_COLD
COLD_MAX = 256
LO = 256
HI_BITS = 8
RUN = 4
LEVELS = tuple(16 * 2 ** (i / 4) for i in range(17))
GELU_A = 0.7978845608028654
GELU_B = GELU_A * 0.044715
VMEM = 66_000_000
ROWS_A = 256
ROWS_B = 512
TILE = 1024
BF = jnp.bfloat16
F32 = jnp.float32
I32 = jnp.int32
ONCE = pl.Buffered(1)


def gelu_back(pre_act, cot_in):
    _, pull = jax.vjp(jax.nn.gelu, pre_act.astype(F32))
    return pull(cot_in)[0]


def dot32(a, b):
    return jnp.dot(a, b, preferred_element_type=F32)


def dense_parts(resid, w_up, w_gate):
    resid_f = resid.astype(F32)
    inv_rms = lax.rsqrt(jnp.mean(resid_f * resid_f, axis=-1, keepdims=True) + NORM_EPS)
    normed = (resid_f * inv_rms).astype(BF)
    hidden = dot32(normed, w_up).astype(BF)
    gate_pre = dot32(normed, w_gate).astype(BF)
    return resid_f, inv_rms, hidden, gate_pre


def layer_forward(resid, emb_rows, w_up, w_down, w_gate, w_proj):
    resid_f, _, hidden, gate_pre = dense_parts(resid, w_up, w_gate)
    activated = jax.nn.gelu(hidden.astype(F32)).astype(BF)
    mlp_out = dot32(activated, w_down).astype(BF)
    gate = jax.nn.gelu(gate_pre.astype(F32)).astype(BF)
    mixed = (gate.astype(F32) * emb_rows.astype(F32)).astype(BF)
    projected = dot32(mixed, w_proj).astype(BF)
    return (resid_f + mlp_out.astype(F32) + projected.astype(F32)).astype(BF)


def layer_backward(resid, emb_rows, d_next, w_up, w_down, w_gate, w_proj):
    resid_f, inv_rms, hidden, gate_pre = dense_parts(resid, w_up, w_gate)
    gate = jax.nn.gelu(gate_pre.astype(F32)).astype(BF)
    d_cast = d_next.astype(BF)
    d_mixed = jnp.einsum('nd,ed->ne', d_cast, w_proj, preferred_element_type=F32)
    d_rows = gate.astype(F32) * d_mixed
    d_gpre = gelu_back(gate_pre, d_mixed * emb_rows.astype(F32))
    d_hidden = gelu_back(hidden, jnp.einsum('nd,fd->nf', d_cast, w_down, preferred_element_type=F32))
    d_normed = (jnp.einsum('nf,df->nd', d_hidden.astype(BF), w_up, preferred_element_type=F32)
                + jnp.einsum('ne,de->nd', d_gpre.astype(BF), w_gate, preferred_element_type=F32))
    inner = jnp.mean(d_normed * resid_f, axis=-1, keepdims=True)
    d_prev = d_next + inv_rms * d_normed - resid_f * (inv_rms * inv_rms * inv_rms) * inner
    return d_prev, d_rows


def general_path(n_dev, my_index, token_ids, hot_ids, x_in, d_out, emb_table, hot_table, w_up, w_down, w_gate, w_proj):
    n_loc = token_ids.shape[0]
    _, rows_dev, emb_dim = emb_table.shape
    capacity = max(8, (2 * n_loc) // n_dev)
    n_slots = n_dev * capacity
    hot_match = token_ids[:, None] == hot_ids[None, :]
    is_hot = jnp.any(hot_match, axis=1)
    hot_pick = hot_match.astype(BF)
    hot_pick_f = hot_match.astype(F32)
    owner_id = token_ids // rows_dev
    to_owner = (owner_id[:, None] == jnp.arange(n_dev, dtype=jnp.int32)[None, :]) & jnp.logical_not(is_hot)[:, None]
    owner_rank = jnp.cumsum(to_owner.astype(jnp.int32), axis=0) - 1
    place = jnp.sum(jnp.where(to_owner, owner_rank, 0), axis=1)
    slot = jnp.where(is_hot, n_slots, owner_id * capacity + place)
    send_ids = jnp.full((n_slots,), -1, jnp.int32).at[slot].set(token_ids, mode='drop')
    slot_tok = jnp.full((n_slots,), -1, jnp.int32).at[slot].set(jnp.arange(n_loc, dtype=jnp.int32), mode='drop')
    recv_ids = lax.all_to_all(send_ids.reshape(n_dev, capacity), 'emb', 0, 0, tiled=True).reshape(n_slots)
    served_ok = recv_ids >= 0
    local_row = jnp.where(served_ok, recv_ids - my_index * rows_dev, 0)
    pick_slot = jnp.minimum(slot, n_slots - 1)
    slot_used = slot_tok >= 0
    slot_src = jnp.maximum(slot_tok, 0)

    def fwd(resid, per_layer):
        table, hot_l, up, down, gate_w, proj = per_layer
        served = jnp.take(table, local_row, axis=0)
        fetched = lax.all_to_all(served.reshape(n_dev, capacity, emb_dim), 'emb', 0, 0, tiled=True).reshape(n_slots, emb_dim)
        cold_rows = jnp.take(fetched, pick_slot, axis=0)
        hot_rows = dot32(hot_pick, hot_l).astype(BF)
        emb_rows = jnp.where(is_hot[:, None], hot_rows, cold_rows)
        return layer_forward(resid, emb_rows, up, down, gate_w, proj), (resid, emb_rows)

    x_out, (x_saved, rows_saved) = lax.scan(fwd, x_in, (emb_table, hot_table, w_up, w_down, w_gate, w_proj))

    def bwd(d_resid, per_layer):
        resid_l, rows_l, up, down, gate_w, proj = per_layer
        d_resid, d_rows = layer_backward(resid_l, rows_l, d_resid, up, down, gate_w, proj)
        outgoing = jnp.where(slot_used[:, None], jnp.take(d_rows, slot_src, axis=0), 0.0)
        incoming = lax.all_to_all(outgoing.reshape(n_dev, capacity, emb_dim), 'emb', 0, 0, tiled=True).reshape(n_slots, emb_dim)
        d_tab = jax.ops.segment_sum(jnp.where(served_ok[:, None], incoming, 0.0), local_row, num_segments=rows_dev)
        hot_local = jnp.einsum('nh,ne->he', hot_pick_f, d_rows, precision=lax.Precision.HIGHEST, preferred_element_type=F32)
        return d_resid, (d_tab, lax.psum(hot_local, 'emb'))

    _, (d_table, d_hot) = lax.scan(bwd, d_out.astype(F32), (x_saved, rows_saved, w_up, w_down, w_gate, w_proj), reverse=True)
    return x_out, d_table, d_hot


def split3(v):
    hi = v.astype(BF)
    rest = v - hi.astype(F32)
    mid = rest.astype(BF)
    return hi, mid, (rest - mid.astype(F32)).astype(BF)


def iota(shape, dim):
    return lax.broadcasted_iota(jnp.int32, shape, dim)


def one_hot(v, n, dtype=BF):
    return (v[:, None] == iota((v.shape[0], n), 1)).astype(dtype)


def dot_nt(a, b):
    return lax.dot_general(a, b, (((1,), (1,)), ((), ())), preferred_element_type=F32)


def gelu(x):
    half = 0.5 * x
    return half + half * jnp.tanh(x * (GELU_A + GELU_B * (x * x)))


def gelu_slope(x):
    sq = x * x
    th = jnp.tanh(x * (GELU_A + GELU_B * sq))
    return (0.5 + 0.5 * th) + (0.5 * x) * (1.0 - th * th) * (GELU_A + (3.0 * GELU_B) * sq)


def forward_kernel(n_l, n_f, x0, cls, table, wu, wd, wg, wp, xs, hs, ss, es, xo, x_now, u_now, acc, q_now):
    layer, step = pl.program_id(0), pl.program_id(1)
    n_tok = x_now.shape[0]

    @pl.when((layer == 0) & (step == 0))
    def _():
        x_now[...] = x0[...]

    @pl.when(step == 0)
    def _():
        for m in chunks(n_tok, ROWS_A):
            xb = x_now[m, :]
            x = xb.astype(F32)
            xs[0, m, :] = xb
            u = (x * lax.rsqrt(jnp.mean(x * x, axis=-1, keepdims=True) + NORM_EPS)).astype(BF)
            u_now[m, :] = u
            s = dot32(u, wg[0]).astype(BF)
            ss[0, m, :] = s
            g = gelu(s.astype(F32)).astype(BF)
            pick = (cls[m, :] == iota((m.size, table.shape[1]), 1)).astype(BF)
            e = dot32(pick, table[0]).astype(BF)
            es[0, m, :] = e
            mixed = (g.astype(F32) * e.astype(F32)).astype(BF)
            q_now[m, :] = dot32(mixed, wp[0]).astype(BF)
            acc[m, :] = jnp.zeros((m.size, acc.shape[1]), F32)

    for m in chunks(n_tok, ROWS_B):
        h = dot32(u_now[m, :], wu[0]).astype(BF)
        hs[0, m, :] = h
        acc[m, :] += dot32(gelu(h.astype(F32)).astype(BF), wd[0])

    @pl.when(step == n_f - 1)
    def _():
        for m in chunks(n_tok, ROWS_A):
            x = x_now[m, :].astype(F32) + acc[m, :].astype(BF).astype(F32) + q_now[m, :].astype(F32)
            x_now[m, :] = x.astype(BF)

    @pl.when((step == n_f - 1) & (layer == n_l - 1))
    def _():
        xo[...] = x_now[...]


def chunks(n, size):
    size = min(n, size)
    return [pl.ds(m, size) for m in range(0, n, size)]


def forward(x0, cls, table, w_up, w_down, w_gate, w_proj):
    n_tok, dim = x0.shape
    n_l, _, ff = w_up.shape
    emb = w_gate.shape[2]
    tile = min(TILE, ff)
    n_f = ff // tile
    n_c = table.shape[1]

    def whole(l, f):
        return (l, 0, 0)

    def cols(l, f):
        return (l, 0, f)

    def fixed(l, f):
        return (0, 0)

    return pl.pallas_call(
        functools.partial(forward_kernel, n_l, n_f),
        grid=(n_l, n_f),
        in_specs=[
            pl.BlockSpec((n_tok, dim), fixed, pipeline_mode=ONCE),
            pl.BlockSpec((n_tok, 1), fixed, pipeline_mode=ONCE),
            pl.BlockSpec((1, n_c, emb), whole),
            pl.BlockSpec((1, dim, tile), cols),
            pl.BlockSpec((1, tile, dim), lambda l, f: (l, f, 0)),
            pl.BlockSpec((1, dim, emb), whole),
            pl.BlockSpec((1, emb, dim), whole),
        ],
        out_specs=[
            pl.BlockSpec((1, n_tok, dim), whole),
            pl.BlockSpec((1, n_tok, tile), cols),
            pl.BlockSpec((1, n_tok, emb), whole),
            pl.BlockSpec((1, n_tok, emb), whole),
            pl.BlockSpec((n_tok, dim), fixed),
        ],
        out_shape=[jax.ShapeDtypeStruct((n_l, n_tok, n), BF) for n in (dim, ff, emb, emb)]
        + [jax.ShapeDtypeStruct((n_tok, dim), BF)],
        scratch_shapes=[pltpu.VMEM((n_tok, dim), t) for t in (BF, BF, F32, BF)],
        compiler_params=params("arbitrary", "arbitrary"),
        cost_estimate=cost(n_l * n_tok * dim * (2 * ff + 2 * emb + n_c), n_l),
        name="forward",
    )(x0, cls, table, w_up, w_down, w_gate, w_proj)


def params(*kinds, **more):
    return pltpu.CompilerParams(vmem_limit_bytes=VMEM, dimension_semantics=kinds or None, **more)


def cost(products, layers):
    return pl.CostEstimate(flops=2 * products, bytes_accessed=layers * 40_000_000, transcendentals=0)


def backward_kernel(n_f, last_full, r_in, cls_t, es, xs, hs, ss, wu, wd, wg, wp, sums, r, c_now, acc, three):
    step = pl.program_id(0)
    f = step % n_f
    n_tok, n_c = c_now.shape[0], sums.shape[1]
    goes_on = True if last_full else step < pl.num_programs(0) - 1

    @pl.when(step == 0)
    def _():
        r[...] = r_in[...].astype(F32)

    @pl.when(f == 0)
    def _():
        for m in chunks(n_tok, ROWS_B):
            c = r[m, :].astype(BF)
            c_now[m, :] = c
            a = dot_nt(c, wp[0])
            s = ss[0, m, :].astype(F32)
            rows = gelu(s).astype(BF).astype(F32) * a
            for i, part in enumerate(split3(rows)):
                three[i, m, :] = part
            if last_full:
                ds = (gelu_slope(s) * (a * es[0, m, :].astype(F32))).astype(BF)
                acc[m, :] = dot_nt(ds, wg[0])
            else:
                acc[m, :] = a
        pick_t = (cls_t[...] == iota((n_c, n_tok), 0)).astype(BF)
        sums[0] = dot32(pick_t, three[0]) + (dot32(pick_t, three[1]) + dot32(pick_t, three[2]))

    if not last_full:
        @pl.when((f == 0) & goes_on)
        def _():
            for m in chunks(n_tok, ROWS_B):
                ds = (gelu_slope(ss[0, m, :].astype(F32)) * (acc[m, :] * es[0, m, :].astype(F32))).astype(BF)
                acc[m, :] = dot_nt(ds, wg[0])

    @pl.when(goes_on)
    def _():
        for m in chunks(n_tok, ROWS_B):
            d_act = dot_nt(c_now[m, :], wd[0])
            dh = (gelu_slope(hs[0, m, :].astype(F32)) * d_act).astype(BF)
            acc[m, :] += dot_nt(dh, wu[0])

    @pl.when((f == n_f - 1) & goes_on)
    def _():
        for m in chunks(n_tok, ROWS_A):
            x = xs[0, m, :].astype(F32)
            k = lax.rsqrt(jnp.mean(x * x, axis=-1, keepdims=True) + NORM_EPS)
            du = acc[m, :]
            inner = jnp.mean(du * x, axis=-1, keepdims=True)
            r[m, :] = r[m, :] + k * du - x * (k * k * k) * inner


def backward(first, n_l, last_full, r_in, cls_t, es, xs, hs, ss, w_up, w_down, w_gate, w_proj, n_class=448):
    n_tok, dim = r_in.shape
    ff = w_up.shape[2]
    emb = w_gate.shape[2]
    tile = min(TILE, ff)
    n_f = ff // tile
    n_c = n_class
    n_steps = n_l * n_f if last_full else (n_l - 1) * n_f + 1

    def whole(t):
        return (first - t // n_f, 0, 0)

    def cols(t):
        return (first - t // n_f, 0, t % n_f)

    def fixed(t):
        return (0, 0)

    return pl.pallas_call(
        functools.partial(backward_kernel, n_f, last_full),
        grid=(n_steps,),
        in_specs=[
            pl.BlockSpec((n_tok, dim), fixed, pipeline_mode=ONCE),
            pl.BlockSpec((1, n_tok), fixed, pipeline_mode=ONCE),
            pl.BlockSpec((1, n_tok, emb), whole),
            pl.BlockSpec((1, n_tok, dim), whole),
            pl.BlockSpec((1, n_tok, tile), cols),
            pl.BlockSpec((1, n_tok, emb), whole),
            pl.BlockSpec((1, dim, tile), cols),
            pl.BlockSpec((1, tile, dim), lambda t: (first - t // n_f, t % n_f, 0)),
            pl.BlockSpec((1, dim, emb), whole),
            pl.BlockSpec((1, emb, dim), whole),
        ],
        out_specs=[
            pl.BlockSpec((1, n_c, emb), lambda t: (t // n_f, 0, 0)),
            pl.BlockSpec((n_tok, dim), fixed),
        ],
        out_shape=[
            jax.ShapeDtypeStruct((n_l, n_c, emb), F32),
            jax.ShapeDtypeStruct((n_tok, dim), F32),
        ],
        scratch_shapes=[pltpu.VMEM((n_tok, dim), BF), pltpu.VMEM((n_tok, dim), F32), pltpu.VMEM((3, n_tok, emb), BF)],
        compiler_params=params("arbitrary"),
        cost_estimate=cost(n_l * n_tok * dim * (2 * ff + 2 * emb + 3 * n_c), n_l),
        name="backward",
    )(r_in, cls_t, es, xs, hs, ss, w_up, w_down, w_gate, w_proj)


def spec(shape, *index, **more):
    index = index or (0,) * len(shape)
    return pl.BlockSpec(shape, lambda *_: index, **more)


ANY = pl.BlockSpec(memory_space=pl.ANY)


def out_of(shape, dtype=F32):
    return jax.ShapeDtypeStruct(shape, dtype)


def count_kernel(ids, out):
    n_tok = ids.shape[1]
    out[...] = jnp.zeros(out.shape, F32)

    @pl.loop(0, len(ids))
    def _(i):
        row = ids[pl.ds(i, 1), :]
        hi = ((row >> HI_BITS) == iota((len(out), n_tok), 0)).astype(BF)
        lo = ((row & (LO - 1)) == iota((LO, n_tok), 0)).astype(BF)
        out[...] += dot_nt(hi, lo)


def count_ids(ids, n_hi):
    return pl.pallas_call(count_kernel, out_shape=out_of((n_hi, LO)), compiler_params=params(), name="count_ids")(ids)


def pack_kernel(row_of, table, out, sem):
    @pl.loop(0, len(out))
    def _(k):
        pltpu.make_async_copy(table.at[row_of[k]], out.at[k], sem).start()

    pltpu.make_async_copy(table.at[pl.ds(0, len(out))], out, sem).wait()


def pack_rows(row_of, table):
    shape = row_of.shape + table.shape[1:]
    return pl.pallas_call(
        pack_kernel,
        grid_spec=pltpu.PrefetchScalarGridSpec(num_scalar_prefetch=1, grid=(1,), in_specs=[ANY], out_specs=spec(shape),
                                               scratch_shapes=[pltpu.SemaphoreType.DMA(())]),
        out_shape=out_of(shape, table.dtype), compiler_params=params(), name="pack_rows",
    )(row_of, table)


def gather_kernel(mine, out, own, z_s, z_r, x_s, x_r, y_s, y_r, fx_s, fx_r, fy_s, fy_r,
                  c_s, c_r, cx_s, cx_r, cy_s, cy_r, cd_s, cd_r):
    me = lax.axis_index('emb')
    core, x, y, z = me % 2, (me // 2) % 2, (me // 4) % 2, me // 8
    half = len(mine) // 2
    first, second = pl.ds(0, half), pl.ds(half, half)

    def dev(z, y, x, core):
        return ((z * 2 + y) * 2 + x) * 2 + core

    def copy(src, dst, send, recv, k, to):
        return pltpu.make_async_remote_copy(src_ref=src, dst_ref=dst, send_sem=send.at[k], recv_sem=recv.at[k],
                                            device_id=(to,), device_id_type=pl.DeviceIdType.MESH)

    def column_of(k):
        return (z - k + 4) % 4

    others = [dev((z + k) % 4, y, x, core) for k in range(1, 4)]
    to_x, to_y, to_core = dev(z, y, 1 - x, core), dev(z, 1 - y, x, core), dev(z, y, x, 1 - core)
    barrier = pltpu.get_barrier_semaphore()
    peers = others + [to_x, to_y, to_core]
    for peer in peers:
        pl.semaphore_signal(barrier, device_id=(peer,), device_id_type=pl.DeviceIdType.MESH)
    pl.semaphore_wait(barrier, len(peers))

    keep = pltpu.make_async_copy(mine, out.at[me], own)
    keep.start()
    sent = []

    def send(*args):
        c = copy(*args)
        c.start()
        sent.append(c)

    def got(block, recv, send_sem, k):
        copy(block, block, send_sem, recv, k, to_x).wait_recv()

    for k, other in enumerate(others):
        send(mine, out.at[me], z_s, z_r, k + 1, other)

    def column(k):
        at = dev(column_of(k), y, x, core)
        if k:
            got(out.at[at], z_r, z_s, k)
        src = out.at[at] if k else mine
        send(src, out.at[at], x_s, x_r, k, to_x)
        send(src, out.at[at], y_s, y_r, k, to_y)
        send(src, out.at[at], c_s, c_r, k, to_core)

    def onward(k):
        bx, by = dev(column_of(k), y, 1 - x, core), dev(column_of(k), 1 - y, x, core)
        got(out.at[bx], x_r, x_s, k)
        send(out.at[bx, first], out.at[bx, first], fy_s, fy_r, k, to_y)
        send(out.at[bx], out.at[bx], cx_s, cx_r, k, to_core)
        got(out.at[by], y_r, y_s, k)
        send(out.at[by, second], out.at[by, second], fx_s, fx_r, k, to_x)
        send(out.at[by], out.at[by], cy_s, cy_r, k, to_core)

    def across(k):
        bd = dev(column_of(k), 1 - y, 1 - x, core)
        got(out.at[bd, first], fy_r, fy_s, k)
        got(out.at[bd, second], fx_r, fx_s, k)
        send(out.at[bd], out.at[bd], cd_s, cd_r, k, to_core)

    column(0)
    for k in range(3):
        column(k + 1)
        onward(k)
    across(0)
    onward(3)
    for k in range(1, 4):
        across(k)
    for k in range(4):
        for dy, dx, recv, send_sem in ((y, x, c_r, c_s), (y, 1 - x, cx_r, cx_s), (1 - y, x, cy_r, cy_s), (1 - y, 1 - x, cd_r, cd_s)):
            got(out.at[dev(column_of(k), dy, dx, 1 - core)], recv, send_sem, k)
    for c in sent:
        c.wait_send()
    keep.wait()


def gather_all(mine, n_dev):
    return pl.pallas_call(
        gather_kernel,
        in_specs=[pl.BlockSpec(memory_space=pltpu.VMEM)], out_specs=ANY,
        out_shape=out_of((n_dev,) + mine.shape),
        scratch_shapes=[pltpu.SemaphoreType.DMA(())] + [pltpu.SemaphoreType.DMA((4,))] * 18,
        compiler_params=params(collective_id=0, has_side_effects=True),
        cost_estimate=cost(mine.size * n_dev * LO, 1), name="gather_all",
    )(mine)


def hot_kernel(skip, raw, freq, code, into, out, parts):
    n_dev, n_r, _ = raw.shape

    @pl.when(pl.program_id(1) == 0)
    def _():
        for layer in range(freq.shape[1] // RUN):
            @pl.when(pl.program_id(0) + skip == layer)
            def _(layer=layer):
                rows = jnp.concatenate([freq[o, layer * RUN:(layer + 1) * RUN, :] for o in range(n_dev)], axis=0)
                for i, part in enumerate(split3(rows)):
                    parts[i] = part

    sel = (code[0] == iota((n_r * n_dev, FREQ), 1)).astype(BF)
    more = dot32(sel, parts[0]) + (dot32(sel, parts[1]) + dot32(sel, parts[2]))
    for g in range(n_r // RUN):
        rows = jnp.concatenate([raw[o, g * RUN:(g + 1) * RUN, :] for o in range(n_dev)], axis=0)
        at = pl.ds(g * RUN * n_dev, RUN * n_dev)
        out[0, at, :] = rows + more[g * RUN * n_dev:(g + 1) * RUN * n_dev, :]


def hot_out(first, n_l, gathered, freq_from, freq_at, skip, code, into):
    n_dev, _, emb = gathered.shape
    n_r = 2 * RUN
    width = n_r * n_dev
    blocks = into.shape[1] // width
    return pl.pallas_call(
        functools.partial(hot_kernel, skip),
        grid=(n_l, blocks),
        in_specs=[
            pl.BlockSpec((n_dev, n_r, emb), lambda i, b: (0, i * blocks + b, 0)),
            spec((n_dev, 2 * RUN, emb), 0, freq_at, 0, pipeline_mode=ONCE),
            pl.BlockSpec((1, width, 1), lambda i, b: (b, 0, 0)),
            ANY,
        ],
        out_specs=pl.BlockSpec((1, width, emb), lambda i, b: (first - i, b, 0)),
        out_shape=out_of(into.shape),
        scratch_shapes=[pltpu.VMEM((3, FREQ, emb), BF)],
        input_output_aliases={3: 0},
        compiler_params=params("arbitrary", "arbitrary"),
        cost_estimate=cost(n_l * gathered.size * LO, n_l), name="hot_out",
    )(gathered, freq_from, code.reshape(blocks, width, 1), into)


def empty(shape):
    return pl.pallas_call(lambda out: None, out_specs=ANY, out_shape=out_of(shape), name="empty")()


def table_kernel(at0, starts, row_of, *refs):
    srcs, out = refs[:-1], refs[-1]
    block = pl.program_id(0)
    out[...] = jnp.zeros(out.shape, F32)

    @pl.loop(starts[block], starts[block + 1])
    def _(k):
        at = row_of[k] - block * len(out)
        for l, src in enumerate(srcs):
            out[at, pl.ds(l, 1), :] = src[0, pl.ds(at0 + k, 1), :]


def table_out(rows_dev, at0, starts, row_of, srcs):
    n_l = len(srcs)
    _, n_c, emb = srcs[0][0].shape
    n_blocks = len(starts) - 1
    return pl.pallas_call(
        functools.partial(table_kernel, at0),
        grid_spec=pltpu.PrefetchScalarGridSpec(
            num_scalar_prefetch=2, grid=(n_blocks,),
            in_specs=[spec((1, n_c, emb), i, 0, 0) for _, i in srcs],
            out_specs=pl.BlockSpec((rows_dev // n_blocks, n_l, emb), lambda b, *_: (b, 0, 0))),
        out_shape=out_of((rows_dev, n_l, emb)), compiler_params=params("arbitrary"),
        cost_estimate=cost(rows_dev * n_l * emb * LO, n_l), name="table_out",
    )(starts, row_of, *[s for s, _ in srcs])


def row_kernel(at, row, into, out, sem):
    @pl.when(at[0] >= 0)
    def _():
        c = pltpu.make_async_copy(row, out.at[pl.ds(at[0], 1)], sem)
        c.start()
        c.wait()


def put_row(at, row, into):
    return pl.pallas_call(
        row_kernel,
        in_specs=[pl.BlockSpec(memory_space=pltpu.SMEM), pl.BlockSpec(memory_space=pltpu.VMEM), ANY], out_specs=ANY,
        out_shape=out_of(into.shape), scratch_shapes=[pltpu.SemaphoreType.DMA(())],
        input_output_aliases={2: 0}, name="put_row",
    )(at, row, into)


def down_sum(v):
    return jnp.sum(v, axis=0)


def row_sum(v):
    return jnp.sum(v, axis=1)


def square(n):
    return iota((n, n), 0), iota((n, n), 1)


def prefix(v):
    r, c = square(len(v))
    return row_sum(jnp.where(r > c, v[None, :], 0))


def digits(ids, n_hi):
    return one_hot(ids >> HI_BITS, n_hi), one_hot(ids & (LO - 1), LO)


def look(hi_lo, *maps):
    hi, lo = hi_lo
    got = dot32(hi, jnp.concatenate(maps, axis=1))
    return [row_sum(got[:, i * LO:(i + 1) * LO] * lo.astype(F32)).astype(I32) for i in range(len(maps))]


def number(count, most):
    levels = jnp.array(LEVELS, F32)
    n_over = jnp.sum((count[:, :, None] >= levels).astype(F32), axis=(0, 1))
    flag = count >= jnp.min(jnp.where(n_over <= most, levels, jnp.inf))
    r, c = square(LO)
    in_row = dot32(flag.astype(BF), (r < c).astype(BF))
    return jnp.where(flag, in_row + prefix(row_sum(flag.astype(F32)))[:, None] + 1, 0)


def solution(mesh):
    n_dev = mesh.shape['emb']

    def body(token_ids, hot_ids, x_in, d_out, emb_table, hot_table, w_up, w_down, w_gate, w_proj):
        n_loc = len(token_ids)
        layers, rows_dev, emb_dim = emb_table.shape
        n_hot = len(hot_ids)
        places, hot_dev, per_dev = n_loc // n_dev, n_hot // n_dev, FREQ // n_dev
        n_hi = -(-rows_dev * n_dev // (8 * LO)) * 8
        me = lax.axis_index('emb')
        hot_at, cold_at = FREQ, FREQ + hot_dev

        def swap(v):
            return lax.all_to_all(v, 'emb', 0, 0, tiled=True)

        def exchange(v):
            return swap(v.reshape(n_dev, places, -1)).reshape(n_loc, -1)

        def prepare(got_class, hot_hi, hot_lo, row_used, cold_owner, freq_cold, freq_map, hot_table, by_row, move, d_out):
            (hot_f,) = look((hot_hi, hot_lo), freq_map)
            used_rank = prefix(row_used.astype(I32))
            at_rank = (used_rank[None, :] == iota((COLD_MAX, rows_dev), 0)) & row_used[None, :]
            row_of = row_sum(jnp.where(at_rank, iota((COLD_MAX, rows_dev), 1), 0))
            packed = pack_rows(row_of, by_row)
            hot_pick = one_hot(hot_f - 1, FREQ_HOT).T
            by_owner = hot_table.reshape(layers, hot_dev // RUN, n_dev, RUN, emb_dim)
            hot_mine = lax.dynamic_index_in_dim(by_owner, me, 2, keepdims=False).reshape(layers, hot_dev, emb_dim)
            table = jnp.stack([jnp.concatenate([
                dot32(hot_pick, hot_table[i]).astype(BF), dot32(one_hot(cold_owner, n_dev), freq_cold[:, i]).astype(BF),
                hot_mine[i], packed[:, i]], axis=0) for i in range(layers)])
            n_blocks = 12 if rows_dev % 12 == 0 else 1
            edge_shape = (n_blocks + 1, rows_dev)
            before = iota(edge_shape, 1) < (rows_dev // n_blocks) * iota(edge_shape, 0)
            starts = jnp.minimum(row_sum(jnp.where(row_used[None, :] & before, 1, 0)), COLD_MAX)
            row_no = got_class - cold_at
            used_before = row_sum(jnp.where(row_used[None, :] & (iota((n_loc, rows_dev), 1) < row_no[:, None]), 1, 0))
            cls = jnp.where(row_no >= 0, cold_at + used_before, got_class)
            code = jnp.where(hot_f <= FREQ_HOT, hot_f - 1, -1)
            d_placed = dot32(move, d_out).astype(BF)
            return d_placed, table, cls, starts, row_of, code

        count = count_ids(swap(jnp.broadcast_to(token_ids[None, :], (n_dev, n_loc))), n_hi)
        tok, hot = digits(token_ids, n_hi), digits(hot_ids, n_hi)
        slot_no = jnp.arange(n_hot, dtype=I32)
        hot_place = slot_no // (RUN * n_dev) * RUN + slot_no % RUN
        hot_owner = slot_no // RUN % n_dev
        q_map = dot32(hot[0].T, hot[1] * (hot_place + 1).astype(BF)[:, None]).astype(BF)
        r_map = dot32(hot[0].T, hot[1] * hot_owner.astype(BF)[:, None]).astype(BF)
        hot_no = number(jnp.where(q_map > 0, count, 0), FREQ_HOT)
        cold_no = number(jnp.where(q_map > 0, 0, count), FREQ_COLD)
        freq_map = jnp.where(hot_no > 0, hot_no, jnp.where(cold_no > 0, FREQ_HOT + cold_no, 0)).astype(BF)
        id_map = iota((n_hi, LO), 0) * LO + iota((n_hi, LO), 1) + 1
        cold_id = jnp.sum(jnp.where(cold_no.astype(I32)[None] == iota((FREQ_COLD, 1, 1), 0) + 1, id_map[None], 0), axis=(1, 2)) - 1
        cold_owner = jnp.where(cold_id >= 0, cold_id // rows_dev, -1)
        my_cold = (cold_owner == me).astype(I32)
        my_row = jnp.minimum(jnp.sum(my_cold * (cold_id - me * rows_dev + 1)) - 1, rows_dev - 1)
        by_row = emb_table.transpose(1, 0, 2)
        cold_row = lax.dynamic_slice_in_dim(by_row, jnp.maximum(my_row, 0), 1)
        freq_cold = swap(jnp.broadcast_to(cold_row, (n_dev, layers, emb_dim)))

        tok_f, tok_q, tok_r = look(tok, freq_map, q_map, r_map)
        rare = tok_f == 0
        owner = jnp.where(tok_q > 0, tok_r, token_ids // rows_dev)
        dev_no = iota((n_loc, n_dev), 1)
        to_dev = (owner[:, None] == dev_no) & rare[:, None]
        marks = jnp.concatenate([to_dev.astype(BF), jnp.logical_not(rare).astype(BF)[:, None]], axis=1)
        r, c = square(n_loc)
        ranks = dot32((r > c).astype(BF), marks)
        sent = down_sum(to_dev.astype(F32))
        free = jnp.maximum(places - sent, 0)
        free_at = prefix(free)
        fill = ranks[:, n_dev:]
        fill_dev = (fill >= free_at) & (fill < free_at + free)
        to_dev = jnp.where(rare[:, None], to_dev, fill_dev)
        place = jnp.where(rare[:, None], ranks[:, :n_dev], fill + (sent - free_at))
        slot = row_sum(jnp.where(to_dev, dev_no * places + place.astype(I32), 0))
        row_ids = me * rows_dev + jnp.arange(rows_dev, dtype=I32)
        row_f, row_q, row_n = look(digits(row_ids, n_hi), freq_map, q_map, (count > 0).astype(BF))
        row_used = (row_n > 0) & (row_f == 0) & (row_q == 0)
        fits = ((jnp.max(sent) <= places) & (jnp.sum(row_used.astype(I32)) <= COLD_MAX) & (jnp.sum(my_cold) <= 1))
        tok_class = jnp.where(rare, jnp.where(tok_q > 0, hot_at + tok_q - 1, cold_at + token_ids % rows_dev), tok_f - 1)
        bad = 1 << 20
        move = r == slot[None, :]
        send_class, freq_cold = lax.optimization_barrier(
            (row_sum(jnp.where(move, tok_class[None, :], 0)) + jnp.where(fits, 0, bad), freq_cold))
        got_class = swap(send_class.reshape(n_dev, places)).reshape(n_loc)
        move = move.astype(BF)
        placed, got_class, hot_hi, hot_lo, row_used, cold_owner = lax.optimization_barrier(
            (dot32(move, x_in).astype(BF), got_class, *hot, row_used, cold_owner))
        x_moved = exchange(placed)
        given = prepare(got_class, hot_hi, hot_lo, row_used, cold_owner, freq_cold, freq_map, hot_table, by_row, move, d_out)
        all_fit = jnp.max(got_class) < bad

        def freq_parts(sums):
            return sums[:, :FREQ].reshape(2, n_dev, per_dev, emb_dim).transpose(1, 0, 2, 3)

        def own_hot(sums):
            return sums[:, hot_at:cold_at].reshape(-1, emb_dim)

        def fast(x_moved, slot, my_cold, my_row, d_placed, table, cls, starts, row_of, code):
            d_moved = exchange(d_placed)
            cls_row = cls.reshape(1, n_loc)
            xs, hs, ss, es, x_last = forward(x_moved, cls.reshape(n_loc, 1), table, w_up, w_down, w_gate, w_proj)
            x_back = exchange(x_last)
            kept = (cls_row, es, xs, hs, ss, w_up, w_down, w_gate, w_proj)
            sums_3, r = backward(3, 1, True, d_moved, *kept)
            all_3 = lax.all_gather(own_hot(sums_3), 'emb')
            sums_2, r = backward(2, 1, True, r, *kept)
            all_2 = lax.all_gather(own_hot(sums_2), 'emb')
            freq_a = swap(freq_parts(jnp.concatenate([sums_3, sums_2], axis=0)))
            r, x_back = lax.optimization_barrier((r, x_back))
            sums_b, _ = backward(1, 2, False, r, *kept)
            freq_b = swap(freq_parts(sums_b))
            x_out = dot32((slot[:, None] == iota((n_loc, n_loc), 1)).astype(BF), x_back).astype(BF)
            d_table = table_out(rows_dev, cold_at, starts, row_of, [(sums_b, 1), (sums_b, 0), (sums_2, 0), (sums_3, 0)])
            totals = [down_sum(v).reshape(2 * per_dev, emb_dim) for v in (freq_a, freq_b)]
            mine = jnp.concatenate([own_hot(sums_b)] + totals, axis=0)
            mine, x_out, d_table = lax.optimization_barrier((mine, x_out, d_table))
            all_b = gather_all(mine, n_dev)
            at_freq = 2 * hot_dev // (2 * RUN)
            into = empty((layers, n_hot, emb_dim))
            into = hot_out(1, 2, all_b, all_b, at_freq + 1, 0, code, into)
            into = hot_out(3, 1, all_3, all_b, at_freq, 0, code, into)
            into = hot_out(2, 1, all_2, all_b, at_freq, 1, code, into)
            pick = jnp.concatenate([jnp.zeros((FREQ_HOT,), F32), my_cold.astype(F32)]).reshape(n_dev, 1, per_dev, 1)
            freq = all_b[:, 2 * hot_dev:].reshape(n_dev, layers, per_dev, emb_dim)
            row = jnp.sum(freq * pick, axis=(0, 2))[::-1]
            d_table = put_row(my_row.reshape(1), row[None], d_table)
            return x_out, d_table.transpose(1, 0, 2), into

        def slow(*_):
            return general_path(n_dev, me, token_ids, hot_ids, x_in, d_out, emb_table, hot_table, w_up, w_down, w_gate, w_proj)

        return lax.cond(all_fit, fast, slow, *lax.optimization_barrier((x_moved, slot, my_cold, my_row, *given)))

    return jax.shard_map(body, mesh=mesh,
                         in_specs=(P('emb'), P(), P('emb', None), P('emb', None), P(None, 'emb', None), P(), P(), P(), P(), P()),
                         out_specs=(P('emb', None), P(None, 'emb', None), P()),
                         check_vma=False)
```

time: 807 us -> 747 us (0.926)
  Pallas kernels: 479 us -> 442 us
  waiting for transfers between devices: 43.8 us -> 27.7 us
  blocking collectives: 86 us -> 72.4 us
  local copies, waits for them, and re-layouts: 53.2 us -> 64.8 us
    pallas_call x1, Pallas kernels: 139 us -> 118 us  [forward(): pl.pallas_call(functools.partial(forward_kernel, n_l, n_f), grid=(n_l, n_...]
    reshape x6 -> x4, local copies, waits for them, and re-layouts: 6.31 us -> 25.9 us  [the longest x1 24.8 us: prepare(): by_owner = hot_table.reshape(layers, hot_dev // RUN, n_dev, RUN, emb_dim)]
    all_to_all x7, waiting for transfers between devices: 43.7 us -> 27.6 us  [swap(): return lax.all_to_all(v, 'emb', 0, 0, tiled=True)]
    pallas_call x6 -> x8, Pallas kernels: 209 us -> 193 us  [the longest x3 136 us: backward(): pl.pallas_call(functools.partial(backward_kernel, n_f, last_full), grid=(...]
    all_to_all x1, blocking collectives: 86 us -> 72.4 us  [swap(): return lax.all_to_all(v, 'emb', 0, 0, tiled=True)]
    slice x13 -> x5, local copies, waits for them, and re-layouts: 23.1 us -> 13.1 us  [the longest x1 8.69 us: prepare(): packed[:, i]]
    reduce_sum x21 -> x22, other arithmetic: 15.8 us -> 16.2 us  [the longest x12 8.63 us: row_sum(): return jnp.sum(v, axis=1)]
  transfers between devices with their start and end apart: 8 -> 9, of which waited for: 3 -> 4; matrix products, arithmetic and copies ran while one was open for 10% -> 14% of each run, Pallas kernels for 45% -> 51%
where the time goes in v1:
time: 747 us; the launch traced here: 739 us
  Pallas kernels  442 us (59%)
  blocking collectives  72.4 us (10%)
  local copies, waits for them, and re-layouts  64.8 us (9%)
  starting transfers between devices  42.6 us (6%)
  matrix products  32.9 us (4%)
  other arithmetic  29.6 us (4%)
  waiting for transfers between devices  27.7 us (4%)
  between operations  18 us (2%)
  loops' own time  9.24 us (1%)
    pallas_call x3, Pallas kernels, backward(): pl.pallas_call(functools.partial(backward_kernel, n_f, last_full), grid=(...  136 us
    pallas_call x1, Pallas kernels, forward(): pl.pallas_call(functools.partial(forward_kernel, n_l, n_f), grid=(n_l, n_...  118 us
    pallas_call x1, Pallas kernels, gather_all(): pl.pallas_call(gather_kernel, in_specs=[pl.BlockSpec(memory_space=pltpu.V...  104 us
    all_to_all x1, blocking collectives, swap(): return lax.all_to_all(v, 'emb', 0, 0, tiled=True)  72.4 us
    pallas_call x3, Pallas kernels, hot_out(): pl.pallas_call(functools.partial(hot_kernel, skip), grid=(n_l, blocks), i...  44.1 us
    all_to_all x7, starting transfers between devices, swap(): return lax.all_to_all(v, 'emb', 0, 0, tiled=True)  42.5 us
    dot_general x19, matrix products, dot32(): return jnp.dot(a, b, preferred_element_type=F32)  32.9 us
    all_to_all x7, waiting for transfers between devices, swap(): return lax.all_to_all(v, 'emb', 0, 0, tiled=True)  27.6 us
  transfers between devices with their start and end apart: 9, of which 4 were waited for; matrix products, arithmetic and copies ran while one was open for 14% of the time, Pallas kernels for 51%

profile of v1, /device:TPU:24, one launch (start us, length us, event | category | flops | bytes accessed | tf_op | source)
XLA Modules:
  0.0 739.2 jit_solution(10840507947851423560)
XLA Ops:
  7.2 3.1 copy.265
  11.0 5.9 all-to-all-start.7
  17.0 1.4 fusion.207
  20.4 24.8 %reshape.455 = bf16[4,16,32,4,1024]{4,3,2,1,0:T(4,128)(2,1)} reshape(bf16[4,2048,1024]{2,1,0:T(8,128)(2,1)} %param.23) | data formatting | bytes 33554432 | tf_op jit(solution)/shard_map/reshape | solution.py:641
  50.1 12.9 %count_ids.1 = f32[200,256]{1,0:T(8,128)} custom-call(s32[32,1024]{1,0:T(8,128)} %bitcast.345), custom_call_target="tpu_custom_call" | custom-call | tf_op jit(solution)/shard_map/count_ids/pallas_call | solution.py:377
  63.9 1.8 broadcast_select_fusion.2
  67.3 1.5 convert_reduce_fusion.2
  75.4 6.1 all-to-all-start.8
  88.1 5.4 fusion.209
  94.2 5.8 all-to-all-start.9
  100.1 3.7 fusion.208
  105.4 2.3 select_reduce_fusion.1
  109.1 7.1 all-to-all-start.10
  116.2 11.8 %pack_rows.1 = bf16[256,4,1024]{2,1,0:T(4,128)(2,1)} custom-call(s32[256]{0:T(256)S(1)} %select_reduce_fusion.4.row_of, bf16[1572,4,1024]{2,1,0:T(4,128)(2,1)} %bitcast.329), custom_call_target="tpu_custom_call" | custom-call | tf_op jit(solution)/shard_map/pack_rows/pallas_call | solution.py:390
  128.0 8.7 %fusion.309 = (bf16[256,1,1024]{2,1,0:T(2,128)(2,1)}, bf16[256,1,1024]{2,1,0:T(2,128)(2,1)S(1)}, bf16[256,1,1024]{2,1,0:T(2,128)(2,1)S(1)}, bf16[256,1,1024]{2,1,0:T(2,128)(2,1)S(1)}) fusion(bf16[256,4,1024]{2,1,0:T(4,128)(2,1)} %pack_rows.1), kind=kLoop, calls=%fused_computation.452 | loop fusion | bytes 4194304 | tf_op jit(solution)/shard_map/slice | solution.py:645
  138.1 1.5 copy.213
  142.4 3.0 fusion.217
  145.6 3.0 fusion.223
  148.9 3.0 fusion.220
  152.2 3.0 fusion.226
  155.8 2.1 pad_maximum_fusion.2
  157.9 4.9 all-to-all-done.10
  162.9 569.2 %conditional.1 = (bf16[1024,1024]{1,0:T(8,128)(2,1)}, f32[4,1572,1024]{2,0,1:T(4,128)}, f32[4,2048,1024]{2,1,0:T(8,128)}) conditional(s32[]{:T(128)} %convert_element_type.435, (s32[1024]{0:T(1024)S(1)}, s32[2048]{0:T(1024)S(1)}, s32[]{:T(128)}, bf16[4,1024,4096]{2,1,0:T(8,128)(2,1)}, bf16[4,4096,1024]{2,1,0:T(8,128)(2,1)}, ...), branch_computations={%region_29.45_spmd, %region_45.50_spmd} | conditional | flops 201674752000 | bytes 791882176 | solution.py:749
  171.7 6.0 all-to-all-start
  178.7 118.3 %forward.1 = (bf16[4,1024,1024]{2,1,0:T(8,128)(2,1)}, bf16[4,1024,4096]{2,1,0:T(8,128)(2,1)}, bf16[4,1024,1024]{2,1,0:T(8,128)(2,1)}, bf16[4,1024,1024]{2,1,0:T(8,128)(2,1)}, bf16[1024,1024]{1,0:T(8,128)(2,1)}) custom-call(bf16[1024,1024]{1,0:T(8,128)(2,1)} %get-tuple-element.470.x0, s32[1024,1]{1,0:T(8,128)} %copy.149.cls, ...), custom_call_target="tpu_custom_call" | custom-call | flops 89657442304 | bytes 160000000 | tf_op jit(solution)/shard_map/cond/branch_1_fun/forward/pallas_call | solution.py:216
  297.0 42.2 %backward.3 = (f32[1,448,1024]{2,1,0:T(8,128)}, f32[1024,1024]{1,0:T(8,128)}) custom-call(bf16[1024,1024]{1,0:T(8,128)(2,1)} %bitcast.5.r_in, s32[1,1024]{1,0:T(1,128)S(1)} %bitcast.350, bf16[4,1024,1024]{2,1,0:T(8,128)(2,1)} %get-tuple-element.476.es, bf16[4,1024,1024]{2,1,0:T(8,128)(2,1)} %get-tuple-element.477.xs, ...), custom_call_target="tpu_custom_call" | custom-call | flops 24293408768 | bytes 40000000 | tf_op jit(solution)/shard_map/cond/branch_1_fun/backward/pallas_call | solution.py:322
  339.2 1.7 slice.75
  340.9 42.9 %backward.4 = (f32[1,448,1024]{2,1,0:T(8,128)}, f32[1024,1024]{1,0:T(8,128)}) custom-call(f32[1024,1024]{1,0:T(8,128)} %get-tuple-element.480.r_in, s32[1,1024]{1,0:T(1,128)S(1)} %bitcast.351, bf16[4,1024,1024]{2,1,0:T(8,128)(2,1)} %get-tuple-element.476.es, bf16[4,1024,1024]{2,1,0:T(8,128)(2,1)} %get-tuple-element.477.xs, ...), custom_call_target="tpu_custom_call" | custom-call | flops 24293408768 | bytes 40000000 | tf_op jit(solution)/shard_map/cond/branch_1_fun/backward/pallas_call | solution.py:322
  383.8 1.7 slice.74
  385.5 72.4 %all_to_all.71 = bf16[32,32,1024]{2,1,0:T(8,128)(2,1)} all-to-all(bf16[32,32,1024]{2,1,0:T(8,128)(2,1)} %bitcast.338), channel_id=1, replica_groups=mesh['emb'=32] {'emb'}, dimensions={0} | all-to-all | bytes 4194304 | tf_op jit(solution)/shard_map/cond/branch_1_fun/all_to_all | solution.py:629
  458.0 51.0 %backward.5 = (f32[2,448,1024]{2,1,0:T(8,128)}, f32[1024,1024]{1,0:T(8,128)}) custom-call(f32[1024,1024]{1,0:T(8,128)} %get-tuple-element.483.r_in, s32[1,1024]{1,0:T(1,128)S(1)} %bitcast.352, bf16[4,1024,1024]{2,1,0:T(8,128)(2,1)} %get-tuple-element.476.es, bf16[4,1024,1024]{2,1,0:T(8,128)(2,1)} %get-tuple-element.477.xs, ...), custom_call_target="tpu_custom_call" | custom-call | flops 48586817536 | bytes 80000000 | tf_op jit(solution)/shard_map/cond/branch_1_fun/backward/pallas_call | solution.py:322
  509.0 2.4 slice.72
  511.4 1.5 reshape.444
  514.0 6.0 all-to-all-start.3
  520.1 2.1 pad_maximum_fusion
  522.2 1.5 reshape.442
  524.8 21.4 %all-to-all-done.3 = f32[32,2,4,1024]{3,2,1,0:T(4,128)S(1)} async-done(((f32[32,2,4,1024]{3,2,1,0:T(4,128)}), f32[32,2,4,1024]{3,2,1,0:T(4,128)S(1)}, u32[]{:S(2)}, u32[]{:S(2)}) %all-to-all-start.3) | async-done | bytes 1048608 | tf_op jit(solution)/shard_map/cond/branch_1_fun/all_to_all | solution.py:629
  546.2 5.6 all-to-all-start.2
  552.8 1.9 reshape.529.code
  555.8 13.3 %table_out.1.into = f32[1572,4,1024]{2,1,0:T(4,128)} custom-call(s32[13]{0:T(128)S(1)} %copy-done.32, s32[256]{0:T(256)S(1)} %copy-done.27, f32[2,448,1024]{2,1,0:T(8,128)} %get-tuple-element.484.refs_0_.refs_1_, f32[2,448,1024]{2,1,0:T(8,128)} %get-tuple-element.484.refs_0_.refs_1_, f32[1,448,1024]{2,1,0:T(8,128)} %get-tuple-element.486.refs_2_, ...), custom_call_target="tpu_custom_call" | custom-call | flops 3296722944 | bytes 160000000 | tf_op jit(solution)/shard_map/cond/branch_1_fun/table_out/pallas_call | solution.py:552
  569.1 5.4 fusion.6
  575.7 1.4 reduce_sum.279
  577.9 104.1 %gather_all.1.raw.freq = f32[32,144,1024]{2,1,0:T(8,128)} custom-call(f32[144,1024]{1,0:T(8,128)} %pad_maximum_fusion.1.mine), custom_call_target="tpu_custom_call" | custom-call | flops 2415919104 | bytes 40000000 | tf_op jit(solution)/shard_map/cond/branch_1_fun/gather_all/pallas_call | solution.py:479
  682.1 1.8 multiply_reduce_fusion
  684.0 2.4 rev.2
  687.8 21.3 %hot_out.3.into = f32[4,2048,1024]{2,1,0:T(8,128)} custom-call(f32[32,144,1024]{2,1,0:T(8,128)} %gather_all.1.raw.freq, f32[32,144,1024]{2,1,0:T(8,128)} %gather_all.1.raw.freq, s32[8,256,1]{2,1,0:T(8,128)} %reshape.529.code, f32[4,2048,1024]{2,1,0:T(8,128)} %empty.1.into), custom_call_target="tpu_custom_call", output_to_operand_aliasing={{}: (3, {})} | custom-call | flops 4831838208 | bytes 80000000 | tf_op jit(solution)/shard_map/cond/branch_1_fun/hot_out/pallas_call | solution.py:514
  709.0 11.4 %hot_out.4.into = f32[4,2048,1024]{2,1,0:T(8,128)} custom-call(f32[32,64,1024]{2,1,0:T(8,128)} %all-gather.5.cloned.1.call-done.raw, f32[32,144,1024]{2,1,0:T(8,128)} %gather_all.1.raw.freq, s32[8,256,1]{2,1,0:T(8,128)} %reshape.529.code, f32[4,2048,1024]{2,1,0:T(8,128)} %hot_out.3.into), custom_call_target="tpu_custom_call", output_to_operand_aliasing={{}: (3, {})} | custom-call | flops 1073741824 | bytes 40000000 | tf_op jit(solution)/shard_map/cond/branch_1_fun/hot_out/pallas_call | solution.py:514
  720.4 11.4 %hot_out.5 = f32[4,2048,1024]{2,1,0:T(8,128)} custom-call(f32[32,64,1024]{2,1,0:T(8,128)} %all-gather.3.cloned.1.call-done.raw, f32[32,144,1024]{2,1,0:T(8,128)} %gather_all.1.raw.freq, s32[8,256,1]{2,1,0:T(8,128)} %reshape.529.code, f32[4,2048,1024]{2,1,0:T(8,128)} %hot_out.4.into), custom_call_target="tpu_custom_call", output_to_operand_aliasing={{}: (3, {})} | custom-call | flops 1073741824 | bytes 40000000 | tf_op jit(solution)/shard_map/cond/branch_1_fun/hot_out/pallas_call | solution.py:514
  (153 shorter events, 38.1 us)
Async XLA Ops:
  7.2 3.1 copy-start.16
  7.2 9.8 %copy-start.28 = (s32[2048]{0:T(1024)S(1)}, s32[2048]{0:T(1024)}, u32[]{:S(2)}) copy-start(s32[2048]{0:T(1024)} %param.19) | copy-start | bytes 24580
  11.0 38.4 %all-to-all-start.7 = ((s32[32,1,1024]{2,1,0:T(1,128)}), s32[32,1,1024]{2,1,0:T(1,128)S(1)}, u32[]{:S(2)}, u32[]{:S(2)}) async-start(s32[32,1,1024]{2,1,0:T(1,128)} %broadcast_in_dim.315), calls=%async_computation.7 | async-start | bytes 262144 | tf_op jit(solution)/shard_map/all_to_all | solution.py:629
  45.2 20.4 %copy-start.31 = (f32[17]{0:T(128)S(1)}, f32[17]{0:T(128)}, u32[]{:S(2)}) copy-start(f32[17]{0:T(128)} %constant.429.clone) | copy-start | bytes 208
  69.4 15.2 %copy-start.13 = (bf16[200,256]{1,0:T(8,128)(2,1)}, bf16[200,256]{1,0:T(8,128)(2,1)S(1)}, u32[]{:S(2)}) copy-start(bf16[200,256]{1,0:T(8,128)(2,1)S(1)} %fusion.243) | copy-start | bytes 307204
  72.1 0.7 copy-start.22
  75.4 18.2 %all-to-all-start.8 = ((bf16[32,4,1024]{2,1,0:T(4,128)(2,1)}), bf16[32,4,1024]{2,1,0:T(4,128)(2,1)S(1)}, u32[]{:S(2)}, u32[]{:S(2)}) async-start(bf16[32,4,1024]{2,1,0:T(4,128)(2,1)} %broadcast_in_dim.330), calls=%async_computation.8 | async-start | bytes 524288 | tf_op jit(solution)/shard_map/all_to_all | solution.py:629
  84.2 15.9 %copy-start.24 = (s32[1024]{0:T(1024)}, s32[1024]{0:T(1024)S(1)}, u32[]{:S(2)}) copy-start(s32[1024]{0:T(1024)S(1)} %fusion.265) | copy-start | bytes 12292
  88.1 12.0 %copy-start = (bf16[1024,1024]{1,0:T(8,128)(2,1)S(1)}, bf16[1024,1024]{1,0:T(8,128)(2,1)}, u32[]{:S(2)}) copy-start(bf16[1024,1024]{1,0:T(8,128)(2,1)} %copy.265) | copy-start | bytes 6291460
  94.2 9.9 %all-to-all-start.9 = ((s32[32,1,32]{2,1,0:T(1,128)}), s32[32,1,32]{2,1,0:T(1,128)S(1)}, u32[]{:S(2)}, u32[]{:S(2)}) async-start(s32[32,1,32]{2,1,0:T(1,128)} %all_to_all.51), calls=%async_computation.9 | async-start | bytes 32768 | tf_op jit(solution)/shard_map/all_to_all | solution.py:629
  109.1 18.9 %copy-start.26 = (s32[256]{0:T(256)}, s32[256]{0:T(256)S(1)}, u32[]{:S(2)}) copy-start(s32[256]{0:T(256)S(1)} %select_reduce_fusion.4.row_of) | copy-start | bytes 3076
  109.1 53.8 %all-to-all-start.10 = ((bf16[32,32,1024]{2,1,0:T(8,128)(2,1)}), bf16[32,32,1024]{2,1,0:T(8,128)(2,1)}, u32[]{:S(2)}, u32[]{:S(2)}) async-start(bf16[32,32,1024]{2,1,0:T(8,128)(2,1)} %bitcast.336), calls=%async_computation.10 | async-start | bytes 4194304 | tf_op jit(solution)/shard_map/all_to_all | solution.py:629
  128.0 8.7 %copy-start.30 = (s32[1024]{0:T(1024)S(1)}, s32[1024]{0:T(1024)}, u32[]{:S(2)}) copy-start(s32[1024]{0:T(1024)} %select_reduce_fusion.1) | copy-start | bytes 12292
  138.0 3.0 copy-start.5
  138.0 3.0 copy-start.6
  138.0 3.0 copy-start.14
  138.1 4.1 copy-start.23
  140.1 5.3 copy-start.12
  145.4 3.3 copy-start.11
  148.6 3.3 copy-start.10
  155.2 7.7 %copy-start.29 = (s32[2048]{0:T(1024)S(1)}, s32[2048]{0:T(1024)}, u32[]{:S(2)}) copy-start(s32[2048]{0:T(1024)} %param.19) | copy-start | bytes 24580
  171.7 125.4 %all-to-all-start = ((bf16[32,32,1024]{2,1,0:T(8,128)(2,1)}), bf16[32,32,1024]{2,1,0:T(8,128)(2,1)}, u32[]{:S(2)}, u32[]{:S(2)}) async-start(bf16[32,32,1024]{2,1,0:T(8,128)(2,1)} %bitcast.335), calls=%async_computation | async-start | bytes 4194304 | tf_op jit(solution)/shard_map/cond/branch_1_fun/all_to_all | solution.py:629
  177.7 531.4 %all-gather.5.cloned.1.call-start = ((), (), s32[]{:S(2)}) async-start(), calls=%async_computation.12 | async-start | bytes 8650752 | tf_op jit(solution)/shard_map/cond/branch_1_fun/all_gather | solution.py:722
  340.9 379.5 %all-gather.3.cloned.1.call-start = ((), (), s32[]{:S(2)}) async-start(), calls=%async_computation.11 | async-start | bytes 8650752 | tf_op jit(solution)/shard_map/cond/branch_1_fun/all_gather | solution.py:724
  509.0 11.1 %copy-start.2 = (f32[1,448,1024]{2,1,0:T(8,128)S(1)}, f32[1,448,1024]{2,1,0:T(8,128)}, u32[]{:S(2)}) copy-start(f32[1,448,1024]{2,1,0:T(8,128)} %get-tuple-element.485.refs_3_) | copy-start | bytes 5505028 | tf_op jit(solution)/shard_map/cond
  514.0 32.2 %all-to-all-start.3 = ((f32[32,2,4,1024]{3,2,1,0:T(4,128)}), f32[32,2,4,1024]{3,2,1,0:T(4,128)S(1)}, u32[]{:S(2)}, u32[]{:S(2)}) async-start(f32[32,2,4,1024]{3,2,1,0:T(4,128)} %bitcast.330), calls=%async_computation.3 | async-start | bytes 2097152 | tf_op jit(solution)/shard_map/cond/branch_1_fun/all_to_all | solution.py:629
  546.2 5.6 copy-start.3
  546.2 29.4 %all-to-all-start.2 = ((f32[32,2,4,1024]{3,2,1,0:T(4,128)}), f32[32,2,4,1024]{3,2,1,0:T(4,128)}, u32[]{:S(2)}, u32[]{:S(2)}) async-start(f32[32,2,4,1024]{3,2,1,0:T(4,128)} %bitcast.245), calls=%async_computation.2 | async-start | bytes 2097152 | tf_op jit(solution)/shard_map/cond/branch_1_fun/all_to_all | solution.py:629
  551.8 0.6 copy-start.33
  551.8 1.0 copy-start.21
  551.9 3.9 copy-start.27
  551.9 3.9 copy-start.32
  555.8 13.3 %copy-start.25 = (s32[1024]{0:T(1024)S(1)}, s32[1024]{0:T(1024)}, u32[]{:S(2)}) copy-start(s32[1024]{0:T(1024)} %get-tuple-element.487) | copy-start | bytes 12292 | tf_op jit(solution)/shard_map/cond
  569.1 5.4 copy-start.4
Sparse Core Ops, SparseCore 0:
  341.0 104.4 all-gather.4
  448.3 81.8 all-gather.2

commit v2 on v1

v2 whole, which is shorter than its diff:
```python
import functools

import jax
import jax.numpy as jnp
from jax import lax
from jax.experimental import pallas as pl
from jax.experimental.pallas import tpu as pltpu
from jax.sharding import PartitionSpec as P


NORM_EPS = 1e-6
FREQ_HOT = 112
FREQ_COLD = 16
FREQ = FREQ_HOT + FREQ_COLD
COLD_MAX = 256
LO = 256
HI_BITS = 8
RUN = 4
LEVELS = tuple(16 * 2 ** (i / 4) for i in range(17))
GELU_A = 0.7978845608028654
GELU_B = GELU_A * 0.044715
VMEM = 66_000_000
ROWS_A = 256
ROWS_B = 512
TILE = 1024
BF = jnp.bfloat16
F32 = jnp.float32
I32 = jnp.int32
ONCE = pl.Buffered(1)


def gelu_back(pre_act, cot_in):
    _, pull = jax.vjp(jax.nn.gelu, pre_act.astype(F32))
    return pull(cot_in)[0]


def swap(v):
    return lax.all_to_all(v, 'emb', 0, 0, tiled=True)


def col(v):
    return v[:, None]


def row(v):
    return v[None, :]


def dot32(a, b):
    return jnp.dot(a, b, preferred_element_type=F32)


def dense_parts(resid, w_up, w_gate):
    resid_f = resid.astype(F32)
    inv_rms = lax.rsqrt(jnp.mean(resid_f * resid_f, axis=-1, keepdims=True) + NORM_EPS)
    normed = (resid_f * inv_rms).astype(BF)
    hidden = dot32(normed, w_up).astype(BF)
    gate_pre = dot32(normed, w_gate).astype(BF)
    return resid_f, inv_rms, hidden, gate_pre


def layer_forward(resid, emb_rows, w_up, w_down, w_gate, w_proj):
    resid_f, _, hidden, gate_pre = dense_parts(resid, w_up, w_gate)
    activated = jax.nn.gelu(hidden.astype(F32)).astype(BF)
    mlp_out = dot32(activated, w_down).astype(BF)
    gate = jax.nn.gelu(gate_pre.astype(F32)).astype(BF)
    mixed = (gate.astype(F32) * emb_rows.astype(F32)).astype(BF)
    projected = dot32(mixed, w_proj).astype(BF)
    return (resid_f + mlp_out.astype(F32) + projected.astype(F32)).astype(BF)


def layer_backward(resid, emb_rows, d_next, w_up, w_down, w_gate, w_proj):
    resid_f, inv_rms, hidden, gate_pre = dense_parts(resid, w_up, w_gate)
    gate = jax.nn.gelu(gate_pre.astype(F32)).astype(BF)
    d_cast = d_next.astype(BF)
    d_mixed = jnp.einsum('nd,ed->ne', d_cast, w_proj, preferred_element_type=F32)
    d_rows = gate.astype(F32) * d_mixed
    d_gpre = gelu_back(gate_pre, d_mixed * emb_rows.astype(F32))
    d_hidden = gelu_back(hidden, jnp.einsum('nd,fd->nf', d_cast, w_down, preferred_element_type=F32))
    d_normed = (jnp.einsum('nf,df->nd', d_hidden.astype(BF), w_up, preferred_element_type=F32)
                + jnp.einsum('ne,de->nd', d_gpre.astype(BF), w_gate, preferred_element_type=F32))
    inner = jnp.mean(d_normed * resid_f, axis=-1, keepdims=True)
    d_prev = d_next + inv_rms * d_normed - resid_f * (inv_rms * inv_rms * inv_rms) * inner
    return d_prev, d_rows


def general_path(n_dev, my_index, token_ids, hot_ids, x_in, d_out, emb_table, hot_table, w_up, w_down, w_gate, w_proj):
    n_loc = token_ids.shape[0]
    _, rows_dev, emb_dim = emb_table.shape
    capacity = max(8, (2 * n_loc) // n_dev)
    n_slots = n_dev * capacity
    hot_match = col(token_ids) == row(hot_ids)
    is_hot = hot_match.any(1)
    hot_pick = hot_match.astype(BF)
    hot_pick_f = hot_match.astype(F32)
    owner_id = token_ids // rows_dev
    to_owner = (col(owner_id) == row(jnp.arange(n_dev, dtype=I32))) & col(jnp.logical_not(is_hot))
    owner_rank = jnp.cumsum(to_owner.astype(jnp.int32), axis=0) - 1
    place = row_sum(jnp.where(to_owner, owner_rank, 0))
    slot = jnp.where(is_hot, n_slots, owner_id * capacity + place)
    none = jnp.full((n_slots,), -1, I32)
    send_ids = none.at[slot].set(token_ids, mode='drop')
    slot_tok = none.at[slot].set(jnp.arange(n_loc, dtype=jnp.int32), mode='drop')
    recv_ids = swap(send_ids.reshape(n_dev, capacity)).reshape(n_slots)
    served_ok = recv_ids >= 0
    local_row = jnp.where(served_ok, recv_ids - my_index * rows_dev, 0)
    pick_slot = jnp.minimum(slot, n_slots - 1)
    slot_used = slot_tok >= 0
    slot_src = jnp.maximum(slot_tok, 0)

    def fwd(resid, per_layer):
        table, hot_l, up, down, gate_w, proj = per_layer
        served = table[local_row]
        fetched = swap(served.reshape(n_dev, capacity, emb_dim)).reshape(n_slots, emb_dim)
        cold_rows = fetched[pick_slot]
        hot_rows = dot32(hot_pick, hot_l).astype(BF)
        emb_rows = jnp.where(col(is_hot), hot_rows, cold_rows)
        return layer_forward(resid, emb_rows, up, down, gate_w, proj), (resid, emb_rows)

    x_out, (x_saved, rows_saved) = lax.scan(fwd, x_in, (emb_table, hot_table, w_up, w_down, w_gate, w_proj))

    def bwd(d_resid, per_layer):
        resid_l, rows_l, up, down, gate_w, proj = per_layer
        d_resid, d_rows = layer_backward(resid_l, rows_l, d_resid, up, down, gate_w, proj)
        outgoing = jnp.where(col(slot_used), d_rows[slot_src], 0.0)
        incoming = swap(outgoing.reshape(n_dev, capacity, emb_dim)).reshape(n_slots, emb_dim)
        d_tab = jax.ops.segment_sum(jnp.where(col(served_ok), incoming, 0.0), local_row, num_segments=rows_dev)
        hot_local = jnp.einsum('nh,ne->he', hot_pick_f, d_rows, precision=lax.Precision.HIGHEST, preferred_element_type=F32)
        return d_resid, (d_tab, lax.psum(hot_local, 'emb'))

    _, (d_table, d_hot) = lax.scan(bwd, d_out.astype(F32), (x_saved, rows_saved, w_up, w_down, w_gate, w_proj), reverse=True)
    return x_out, d_table, d_hot


def split3(v):
    hi = v.astype(BF)
    rest = v - hi.astype(F32)
    mid = rest.astype(BF)
    return hi, mid, (rest - mid.astype(F32)).astype(BF)


def iota(shape, dim):
    return lax.broadcasted_iota(jnp.int32, shape, dim)


def one_hot(v, n, dtype=BF):
    return (col(v) == iota((len(v), n), 1)).astype(dtype)


def dot_nt(a, b):
    return lax.dot_general(a, b, (((1,), (1,)), ((), ())), preferred_element_type=F32)


def gelu(x):
    half = 0.5 * x
    return half + half * jnp.tanh(x * (GELU_A + GELU_B * (x * x)))


def gelu_slope(x):
    sq = x * x
    th = jnp.tanh(x * (GELU_A + GELU_B * sq))
    return (0.5 + 0.5 * th) + (0.5 * x) * (1.0 - th * th) * (GELU_A + (3.0 * GELU_B) * sq)


def forward_kernel(n_l, n_f, x0, cls, table, wu, wd, wg, wp, xs, hs, ss, es, xo, zeros, x_now, u_now, acc, q_now, blank, sem):
    layer, step = pl.program_id(0), pl.program_id(1)
    n_tok = x_now.shape[0]
    n_blank = blank.shape[0]
    blanks = [pltpu.make_async_copy(blank, zeros.at[pl.ds(i, n_blank)], sem) for i in range(0, zeros.shape[0], n_blank)]

    @pl.when((layer == 0) & (step == n_f - 1))
    def _():
        blank[...] = jnp.zeros(blank.shape, F32)
        for b in blanks:
            b.start()

    @pl.when((layer == n_l - 1) & (step == n_f - 1))
    def _():
        for b in blanks:
            b.wait()


    @pl.when((layer == 0) & (step == 0))
    def _():
        x_now[...] = x0[...]

    @pl.when(step == 0)
    def _():
        for m in chunks(n_tok, ROWS_A):
            xb = x_now[m, :]
            x = xb.astype(F32)
            xs[m, :] = xb
            u = (x * lax.rsqrt(jnp.mean(x * x, axis=-1, keepdims=True) + NORM_EPS)).astype(BF)
            u_now[m, :] = u
            s = dot32(u, wg[...]).astype(BF)
            ss[m, :] = s
            g = gelu(s.astype(F32)).astype(BF)
            pick = (cls[m, :] == iota((m.size, table.shape[0]), 1)).astype(BF)
            e = dot32(pick, table[...]).astype(BF)
            es[m, :] = e
            mixed = (g.astype(F32) * e.astype(F32)).astype(BF)
            q_now[m, :] = dot32(mixed, wp[...]).astype(BF)
            acc[m, :] = jnp.zeros((m.size, acc.shape[1]), F32)

    for m in chunks(n_tok, ROWS_B):
        h = dot32(u_now[m, :], wu[...]).astype(BF)
        hs[m, :] = h
        acc[m, :] += dot32(gelu(h.astype(F32)).astype(BF), wd[...])

    @pl.when(step == n_f - 1)
    def _():
        for m in chunks(n_tok, ROWS_A):
            x = x_now[m, :].astype(F32) + acc[m, :].astype(BF).astype(F32) + q_now[m, :].astype(F32)
            x_now[m, :] = x.astype(BF)

    @pl.when((step == n_f - 1) & (layer == n_l - 1))
    def _():
        xo[...] = x_now[...]


def chunks(n, size):
    size = min(n, size)
    return [pl.ds(m, size) for m in range(0, n, size)]


def forward(x0, cls, table, w_up, w_down, w_gate, w_proj, rows_dev):
    n_tok, dim = x0.shape
    n_l, _, ff = w_up.shape
    emb = w_gate.shape[2]
    tile = min(TILE, ff)
    n_f = ff // tile
    n_c = table.shape[1]

    def whole(l, f):
        return (l, 0, 0)

    def cols(l, f):
        return (l, 0, f)

    def fixed(l, f):
        return (0, 0)

    return pl.pallas_call(
        functools.partial(forward_kernel, n_l, n_f),
        grid=(n_l, n_f),
        in_specs=[
            pl.BlockSpec((n_tok, dim), fixed, pipeline_mode=ONCE),
            pl.BlockSpec((n_tok, 1), fixed, pipeline_mode=ONCE),
            pl.BlockSpec((None, n_c, emb), whole),
            pl.BlockSpec((None, dim, tile), cols),
            pl.BlockSpec((None, tile, dim), lambda l, f: (l, f, 0)),
            pl.BlockSpec((None, dim, emb), whole),
            pl.BlockSpec((None, emb, dim), whole),
        ],
        out_specs=[
            pl.BlockSpec((None, n_tok, dim), whole),
            pl.BlockSpec((None, n_tok, tile), cols),
            pl.BlockSpec((None, n_tok, emb), whole),
            pl.BlockSpec((None, n_tok, emb), whole),
            pl.BlockSpec((n_tok, dim), fixed),
            ANY,
        ],
        out_shape=[out_of((n_l, n_tok, n), BF) for n in (dim, ff, emb, emb)] + [out_of((n_tok, dim), BF), out_of((rows_dev, n_l, emb))],
        scratch_shapes=[pltpu.VMEM((n_tok, dim), t) for t in (BF, BF, F32, BF)]
        + [pltpu.VMEM((rows_dev // 12, n_l, emb), F32), pltpu.SemaphoreType.DMA(())],
        compiler_params=params("arbitrary", "arbitrary"),
        cost_estimate=cost(n_l * n_tok * dim * (2 * ff + 2 * emb + n_c), n_l),
        name="forward",
    )(x0, cls, table, w_up, w_down, w_gate, w_proj)


def params(*kinds, **more):
    return pltpu.CompilerParams(vmem_limit_bytes=VMEM, dimension_semantics=kinds or None, **more)


def cost(products, layers):
    return pl.CostEstimate(flops=2 * products, bytes_accessed=layers * 40_000_000, transcendentals=0)


def backward_kernel(n_f, r_in, cls_t, es, xs, hs, ss, wu, wd, wg, wp, *refs):
    talks = len(refs) > 5
    if talks:
        prev, sums, r, out, tot, c_now, acc, three, sems, sems_f, *bufs = refs
        at = Place()
        gather = Spread(at, prev.at[pl.ds(HOT_AT, COLD_AT - HOT_AT)], lambda d: out.at[d], sems)
        fold = Fold(at, prev.at[pl.ds(0, FREQ)], bufs, sems_f)
    else:
        sums, r, c_now, acc, three = refs
    f = pl.program_id(0)
    n_tok = c_now.shape[0]

    @pl.when(f == 0)
    def _():
        if talks:
            at.meet()
            gather.begin()
            fold.begin()
        r[...] = r_in[...].astype(F32)
        for m in chunks(n_tok, ROWS_B):
            c = r[m, :].astype(BF)
            c_now[m, :] = c
            a = dot_nt(c, wp[...])
            s = ss[m, :].astype(F32)
            rows = gelu(s).astype(BF).astype(F32) * a
            for i, part in enumerate(split3(rows)):
                three[i, m, :] = part
            ds = (gelu_slope(s) * (a * es[m, :].astype(F32))).astype(BF)
            acc[m, :] = dot_nt(ds, wg[...])
        class_sums(cls_t, three, sums)
        if talks:
            gather.column(1)
            gather.onward(0)
            fold.step(0)

    if talks:
        @pl.when(f == 1)
        def _():
            gather.column(2)
            gather.onward(1)
            fold.step(1)

        @pl.when(f == 2)
        def _():
            gather.column(3)
            gather.onward(2)
            fold.step(2)

        @pl.when(f == 3)
        def _():
            gather.across(0)
            gather.onward(3)
            tot[...] = fold.total()

    for m in chunks(n_tok, ROWS_B):
        d_act = dot_nt(c_now[m, :], wd[...])
        dh = (gelu_slope(hs[m, :].astype(F32)) * d_act).astype(BF)
        acc[m, :] += dot_nt(dh, wu[...])

    @pl.when(f == n_f - 1)
    def _():
        if talks:
            gather.across(1)
            gather.across(2)
        for m in chunks(n_tok, ROWS_A):
            x = xs[m, :].astype(F32)
            k = lax.rsqrt(jnp.mean(x * x, axis=-1, keepdims=True) + NORM_EPS)
            du = acc[m, :]
            inner = jnp.mean(du * x, axis=-1, keepdims=True)
            r[m, :] = r[m, :] + k * du - x * (k * k * k) * inner
        if talks:
            gather.across(3)
            gather.end()


def backward(layer, r_in, cls_t, es, xs, hs, ss, w_up, w_down, w_gate, w_proj, prev=None, n_dev=0):
    n_tok, dim = r_in.shape
    ff = w_up.shape[2]
    emb = w_gate.shape[2]
    n_c = COLD_AT + COLD_MAX
    n_f = 4
    tile = ff // n_f
    talks = prev is not None
    once = dict(pipeline_mode=ONCE)

    def whole(n, m):
        return spec((None, n, m), layer, 0, 0, **once)

    def cols(n):
        return pl.BlockSpec((None, n, tile), lambda t: (layer, 0, t))

    return pl.pallas_call(
        functools.partial(backward_kernel, n_f),
        grid=(n_f,),
        in_specs=[spec((n_tok, dim), **once), spec((1, n_tok), **once), whole(n_tok, emb), whole(n_tok, dim), cols(n_tok), whole(n_tok, emb),
                  cols(dim), pl.BlockSpec((None, tile, dim), lambda t: (layer, t, 0)), whole(dim, emb), whole(emb, dim)]
        + [spec((n_c, emb), **once)] * talks,
        out_specs=[spec((n_c, emb)), spec((n_tok, dim))] + [ANY, spec((16, emb))] * talks,
        out_shape=[out_of((n_c, emb)), out_of((n_tok, dim))] + [out_of((n_dev, COLD_AT - HOT_AT, emb)), out_of((16, emb))] * talks,
        scratch_shapes=[pltpu.VMEM((n_tok, dim), BF), pltpu.VMEM((n_tok, dim), F32), pltpu.VMEM((3, n_tok, emb), BF)]
        + ([SPREAD_SEMS, FOLD_SEMS] + fold_bufs(emb)) * talks,
        compiler_params=params("arbitrary", **(dict(collective_id=layer - 1, has_side_effects=True) if talks else {})),
        cost_estimate=cost(n_tok * dim * (2 * ff + 2 * emb + 3 * n_c), 1),
        name="backward",
    )(r_in, cls_t, es, xs, hs, ss, w_up, w_down, w_gate, w_proj, *([prev] if talks else []))


def spec(shape, *index, **more):
    index = index or (0,) * len(shape)
    return pl.BlockSpec(shape, lambda *_: index, **more)


ANY = pl.BlockSpec(memory_space=pl.ANY)


def out_of(shape, dtype=F32):
    return jax.ShapeDtypeStruct(shape, dtype)


def count_kernel(ids, out):
    n_tok = ids.shape[1]
    out[...] = jnp.zeros(out.shape, F32)

    @pl.loop(0, len(ids))
    def _(i):
        row = ids[pl.ds(i, 1), :]
        hi = ((row >> HI_BITS) == iota((len(out), n_tok), 0)).astype(BF)
        lo = ((row & (LO - 1)) == iota((LO, n_tok), 0)).astype(BF)
        out[...] += dot_nt(hi, lo)


def count_ids(ids, n_hi):
    return pl.pallas_call(count_kernel, out_shape=out_of((n_hi, LO)), compiler_params=params(), name="count_ids")(ids)


def pack_kernel(row_of, table, out, sem):
    @pl.loop(0, len(out))
    def _(k):
        pltpu.make_async_copy(table.at[row_of[k]], out.at[k], sem).start()

    pltpu.make_async_copy(table.at[pl.ds(0, len(out))], out, sem).wait()


def pack_rows(row_of, table):
    shape = row_of.shape + table.shape[1:]
    return pl.pallas_call(
        pack_kernel,
        grid_spec=pltpu.PrefetchScalarGridSpec(num_scalar_prefetch=1, grid=(1,), in_specs=[ANY], out_specs=spec(shape),
                                               scratch_shapes=[pltpu.SemaphoreType.DMA(())]),
        out_shape=out_of(shape, table.dtype), compiler_params=params(), name="pack_rows",
    )(row_of, table)


class Place:
    def __init__(self):
        me = lax.axis_index('emb')
        self.core, self.x, self.y, self.z = me % 2, (me // 2) % 2, (me // 4) % 2, me // 8
        self.others = [self.dev(z=(self.z + k) % 4) for k in REST]
        self.columns = [(self.z - k + 4) % 4 for k in STOPS]
        self.to_x, self.to_y, self.to_core = self.dev(x=1 - self.x), self.dev(y=1 - self.y), self.dev(core=1 - self.core)

    def dev(self, z=None, y=None, x=None, core=None):
        z, y, x, core = [mine if v is None else v for v, mine in ((z, self.z), (y, self.y), (x, self.x), (core, self.core))]
        return ((z * 2 + y) * 2 + x) * 2 + core

    def meet(self):
        barrier = pltpu.get_barrier_semaphore()
        peers = self.others + [self.to_x, self.to_y, self.to_core]
        for peer in peers:
            pl.semaphore_signal(barrier, device_id=(peer,), device_id_type=pl.DeviceIdType.MESH)
        pl.semaphore_wait(barrier, len(peers))


def remote(src, dst, sems, to):
    return pltpu.make_async_remote_copy(src_ref=src, dst_ref=dst, send_sem=sems[0], recv_sem=sems[1],
                                        device_id=(to,), device_id_type=pl.DeviceIdType.MESH)


Z, X, Y, FX, FY, C, CX, CY, CD, OWN = range(10)


class Spread:
    def __init__(self, at, mine, slot, sems):
        self.at, self.mine, self.slot, self.sems = at, mine, slot, sems
        n = mine.shape[0]
        half = n // 16 * 8
        self.halves = {FY: pl.ds(0, half), FX: pl.ds(half, n - half)}
        self.col = [at.dev(z=z) for z in at.columns]
        self.by_x = [at.dev(z=z, x=1 - at.x) for z in at.columns]
        self.by_y = [at.dev(z=z, y=1 - at.y) for z in at.columns]
        self.by_d = [at.dev(z=z, x=1 - at.x, y=1 - at.y) for z in at.columns]
        self.far = [[at.dev(z=z, x=x, y=y, core=1 - at.core) for z in at.columns]
                    for y, x in ((at.y, at.x), (at.y, 1 - at.x), (1 - at.y, at.x), (1 - at.y, 1 - at.x))]
        self.done = []

    def pair(self, kind, k):
        return self.sems.at[0, kind, k], self.sems.at[1, kind, k]

    def send(self, kind, k, src, dst, to):
        remote(src, dst, self.pair(kind, k), to).start()
        self.done.append((kind, k))

    def got(self, kind, k, block):
        remote(block, block, self.pair(kind, k), self.at.to_x).wait_recv()

    def begin(self):
        own = self.slot(self.col[0])
        pltpu.make_async_copy(self.mine, own, self.sems.at[0, OWN, 0]).start()
        for k, other in enumerate(self.at.others):
            self.send(Z, k + 1, self.mine, own, other)
        self.column(0)

    def column(self, k):
        block = self.slot(self.col[k])
        if k:
            self.got(Z, k, block)
        src = block if k else self.mine
        for kind, to in ((X, self.at.to_x), (Y, self.at.to_y), (C, self.at.to_core)):
            self.send(kind, k, src, block, to)

    def onward(self, k):
        for kind, part, to, other, core in ((X, self.by_x, self.at.to_y, FY, CX), (Y, self.by_y, self.at.to_x, FX, CY)):
            block = self.slot(part[k])
            self.got(kind, k, block)
            half = block.at[self.halves[other]]
            self.send(other, k, half, half, to)
            self.send(core, k, block, block, self.at.to_core)

    def across(self, k):
        block = self.slot(self.by_d[k])
        for kind, half in self.halves.items():
            self.got(kind, k, block.at[half])
        self.send(CD, k, block, block, self.at.to_core)

    def end(self):
        for k in STOPS:
            for kind, far in zip((C, CX, CY, CD), self.far):
                self.got(kind, k, self.slot(far[k]))
        own = self.slot(self.col[0])
        for kind, k in self.done:
            block = own.at[self.halves[kind]] if kind in self.halves else own
            remote(block, block, self.pair(kind, k), self.at.to_x).wait_send()
        pltpu.make_async_copy(self.mine, own, self.sems.at[0, OWN, 0]).wait()


class Fold:
    def __init__(self, at, part, bufs, sems):
        self.at, self.part, self.sems = at, part, sems
        self.ins, self.sums, self.all_z = bufs[:3], bufs[3:5], bufs[5]
        self.bits = at.core, at.x, at.y
        self.to = at.to_core, at.to_x, at.to_y

    def pair(self, i, k=0):
        return self.sems.at[0, i, k], self.sems.at[1, i, k]

    def cut(self, i, bit):
        n = self.ins[i].shape[0]
        return pl.ds(pl.multiple_of(bit * n, n), n)

    def source(self, i):
        return self.sums[i - 1] if i else self.part

    def hop(self, i):
        return remote(self.source(i).at[self.cut(i, 1 - self.bits[i])], self.ins[i], self.pair(i), self.to[i])

    def begin(self):
        self.hop(0).start()

    def step(self, i):
        self.hop(i).wait_recv()
        total = self.source(i)[self.cut(i, self.bits[i]), :] + self.ins[i][...]
        if i < 2:
            self.sums[i][...] = total
            self.hop(i + 1).start()
        else:
            self.all_z[self.at.z] = total
            for k, other in enumerate(self.at.others):
                self.along_z(k, other).start()

    def along_z(self, k, other):
        block = self.all_z.at[self.at.z]
        return remote(block, block, self.pair(3, k), other)

    def total(self):
        for k, other in enumerate(self.at.others):
            self.along_z(k, other).wait_recv()
        for i in range(3):
            self.hop(i).wait_send()
        for k, other in enumerate(self.at.others):
            self.along_z(k, other).wait_send()
        v = self.all_z
        return (v[0] + v[1]) + (v[2] + v[3])


def fold_bufs(emb):
    return [pltpu.VMEM((n, emb), F32) for n in (64, 32, 16, 64, 32)] + [pltpu.VMEM((4, 16, emb), F32)]


SPREAD_SEMS = pltpu.SemaphoreType.DMA((2, 10, 4))
STOPS = range(4)
REST = STOPS[1:]
FOLD_SEMS = pltpu.SemaphoreType.DMA((2, 4, 4))
HOT_AT, COLD_AT = FREQ, FREQ + 64


def last_kernel(r_in, ss, wp, cls_t, prev, *refs):
    early, (sums, out, r, s, w, three, pay, copies, sems_1, sems_0, sems_f1, sems_f0), bufs = refs[:2], refs[2:14], refs[14:]
    n_hot = COLD_AT - HOT_AT
    n = pay.shape[1]
    loads = [pltpu.make_async_copy(src, dst, copies.at[i]) for i, (src, dst) in enumerate(((r_in, r), (ss.at[0], s), (wp.at[0], w)))]
    for load in loads:
        load.start()
    at = Place()
    at.meet()

    def fill(i, hot, totals):
        pay[i, pl.ds(0, n_hot), :] = hot
        for z in STOPS:
            @pl.when(at.z == z)
            def _(z=z):
                for j, t in enumerate(totals):
                    pay[i, pl.ds(n_hot + RUN * j, RUN), :] = t[z * RUN:(z + 1) * RUN, :]

    fold_1 = Fold(at, prev.at[pl.ds(0, FREQ)], bufs[:6], sems_f1)
    fold_0 = Fold(at, sums.at[pl.ds(0, FREQ)], bufs[6:], sems_f0)
    all_1 = Spread(at, pay.at[0], lambda d: out.at[d, pl.ds(0, n)], sems_1)
    all_0 = Spread(at, pay.at[1], lambda d: out.at[d, pl.ds(n, n)], sems_0)
    fold_1.begin()
    fill(0, prev[pl.ds(HOT_AT, n_hot), :], [t[...] for t in early])
    all_1.begin()
    for load in loads:
        load.wait()
    for m in chunks(len(r), ROWS_B):
        a = dot_nt(r[m, :].astype(BF), w[...])
        rows = gelu(s[m, :].astype(F32)).astype(BF).astype(F32) * a
        for i, part in enumerate(split3(rows)):
            three[i, m, :] = part
    fold_1.step(0)
    class_sums(cls_t, three, sums)
    fold_0.begin()
    all_1.column(1)
    all_1.onward(0)
    fold_1.step(1)
    fold_0.step(0)
    all_1.column(2)
    all_1.onward(1)
    fold_1.step(2)
    fold_0.step(1)
    all_1.column(3)
    all_1.onward(2)
    total_1 = fold_1.total()
    fold_0.step(2)
    all_1.across(0)
    all_1.onward(3)
    fill(1, sums[pl.ds(HOT_AT, n_hot), :], [total_1, fold_0.total()])
    all_0.begin()
    for k in REST:
        all_1.across(k)
    for k in REST:
        all_0.column(k)
        all_0.onward(k - 1)
    all_0.across(0)
    all_0.onward(3)
    for k in REST:
        all_0.across(k)
    all_1.end()
    all_0.end()


def class_sums(cls_t, three, sums):
    pick_t = (cls_t[...] == iota((len(sums), cls_t.shape[1]), 0)).astype(BF)
    hi, mid, lo = [dot32(pick_t, three[i]) for i in range(3)]
    sums[...] = hi + (mid + lo)


def last(r_in, ss, w_proj, cls_t, prev, tot_3, tot_2, n_dev):
    n_tok, dim = r_in.shape
    n_c, emb = prev.shape
    n = COLD_AT - HOT_AT + 2 * RUN
    vmem = pl.BlockSpec(memory_space=pltpu.VMEM)
    return pl.pallas_call(
        last_kernel,
        in_specs=[ANY, ANY, ANY] + [vmem] * 4, out_specs=[vmem, ANY],
        out_shape=[out_of((n_c, emb)), out_of((n_dev, 2 * n, emb))],
        scratch_shapes=[pltpu.VMEM((n_tok, dim), F32), pltpu.VMEM((n_tok, emb), BF), pltpu.VMEM((emb, dim), BF),
                        pltpu.VMEM((3, n_tok, emb), BF), pltpu.VMEM((2, n, emb), F32), pltpu.SemaphoreType.DMA((3,)),
                        SPREAD_SEMS, SPREAD_SEMS, FOLD_SEMS, FOLD_SEMS] + fold_bufs(emb) * 2,
        compiler_params=params(collective_id=2, has_side_effects=True),
        cost_estimate=cost(n_tok * dim * 4 * emb, 1), name="last",
    )(r_in, ss, w_proj, cls_t, prev, tot_3, tot_2)


ORDER = [(b & 3) * 8 + (b >> 2 & 1) * 4 + (b >> 3 & 1) * 2 + (b >> 4) for b in range(FREQ // RUN)]


def hot_kernel(skip, any_freq, raw, freq, code, into, out, parts):
    n_dev, n_r, _ = raw.shape
    layer, block = pl.program_id(0), pl.program_id(1)
    n = RUN * n_dev
    for g in range(n_r // RUN):
        for o in range(n_dev):
            out[0, pl.ds(g * n + o * RUN, RUN), :] = raw[o, pl.ds(g * RUN, RUN), :]

    @pl.when(any_freq[block] > 0)
    def _():
        for j in range(2):
            @pl.when(layer + skip == j)
            def _(j=j):
                rows = jnp.concatenate([freq[o, j * RUN:(j + 1) * RUN, :] for o in ORDER])
                for i, part in enumerate(split3(rows)):
                    parts[i] = part
        sel = (code[0] == iota((n_r * n_dev, FREQ), 1)).astype(BF)
        out[0] += dot32(sel, parts[0]) + (dot32(sel, parts[1]) + dot32(sel, parts[2]))


def hot_out(first, n_l, gathered, stride, freq_from, freq_at, skip, code, into):
    n_dev, _, emb = gathered.shape
    n_r = 2 * RUN
    width = n_r * n_dev
    blocks = into.shape[1] // width
    code = code.reshape(blocks, width, 1)
    return pl.pallas_call(
        functools.partial(hot_kernel, skip),
        grid_spec=pltpu.PrefetchScalarGridSpec(
            num_scalar_prefetch=1, grid=(n_l, blocks),
            in_specs=[
                pl.BlockSpec((n_dev, n_r, emb), lambda i, b, _: (0, i * stride + b, 0)),
                spec((n_dev, n_r, emb), 0, freq_at, 0, pipeline_mode=ONCE),
                pl.BlockSpec((1, width, 1), lambda i, b, _: (b, 0, 0)),
                ANY,
            ],
            out_specs=pl.BlockSpec((1, width, emb), lambda i, b, _: (first - i, b, 0)),
            scratch_shapes=[pltpu.VMEM((3, FREQ, emb), BF)]),
        out_shape=out_of(into.shape),
        input_output_aliases={4: 0},
        compiler_params=params("arbitrary", "arbitrary"),
        cost_estimate=cost(n_l * gathered.size * LO, n_l), name="hot_out",
    )((code[:, :, 0] >= 0).any(axis=1).astype(I32), gathered, freq_from, code, into)


def empty(shape):
    return pl.pallas_call(lambda out: None, out_specs=ANY, out_shape=out_of(shape), name="empty")()


def rows_kernel(numbers, row_of, *refs):
    srcs, (freq, into, out, stage, got, sem) = refs[:-6], refs[-6:]
    n_used, cold_row, cold_no = [numbers[i] for i in range(3)]
    n_l = len(srcs)

    def put(k, row):
        return pltpu.make_async_copy(stage.at[pl.ds(k, 1)], out.at[pl.ds(row, 1)], sem)

    @pl.loop(0, n_used)
    def _(k):
        for l, src in enumerate(srcs):
            stage[k, pl.ds(l, 1), :] = src[pl.ds(COLD_AT + k, 1), :]
        put(k, row_of[k]).start()

    @pl.when(cold_row >= 0)
    def _():
        n = freq.shape[1] // 2
        for j in range(2):
            c = pltpu.make_async_copy(freq.at[cold_no // RUN * 8 + 7, pl.ds(j * n + n - 8, 8)], got.at[j], sem)
            c.start()
            c.wait()
        for l in range(n_l):
            i = n_l - 1 - l
            stage[COLD_MAX, pl.ds(l, 1), :] = got[i // 2, pl.ds(i % 2 * RUN + cold_no % RUN, 1), :]
        put(COLD_MAX, cold_row).start()
        put(0, 0).wait()

    @pl.loop(0, n_used)
    def _(k):
        put(0, 0).wait()


def put_rows(numbers, row_of, srcs, freq, into):
    n_l = len(srcs)
    shape = srcs[0].shape
    emb = shape[-1]
    return pl.pallas_call(
        rows_kernel,
        grid_spec=pltpu.PrefetchScalarGridSpec(
            num_scalar_prefetch=2, grid=(1,),
            in_specs=[spec(shape)] * n_l + [ANY, ANY], out_specs=ANY,
            scratch_shapes=[pltpu.VMEM((COLD_MAX + 1, n_l, emb), F32), pltpu.VMEM((2, 8, emb), F32), pltpu.SemaphoreType.DMA(())]),
        out_shape=out_of(into.shape), input_output_aliases={n_l + 3: 0},
        compiler_params=params("arbitrary"), name="put_rows",
    )(numbers, row_of, *srcs, freq, into)


def down_sum(v):
    return jnp.sum(v, axis=0)


def beside(*v):
    return jnp.concatenate(v, axis=1)


def row_sum(v):
    return jnp.sum(v, axis=1)


def square(n):
    return iota((n, n), 0), iota((n, n), 1)


def prefix(v):
    r, c = square(len(v))
    return row_sum(jnp.where(r > c, row(v), 0))


def digits(ids, n_hi):
    return one_hot(ids >> HI_BITS, n_hi), one_hot(ids & (LO - 1), LO)


def look(hi_lo, *maps):
    hi, lo = hi_lo
    got = dot32(hi, beside(*maps))
    return [row_sum(got[:, i * LO:(i + 1) * LO] * lo.astype(F32)).astype(I32) for i in range(len(maps))]


def number(count, most):
    levels = jnp.array(LEVELS, F32)
    n_over = jnp.sum((count[:, :, None] >= levels).astype(F32), axis=(0, 1))
    flag = count >= jnp.min(jnp.where(n_over <= most, levels, jnp.inf))
    r, c = square(LO)
    in_row = dot32(flag.astype(BF), (r < c).astype(BF))
    return jnp.where(flag, in_row + col(prefix(row_sum(flag.astype(F32)))) + 1, 0)


def solution(mesh):
    n_dev = mesh.shape['emb']

    def body(token_ids, hot_ids, x_in, d_out, emb_table, hot_table, w_up, w_down, w_gate, w_proj):
        n_loc = len(token_ids)
        layers, rows_dev, emb_dim = emb_table.shape
        n_hot = len(hot_ids)
        places, hot_dev = n_loc // n_dev, n_hot // n_dev
        n_hi = -(-rows_dev * n_dev // (8 * LO)) * 8
        me = lax.axis_index('emb')
        hot_at, cold_at = FREQ, FREQ + hot_dev

        def exchange(v):
            return swap(v.reshape(n_dev, places, -1)).reshape(n_loc, -1)

        def prepare(got_class, hot_hi, hot_lo, row_used, cold_owner, freq_cold, freq_map, hot_table, by_row, move, d_out):
            (hot_f,) = look((hot_hi, hot_lo), freq_map)
            used_rank = prefix(row_used.astype(I32))
            at_rank = (row(used_rank) == iota((COLD_MAX, rows_dev), 0)) & row(row_used)
            row_of = row_sum(jnp.where(at_rank, iota((COLD_MAX, rows_dev), 1), 0))
            packed = pack_rows(row_of, by_row)
            mine_no = jnp.where(hot_owner == me, FREQ_HOT + hot_place, -1)
            hot_pick = (one_hot(hot_f - 1, FREQ_HOT + hot_dev) * col((hot_f <= FREQ_HOT).astype(BF)) + one_hot(mine_no, FREQ_HOT + hot_dev)).T
            hot_rows = [dot32(hot_pick, hot_table[i]).astype(BF) for i in range(layers)]
            table = jnp.stack([jnp.concatenate([
                hot_rows[i][:FREQ_HOT], dot32(one_hot(cold_owner, n_dev), freq_cold[:, i]).astype(BF),
                hot_rows[i][FREQ_HOT:], packed[:, i]]) for i in range(layers)])
            n_used = jnp.minimum(jnp.sum(row_used.astype(I32)), COLD_MAX)
            row_no = got_class - cold_at
            used_before = row_sum(jnp.where(row(row_used) & (iota((n_loc, rows_dev), 1) < col(row_no)), 1, 0))
            cls = jnp.where(row_no >= 0, cold_at + used_before, got_class)
            code = jnp.where(hot_f <= FREQ_HOT, hot_f - 1, -1)
            d_placed = dot32(move, d_out).astype(BF)
            return d_placed, table, cls, n_used, row_of, code

        count = count_ids(swap(jnp.broadcast_to(row(token_ids), (n_dev, n_loc))), n_hi)
        tok, hot = digits(token_ids, n_hi), digits(hot_ids, n_hi)
        slot_no = jnp.arange(n_hot, dtype=I32)
        hot_place = slot_no // (RUN * n_dev) * RUN + slot_no % RUN
        hot_owner = slot_no // RUN % n_dev
        q_map = dot32(hot[0].T, hot[1] * col((hot_place + 1).astype(BF))).astype(BF)
        r_map = dot32(hot[0].T, hot[1] * col(hot_owner.astype(BF))).astype(BF)
        hot_no = number(jnp.where(q_map > 0, count, 0), FREQ_HOT)
        cold_no = number(jnp.where(q_map > 0, 0, count), FREQ_COLD)
        freq_map = jnp.where(hot_no > 0, hot_no, jnp.where(cold_no > 0, FREQ_HOT + cold_no, 0)).astype(BF)
        id_map = iota((n_hi, LO), 0) * LO + iota((n_hi, LO), 1) + 1
        cold_id = jnp.sum(jnp.where(cold_no.astype(I32)[None] == iota((FREQ_COLD, 1, 1), 0) + 1, id_map[None], 0), axis=(1, 2)) - 1
        cold_owner = jnp.where(cold_id >= 0, cold_id // rows_dev, -1)
        my_cold = (cold_owner == me).astype(I32)
        my_row = jnp.minimum(jnp.sum(my_cold * (cold_id - me * rows_dev + 1)) - 1, rows_dev - 1)
        by_row = emb_table.transpose(1, 0, 2)
        cold_row = lax.dynamic_slice_in_dim(by_row, jnp.maximum(my_row, 0), 1)
        freq_cold = swap(jnp.broadcast_to(cold_row, (n_dev, layers, emb_dim)))

        tok_f, tok_q, tok_r = look(tok, freq_map, q_map, r_map)
        rare = tok_f == 0
        owner = jnp.where(tok_q > 0, tok_r, token_ids // rows_dev)
        dev_no = iota((n_loc, n_dev), 1)
        to_dev = (col(owner) == dev_no) & col(rare)
        marks = beside(to_dev.astype(BF), col(jnp.logical_not(rare).astype(BF)))
        r, c = square(n_loc)
        ranks = dot32((r > c).astype(BF), marks)
        sent = down_sum(to_dev.astype(F32))
        free = jnp.maximum(places - sent, 0)
        free_at = prefix(free)
        fill = ranks[:, n_dev:]
        fill_dev = (fill >= free_at) & (fill < free_at + free)
        to_dev = jnp.where(col(rare), to_dev, fill_dev)
        place = jnp.where(col(rare), ranks[:, :n_dev], fill + (sent - free_at))
        slot = row_sum(jnp.where(to_dev, dev_no * places + place.astype(I32), 0))
        row_ids = me * rows_dev + jnp.arange(rows_dev, dtype=I32)
        row_f, row_q, row_n = look(digits(row_ids, n_hi), freq_map, q_map, (count > 0).astype(BF))
        row_used = (row_n > 0) & (row_f == 0) & (row_q == 0)
        fits = ((jnp.max(sent) <= places) & (jnp.sum(row_used.astype(I32)) <= COLD_MAX) & (jnp.sum(my_cold) <= 1))
        tok_class = jnp.where(rare, jnp.where(tok_q > 0, hot_at + tok_q - 1, cold_at + token_ids % rows_dev), tok_f - 1)
        bad = 1 << 20
        move = r == row(slot)
        send_class, freq_cold = lax.optimization_barrier(
            (row_sum(jnp.where(move, row(tok_class), 0)) + jnp.where(fits, 0, bad), freq_cold))
        got_class = swap(send_class.reshape(n_dev, places)).reshape(n_loc)
        move = move.astype(BF)
        placed, got_class, hot_hi, hot_lo, row_used, cold_owner = lax.optimization_barrier(
            (dot32(move, x_in).astype(BF), got_class, *hot, row_used, cold_owner))
        x_moved = exchange(placed)
        given = prepare(got_class, hot_hi, hot_lo, row_used, cold_owner, freq_cold, freq_map, hot_table, by_row, move, d_out)
        all_fit = jnp.max(got_class) < bad

        def fast(x_moved, slot, my_cold, my_row, d_placed, table, cls, n_used, row_of, code):
            d_moved = exchange(d_placed)
            cls_row = cls.reshape(1, n_loc)
            xs, hs, ss, es, x_last, zeros = forward(x_moved, cls.reshape(n_loc, 1), table, w_up, w_down, w_gate, w_proj, rows_dev)
            x_back = exchange(x_last)
            kept = (cls_row, es, xs, hs, ss, w_up, w_down, w_gate, w_proj)
            sums_3, r = backward(3, d_moved, *kept)
            sums_2, r, all_3, tot_3 = backward(2, r, *kept, sums_3, n_dev)
            r, x_back = lax.optimization_barrier((r, x_back))
            sums_1, r, all_2, tot_2 = backward(1, r, *kept, sums_2, n_dev)
            sums_0, all_b = last(r, ss, w_proj, cls_row, sums_1, tot_3, tot_2, n_dev)
            x_out = dot32((col(slot) == iota((n_loc, n_loc), 1)).astype(BF), x_back).astype(BF)
            numbers = jnp.stack([n_used, my_row, jnp.sum(my_cold * jnp.arange(FREQ_COLD, dtype=I32))])
            d_table = put_rows(numbers, row_of, [sums_0, sums_1, sums_2, sums_3], all_b, zeros)
            at_freq = hot_dev // (2 * RUN)
            into = empty((layers, n_hot, emb_dim))
            into = hot_out(3, 1, all_3, 0, all_b, at_freq, 0, code, into)
            into = hot_out(2, 1, all_2, 0, all_b, at_freq, 1, code, into)
            into = hot_out(1, 2, all_b, at_freq + 1, all_b, 2 * at_freq + 1, 0, code, into)
            return x_out, d_table.transpose(1, 0, 2), into

        def slow(*_):
            return general_path(n_dev, me, token_ids, hot_ids, x_in, d_out, emb_table, hot_table, w_up, w_down, w_gate, w_proj)

        return lax.cond(all_fit, fast, slow, *lax.optimization_barrier((x_moved, slot, my_cold, my_row, *given)))

    return jax.shard_map(body, mesh=mesh,
                         in_specs=(P('emb'), P(), P('emb', None), P('emb', None), P(None, 'emb', None), P(), P(), P(), P(), P()),
                         out_specs=(P('emb', None), P(None, 'emb', None), P()),
                         check_vma=False)
```

time: 747 us -> 644 us (0.86)
  the two profiles are of different devices: /device:TPU:24 before, /device:TPU:0 now
where the time goes in v2:
time: 644 us; the launch traced here: 633 us
  Pallas kernels  468 us (73%)
  matrix products  40.5 us (6%)
  starting transfers between devices  28.6 us (4%)
  waiting for transfers between devices  23.6 us (4%)
  other arithmetic  22.7 us (4%)
  local copies, waits for them, and re-layouts  20.3 us (3%)
  between operations  19 us (3%)
  loops' own time  9.76 us (2%)
    pallas_call x3, Pallas kernels, backward(): pl.pallas_call(functools.partial(backward_kernel, n_f), grid=(n_f,), in_s...  172 us
    pallas_call x1, Pallas kernels, forward(): pl.pallas_call(functools.partial(forward_kernel, n_l, n_f), grid=(n_l, n_...  123 us
    pallas_call x1, Pallas kernels, last(): pl.pallas_call(last_kernel, in_specs=[ANY, ANY, ANY] + [vmem] * 4, out_sp...  103 us
    pallas_call x3, Pallas kernels, hot_out(): pl.pallas_call(functools.partial(hot_kernel, skip), grid_spec=pltpu.Prefe...  43.5 us
    dot_general x19, matrix products, dot32(): return jnp.dot(a, b, preferred_element_type=F32)  40.5 us
    all_to_all x6, starting transfers between devices, swap(): return lax.all_to_all(v, 'emb', 0, 0, tiled=True)  28.6 us
    all_to_all x6, waiting for transfers between devices, swap(): return lax.all_to_all(v, 'emb', 0, 0, tiled=True)  23.6 us
    pallas_call x1, Pallas kernels, count_ids(): pl.pallas_call(count_kernel, out_shape=out_of((n_hi, LO)), compiler_param...  12.9 us
  transfers between devices with their start and end apart: 6, of which 4 were waited for; matrix products, arithmetic and copies ran while one was open for 7% of the time, Pallas kernels for 38%

profile of v2, /device:TPU:0, one launch (start us, length us, event | category | flops | bytes accessed | tf_op | source)
XLA Modules:
  0.0 632.5 jit_solution(6856679443530444825)
XLA Ops:
  7.2 3.1 copy.233
  11.0 7.3 %all-to-all-start.5 = ((s32[32,1,1024]{2,1,0:T(1,128)}), s32[32,1,1024]{2,1,0:T(1,128)S(1)}, u32[]{:S(2)}, u32[]{:S(2)}) async-start(s32[32,1,1024]{2,1,0:T(1,128)} %broadcast_in_dim.279), calls=%async_computation.5 | async-start | bytes 262144 | tf_op jit(solution)/shard_map/all_to_all | solution.py:38
  18.4 1.3 fusion.207
  19.8 1.2 fusion.204
  20.9 0.9 convolution_convert_fusion
  22.0 4.6 all-to-all-done.5
  27.2 12.9 %count_ids.1 = f32[200,256]{1,0:T(8,128)} custom-call(s32[32,1024]{1,0:T(8,128)} %bitcast.312), custom_call_target="tpu_custom_call" | custom-call | tf_op jit(solution)/shard_map/count_ids/pallas_call | solution.py:412
  40.1 1.8 broadcast_select_fusion.2
  41.9 1.0 convert_reduce_fusion
  43.6 1.4 convert_reduce_fusion.2
  45.7 0.8 fusion.255
  51.9 0.8 broadcast_in_dim.294
  52.7 2.6 all-to-all-start.6
  56.6 0.9 fusion.215
  57.5 1.2 fusion.214
  60.6 3.7 fusion.210
  64.3 1.6 all-to-all-done.6
  66.5 4.3 all-to-all-start.7
  70.8 5.4 fusion.211
  76.3 1.6 all-to-all-done.7
  79.8 4.9 fusion.228
  84.7 4.9 fusion.225
  89.6 5.0 fusion.222
  94.6 4.3 all-to-all-start.8
  99.0 4.9 fusion.219
  105.3 1.7 select_reduce_fusion.1
  108.6 1.1 select_reduce_fusion.4.row_of
  109.7 8.0 %pack_rows.1 = bf16[256,4,1024]{2,1,0:T(4,128)(2,1)} custom-call(s32[256]{0:T(256)S(1)} %select_reduce_fusion.4.row_of, bf16[1572,4,1024]{2,1,0:T(4,128)(2,1)} %bitcast.303), custom_call_target="tpu_custom_call" | custom-call | tf_op jit(solution)/shard_map/pack_rows/pallas_call | solution.py:425
  117.8 7.9 %fusion.328 = (bf16[256,1,1024]{2,1,0:T(2,128)(2,1)S(1)}, bf16[256,1,1024]{2,1,0:T(2,128)(2,1)S(1)}, bf16[256,1,1024]{2,1,0:T(2,128)(2,1)S(1)}, bf16[256,1,1024]{2,1,0:T(2,128)(2,1)S(1)}) fusion(bf16[256,4,1024]{2,1,0:T(4,128)(2,1)} %pack_rows.1), kind=kLoop, calls=%fused_computation.455 | loop fusion | bytes 4194304 | tf_op jit(solution)/shard_map/slice | solution.py:837
  127.9 1.1 maximum_bitcast_fusion.3
  129.8 2.1 pad_maximum_fusion
  131.9 15.8 %all-to-all-done.8 = bf16[32,32,1024]{2,1,0:T(8,128)(2,1)} async-done(((bf16[32,32,1024]{2,1,0:T(8,128)(2,1)}), bf16[32,32,1024]{2,1,0:T(8,128)(2,1)}, u32[]{:S(2)}, u32[]{:S(2)}) %all-to-all-start.8) | async-done | bytes 2097184 | tf_op jit(solution)/shard_map/all_to_all | solution.py:38
  147.7 477.5 %conditional.1 = (bf16[1024,1024]{1,0:T(8,128)(2,1)}, f32[4,1572,1024]{2,0,1:T(4,128)}, f32[4,2048,1024]{2,1,0:T(8,128)}) conditional(s32[]{:T(128)} %convert_element_type.451, (s32[1024]{0:T(1024)S(1)}, s32[2048]{0:T(1024)S(1)}, s32[]{:T(128)}, bf16[4,1024,4096]{2,1,0:T(8,128)(2,1)}, bf16[4,4096,1024]{2,1,0:T(8,128)(2,1)}, ...), branch_computations={%region_29.45_spmd, %region_45.48_spmd} | conditional | flops 180256505856 | bytes 561294080 | solution.py:922
  157.1 4.2 all-to-all-start
  161.4 1.0 copy.131.cls
  162.4 122.9 %forward.1 = (bf16[4,1024,1024]{2,1,0:T(8,128)(2,1)}, bf16[4,1024,4096]{2,1,0:T(8,128)(2,1)}, bf16[4,1024,1024]{2,1,0:T(8,128)(2,1)}, bf16[4,1024,1024]{2,1,0:T(...) custom-call(bf16[1024,1024]{1,0:T(8,128)(2,1)} %get-tuple-element.471.x0, s32[1024,1]{1,0:T(8,128)} %copy.131.cls, ...), custom_call_target="tpu_custom_call" | custom-call | flops 89657442304 | bytes 160000000 | tf_op jit(solution)/shard_map/cond/branch_1_fun/forward/pallas_call | solution.py:243
  285.3 1.8 reshape.471.code
  288.4 1.2 pad_add_fusion.numbers
  289.6 5.9 all-to-all-start.1
  295.5 41.0 %backward.3 = (f32[448,1024]{1,0:T(8,128)}, f32[1024,1024]{1,0:T(8,128)}) custom-call(bf16[1024,1024]{1,0:T(8,128)(2,1)} %bitcast.5.r_in, s32[1,1024]{1,0:T(1,128)S(1)} %bitcast.318, bf16[4,1024,1024]{2,1,0:T(8,128)(2,1)} %get-tuple-element.477.es, bf16[4,1024,1024]{2,1,0:T(8,128)(2,1)} %get-tuple-element.478.xs, ...), custom_call_target="tpu_custom_call" | custom-call | flops 24293408768 | bytes 40000000 | tf_op jit(solution)/shard_map/cond/branch_1_fun/backward/pallas_call | solution.py:371
  336.5 65.7 %backward.4 = (f32[448,1024]{1,0:T(8,128)}, f32[1024,1024]{1,0:T(8,128)}, f32[32,64,1024]{2,1,0:T(8,128)}, f32[16,1024]{1,0:T(8,128)}) custom-call(f32[1024,1024]{1,0:T(8,128)} %get-tuple-element.481.r_in, s32[1,1024]{1,0:T(1,128)S(1)} %bitcast.319, bf16[4,1024,1024]{2,1,0:T(8,128)(2,1)} %get-tuple-element.477.es, ...), custom_call_target="tpu_custom_call" | custom-call | flops 24293408768 | bytes 40000000 | tf_op jit(solution)/shard_map/cond/branch_1_fun/backward/pallas_call | solution.py:371
  402.2 64.8 %backward.5 = (f32[448,1024]{1,0:T(8,128)}, f32[1024,1024]{1,0:T(8,128)}, f32[32,64,1024]{2,1,0:T(8,128)}, f32[16,1024]{1,0:T(8,128)}) custom-call(f32[1024,1024]{1,0:T(8,128)} %get-tuple-element.490.r_in, s32[1,1024]{1,0:T(1,128)S(1)} %bitcast.320, bf16[4,1024,1024]{2,1,0:T(8,128)(2,1)} %get-tuple-element.477.es, ...), custom_call_target="tpu_custom_call" | custom-call | flops 24293408768 | bytes 40000000 | tf_op jit(solution)/shard_map/cond/branch_1_fun/backward/pallas_call | solution.py:371
  467.0 103.5 %last.1 = (f32[448,1024]{1,0:T(8,128)}, f32[32,144,1024]{2,1,0:T(8,128)}) custom-call(f32[1024,1024]{1,0:T(8,128)} %get-tuple-element.492.r_in, bf16[4,1024,1024]{2,1,0:T(8,128)(2,1)} %get-tuple-element.480.ss, bf16[4,1024,1024]{2,1,0:T(8,128)(2,1)} %get-tuple-element.476.wp, s32[1,1024]{1,0:T(1,128)S(1)} %bitcast.321, ...), custom_call_target="tpu_custom_call" | custom-call | flops 8589934592 | bytes 40000000 | tf_op jit(solution)/shard_map/cond/branch_1_fun/last/pallas_call | solution.py:660
  570.5 11.2 %hot_out.3.into = f32[4,2048,1024]{2,1,0:T(8,128)} custom-call(s32[8]{0:T(128)} %convert_element_type.377.any_freq, f32[32,64,1024]{2,1,0:T(8,128)} %get-tuple-element.501.raw, f32[32,144,1024]{2,1,0:T(8,128)} %get-tuple-element.497.refs_4_.freq.raw, s32[8,256,1]{2,1,0:T(8,128)} %reshape.471.code, ...), custom_call_target="tpu_custom_call", output_to_operand_aliasing={{}: (4, {})} | custom-call | flops 1073741824 | bytes 40000000 | tf_op jit(solution)/shard_map/cond/branch_1_fun/hot_out/pallas_call | solution.py:701
  581.7 11.2 %hot_out.4.into = f32[4,2048,1024]{2,1,0:T(8,128)} custom-call(s32[8]{0:T(128)} %convert_element_type.377.any_freq, f32[32,64,1024]{2,1,0:T(8,128)} %get-tuple-element.500.raw, f32[32,144,1024]{2,1,0:T(8,128)} %get-tuple-element.497.refs_4_.freq.raw, s32[8,256,1]{2,1,0:T(8,128)} %reshape.471.code, ...), custom_call_target="tpu_custom_call", output_to_operand_aliasing={{}: (4, {})} | custom-call | flops 1073741824 | bytes 40000000 | tf_op jit(solution)/shard_map/cond/branch_1_fun/hot_out/pallas_call | solution.py:701
  592.8 21.2 %hot_out.5 = f32[4,2048,1024]{2,1,0:T(8,128)} custom-call(s32[8]{0:T(128)} %convert_element_type.377.any_freq, f32[32,144,1024]{2,1,0:T(8,128)} %get-tuple-element.497.refs_4_.freq.raw, f32[32,144,1024]{2,1,0:T(8,128)} %get-tuple-element.497.refs_4_.freq.raw, s32[8,256,1]{2,1,0:T(8,128)} %reshape.471.code, ...), custom_call_target="tpu_custom_call", output_to_operand_aliasing={{}: (4, {})} | custom-call | flops 4831838208 | bytes 80000000 | tf_op jit(solution)/shard_map/cond/branch_1_fun/hot_out/pallas_call | solution.py:701
  614.0 5.3 fusion.6
  619.3 5.7 put_rows.1
  (111 shorter events, 17.3 us)
Async XLA Ops:
  7.2 3.1 copy-start.12
  7.2 11.2 %copy-start.21 = (s32[2048]{0:T(1024)S(1)}, s32[2048]{0:T(1024)}, u32[]{:S(2)}) copy-start(s32[2048]{0:T(1024)} %param.19) | copy-start | bytes 24580
  11.0 15.5 %all-to-all-start.5 = ((s32[32,1,1024]{2,1,0:T(1,128)}), s32[32,1,1024]{2,1,0:T(1,128)S(1)}, u32[]{:S(2)}, u32[]{:S(2)}) async-start(s32[32,1,1024]{2,1,0:T(1,128)} %broadcast_in_dim.279), calls=%async_computation.5 | async-start | bytes 262144 | tf_op jit(solution)/shard_map/all_to_all | solution.py:38
  19.8 22.1 %copy-start.22 = (f32[17]{0:T(128)S(1)}, f32[17]{0:T(128)}, u32[]{:S(2)}) copy-start(f32[17]{0:T(128)} %constant.380.clone) | copy-start | bytes 208
  43.6 3.5 copy-start.7
  52.7 13.2 %all-to-all-start.6 = ((bf16[32,4,1024]{2,1,0:T(4,128)(2,1)}), bf16[32,4,1024]{2,1,0:T(4,128)(2,1)S(1)}, u32[]{:S(2)}, u32[]{:S(2)}) async-start(bf16[32,4,1024]{2,1,0:T(4,128)(2,1)} %broadcast_in_dim.294), calls=%async_computation.6 | async-start | bytes 524288 | tf_op jit(solution)/shard_map/all_to_all | solution.py:38
  55.4 15.4 %copy-start.17 = (s32[1024]{0:T(1024)}, s32[1024]{0:T(1024)S(1)}, u32[]{:S(2)}) copy-start(s32[1024]{0:T(1024)S(1)} %fusion.284) | copy-start | bytes 12292
  57.4 3.2 copy-start
  66.5 11.5 %all-to-all-start.7 = ((s32[32,1,32]{2,1,0:T(1,128)}), s32[32,1,32]{2,1,0:T(1,128)S(1)}, u32[]{:S(2)}, u32[]{:S(2)}) async-start(s32[32,1,32]{2,1,0:T(1,128)} %all_to_all.45), calls=%async_computation.7 | async-start | bytes 32768 | tf_op jit(solution)/shard_map/all_to_all | solution.py:38
  70.8 8.5 %copy-start.2 = (bf16[2048,200]{1,0:T(8,128)(2,1)S(1)}, bf16[2048,200]{1,0:T(8,128)(2,1)}, u32[]{:S(2)}) copy-start(bf16[2048,200]{1,0:T(8,128)(2,1)} %fusion.207) | copy-start | bytes 2457604
  70.8 8.5 %copy-start.3 = (bf16[2048,256]{0,1:T(8,128)(2,1)S(1)}, bf16[2048,256]{0,1:T(8,128)(2,1)}, u32[]{:S(2)}) copy-start(bf16[2048,256]{0,1:T(8,128)(2,1)} %fusion.204) | copy-start | bytes 3145732
  89.6 15.7 %copy-start.6 = (bf16[176,1024]{1,0:T(8,128)(2,1)}, bf16[176,1024]{1,0:T(8,128)(2,1)S(1)}, u32[]{:S(2)}) copy-start(bf16[176,1024]{1,0:T(8,128)(2,1)S(1)} %fusion.225) | copy-start | bytes 1081348
  94.6 10.7 %copy-start.5 = (bf16[176,1024]{1,0:T(8,128)(2,1)}, bf16[176,1024]{1,0:T(8,128)(2,1)S(1)}, u32[]{:S(2)}) copy-start(bf16[176,1024]{1,0:T(8,128)(2,1)S(1)} %fusion.222) | copy-start | bytes 1081348
  94.6 53.1 %all-to-all-start.8 = ((bf16[32,32,1024]{2,1,0:T(8,128)(2,1)}), bf16[32,32,1024]{2,1,0:T(8,128)(2,1)}, u32[]{:S(2)}, u32[]{:S(2)}) async-start(bf16[32,32,1024]{2,1,0:T(8,128)(2,1)} %bitcast.16), calls=%async_computation.8 | async-start | bytes 4194304 | tf_op jit(solution)/shard_map/all_to_all | solution.py:38
  103.9 13.9 %copy-start.4 = (bf16[176,1024]{1,0:T(8,128)(2,1)}, bf16[176,1024]{1,0:T(8,128)(2,1)S(1)}, u32[]{:S(2)}) copy-start(bf16[176,1024]{1,0:T(8,128)(2,1)S(1)} %fusion.219) | copy-start | bytes 1081348
  109.7 8.1 %copy-start.19 = (s32[256]{0:T(256)}, s32[256]{0:T(256)S(1)}, u32[]{:S(2)}) copy-start(s32[256]{0:T(256)S(1)} %select_reduce_fusion.4.row_of) | copy-start | bytes 3076
  125.7 3.5 slice-start.4
  125.7 3.5 slice-start.5
  125.9 3.6 slice-start.2
  125.9 3.6 slice-start.3
  126.1 3.7 slice-start
  126.1 3.6 slice-start.1
  157.1 132.5 %all-to-all-start = ((bf16[32,32,1024]{2,1,0:T(8,128)(2,1)}), bf16[32,32,1024]{2,1,0:T(8,128)(2,1)}, u32[]{:S(2)}, u32[]{:S(2)}) async-start(bf16[32,32,1024]{2,1,0:T(8,128)(2,1)} %bitcast.308), calls=%async_computation | async-start | bytes 4194304 | tf_op jit(solution)/shard_map/cond/branch_1_fun/all_to_all | solution.py:38
  289.6 112.6 %all-to-all-start.1 = ((bf16[32,32,1024]{2,1,0:T(8,128)(2,1)}), bf16[32,32,1024]{2,1,0:T(8,128)(2,1)}, u32[]{:S(2)}, u32[]{:S(2)}) async-start(bf16[32,32,1024]{2,1,0:T(8,128)(2,1)} %bitcast.8), calls=%async_computation.1 | async-start | bytes 4194304 | tf_op jit(solution)/shard_map/cond/branch_1_fun/all_to_all | solution.py:38
  592.8 21.2 %copy-start.18 = (s32[1024]{0:T(1024)S(1)}, s32[1024]{0:T(1024)}, u32[]{:S(2)}) copy-start(s32[1024]{0:T(1024)} %get-tuple-element.468) | copy-start | bytes 12292 | tf_op jit(solution)/shard_map/cond
  614.0 5.3 copy-start.20

commit v3 on v2

--- a/solution.py
+++ b/solution.py
@@ -9,14 +9,14 @@
 
 
 NORM_EPS = 1e-6
-FREQ_HOT = 112
-FREQ_COLD = 16
+FREQ_HOT = 124
+FREQ_COLD = 4
 FREQ = FREQ_HOT + FREQ_COLD
 COLD_MAX = 256
 LO = 256
 HI_BITS = 8
 RUN = 4
-LEVELS = tuple(16 * 2 ** (i / 4) for i in range(17))
+LEVELS = tuple(12 * 2 ** (i / 6) for i in range(27))
 GELU_A = 0.7978845608028654
 GELU_B = GELU_A * 0.044715
 VMEM = 66_000_000
@@ -277,135 +277,130 @@
     return pl.CostEstimate(flops=2 * products, bytes_accessed=layers * 40_000_000, transcendentals=0)
 
 
-def backward_kernel(n_f, r_in, cls_t, es, xs, hs, ss, wu, wd, wg, wp, *refs):
-    talks = len(refs) > 5
-    if talks:
-        prev, sums, r, out, tot, c_now, acc, three, sems, sems_f, *bufs = refs
-        at = Place()
-        gather = Spread(at, prev.at[pl.ds(HOT_AT, COLD_AT - HOT_AT)], lambda d: out.at[d], sems)
-        fold = Fold(at, prev.at[pl.ds(0, FREQ)], bufs, sems_f)
-    else:
-        sums, r, c_now, acc, three = refs
+def spec(shape, *index, **more):
+    index = index or (0,) * len(shape)
+    return pl.BlockSpec(shape, lambda *_: index, **more)
+
+
+ANY = pl.BlockSpec(memory_space=pl.ANY)
+
+
+def out_of(shape, dtype=F32):
+    return jax.ShapeDtypeStruct(shape, dtype)
+
+
+def backward_kernel(n_f, r_in, ss, wp, es, wg, xs, cls_t, hs, wu, wd, *refs):
+    prev, refs = (refs[0], refs[1:]) if len(refs) > 20 else (None, refs)
+    sums, r, tot, out, refs = (*refs[:3], refs[3], refs[4:]) if prev is not None else (*refs[:3], None, refs[3:])
+    c_now, acc, three, s_now, p_now, e_now, g_now, x_now, loads, sems, sems_f, *bufs = refs
     f = pl.program_id(0)
-    n_tok = c_now.shape[0]
+    n_tok = len(c_now)
+    at = Place()
+    gather = None if prev is None else Spread(at, prev.at[pl.ds(HOT_AT, COLD_AT - HOT_AT)], lambda d: out.at[d], sems)
+    fold = Fold(at, sums.at[pl.ds(0, FREQ)], bufs, sems_f)
+    rounded = r_in.dtype == BF
+    srcs = (wp, p_now), (r_in, c_now if rounded else r), (ss, s_now), (es, e_now), (wg, g_now), (xs, x_now)
+    copies = [pltpu.make_async_copy(src, dst, loads.at[i]) for i, (src, dst) in enumerate(srcs)]
+
+    def talk(*steps):
+        if gather is not None:
+            for name, k in steps:
+                getattr(gather, name)(k)
 
     @pl.when(f == 0)
     def _():
-        if talks:
-            at.meet()
-            gather.begin()
-            fold.begin()
-        r[...] = r_in[...].astype(F32)
+        for c in copies:
+            c.start()
+        at.meet()
+        talk(("begin", 0))
+        for c in copies[:-1]:
+            c.wait()
         for m in chunks(n_tok, ROWS_B):
-            c = r[m, :].astype(BF)
-            c_now[m, :] = c
-            a = dot_nt(c, wp[...])
-            s = ss[m, :].astype(F32)
+            if rounded:
+                r[m, :] = c_now[m, :].astype(F32)
+            else:
+                c_now[m, :] = r[m, :].astype(BF)
+            a = dot_nt(c_now[m, :], p_now[...])
+            s = s_now[m, :].astype(F32)
             rows = gelu(s).astype(BF).astype(F32) * a
-            for i, part in enumerate(split3(rows)):
-                three[i, m, :] = part
-            ds = (gelu_slope(s) * (a * es[m, :].astype(F32))).astype(BF)
-            acc[m, :] = dot_nt(ds, wg[...])
+            for j, part in enumerate(split3(rows)):
+                three[j, m, :] = part
+            ds = (gelu_slope(s) * (a * e_now[m, :].astype(F32))).astype(BF)
+            acc[m, :] = dot_nt(ds, g_now[...])
+        talk(("onward", 0))
         class_sums(cls_t, three, sums)
-        if talks:
-            gather.column(1)
-            gather.onward(0)
-            fold.step(0)
-
-    if talks:
-        @pl.when(f == 1)
-        def _():
-            gather.column(2)
-            gather.onward(1)
-            fold.step(1)
-
-        @pl.when(f == 2)
-        def _():
-            gather.column(3)
-            gather.onward(2)
-            fold.step(2)
-
-        @pl.when(f == 3)
-        def _():
-            gather.across(0)
-            gather.onward(3)
-            tot[...] = fold.total()
-
-    for m in chunks(n_tok, ROWS_B):
+        fold.begin()
+        talk(("column", 1))
+
+    plan = {(0, 1): (("onward", 1), ("column", 2)), (1, 0): (("column", 3),), (1, 1): (("onward", 2),),
+            (2, 0): (("across", 0), ("onward", 3)), (2, 1): (("across", 1),), (3, 0): (("across", 2),)}
+    for i, m in enumerate(chunks(n_tok, ROWS_B)):
         d_act = dot_nt(c_now[m, :], wd[...])
         dh = (gelu_slope(hs[m, :].astype(F32)) * d_act).astype(BF)
         acc[m, :] += dot_nt(dh, wu[...])
+        for k in range(n_f):
+            @pl.when(f == k)
+            def _(k=k, i=i):
+                if i and k < 3:
+                    fold.step(k)
+                talk(*plan.get((k, i), ()))
 
     @pl.when(f == n_f - 1)
     def _():
-        if talks:
-            gather.across(1)
-            gather.across(2)
+        copies[-1].wait()
         for m in chunks(n_tok, ROWS_A):
-            x = xs[m, :].astype(F32)
+            x = x_now[m, :].astype(F32)
             k = lax.rsqrt(jnp.mean(x * x, axis=-1, keepdims=True) + NORM_EPS)
             du = acc[m, :]
             inner = jnp.mean(du * x, axis=-1, keepdims=True)
             r[m, :] = r[m, :] + k * du - x * (k * k * k) * inner
-        if talks:
-            gather.across(3)
-            gather.end()
-
-
-def backward(layer, r_in, cls_t, es, xs, hs, ss, w_up, w_down, w_gate, w_proj, prev=None, n_dev=0):
+        tot[...] = fold.total()
+        talk(("across", 3), ("end", 0))
+
+
+def backward(layer, r_in, cls_t, es, xs, hs, ss, w_up, w_down, w_gate, w_proj, n_dev, prev=None):
     n_tok, dim = r_in.shape
     ff = w_up.shape[2]
     emb = w_gate.shape[2]
     n_c = COLD_AT + COLD_MAX
     n_f = 4
     tile = ff // n_f
-    talks = prev is not None
-    once = dict(pipeline_mode=ONCE)
-
-    def whole(n, m):
-        return spec((None, n, m), layer, 0, 0, **once)
+    more = prev is not None
 
     def cols(n):
         return pl.BlockSpec((None, n, tile), lambda t: (layer, 0, t))
 
+    def kernel(r_in, ss, wp, es, wg, xs, *refs):
+        backward_kernel(n_f, r_in, *[v.at[layer] for v in (ss, wp, es, wg, xs)], *refs)
+
     return pl.pallas_call(
-        functools.partial(backward_kernel, n_f),
+        kernel,
         grid=(n_f,),
-        in_specs=[spec((n_tok, dim), **once), spec((1, n_tok), **once), whole(n_tok, emb), whole(n_tok, dim), cols(n_tok), whole(n_tok, emb),
-                  cols(dim), pl.BlockSpec((None, tile, dim), lambda t: (layer, t, 0)), whole(dim, emb), whole(emb, dim)]
-        + [spec((n_c, emb), **once)] * talks,
-        out_specs=[spec((n_c, emb)), spec((n_tok, dim))] + [ANY, spec((16, emb))] * talks,
-        out_shape=[out_of((n_c, emb)), out_of((n_tok, dim))] + [out_of((n_dev, COLD_AT - HOT_AT, emb)), out_of((16, emb))] * talks,
+        in_specs=[ANY] * 6 + [spec((1, n_tok)), cols(n_tok), cols(dim), pl.BlockSpec((None, tile, dim), lambda t: (layer, t, 0))]
+        + [spec((n_c, emb), pipeline_mode=ONCE)] * more,
+        out_specs=[spec((n_c, emb)), spec((n_tok, dim)), spec((16, emb))] + [ANY] * more,
+        out_shape=[out_of((n_c, emb)), out_of((n_tok, dim)), out_of((16, emb))] + [out_of((n_dev, COLD_AT - HOT_AT, emb))] * more,
         scratch_shapes=[pltpu.VMEM((n_tok, dim), BF), pltpu.VMEM((n_tok, dim), F32), pltpu.VMEM((3, n_tok, emb), BF)]
-        + ([SPREAD_SEMS, FOLD_SEMS] + fold_bufs(emb)) * talks,
-        compiler_params=params("arbitrary", **(dict(collective_id=layer - 1, has_side_effects=True) if talks else {})),
+        + [pltpu.VMEM(v, BF) for v in ((n_tok, emb), (emb, dim), (n_tok, emb), (dim, emb), (n_tok, dim))]
+        + [pltpu.SemaphoreType.DMA((6,)), SPREAD_SEMS, FOLD_SEMS] + fold_bufs(emb),
+        compiler_params=params("arbitrary", collective_id=layer, has_side_effects=True),
         cost_estimate=cost(n_tok * dim * (2 * ff + 2 * emb + 3 * n_c), 1),
         name="backward",
-    )(r_in, cls_t, es, xs, hs, ss, w_up, w_down, w_gate, w_proj, *([prev] if talks else []))
-
-
-def spec(shape, *index, **more):
-    index = index or (0,) * len(shape)
-    return pl.BlockSpec(shape, lambda *_: index, **more)
-
-
-ANY = pl.BlockSpec(memory_space=pl.ANY)
-
-
-def out_of(shape, dtype=F32):
-    return jax.ShapeDtypeStruct(shape, dtype)
+    )(r_in, ss, w_proj, es, w_gate, xs, cls_t, hs, w_up, w_down, *([prev] if more else []))
 
 
 def count_kernel(ids, out):
     n_tok = ids.shape[1]
     out[...] = jnp.zeros(out.shape, F32)
 
+    def hits(v, n):
+        same = v.astype(F32).astype(BF) == iota((n, n_tok), 0).astype(F32).astype(BF)
+        return jnp.where(same, jnp.ones((), BF), jnp.zeros((), BF))
+
     @pl.loop(0, len(ids))
     def _(i):
-        row = ids[pl.ds(i, 1), :]
-        hi = ((row >> HI_BITS) == iota((len(out), n_tok), 0)).astype(BF)
-        lo = ((row & (LO - 1)) == iota((LO, n_tok), 0)).astype(BF)
-        out[...] += dot_nt(hi, lo)
+        ids_i = ids[pl.ds(i, 1), :]
+        out[...] += dot_nt(hits(ids_i >> HI_BITS, len(out)), hits(ids_i & (LO - 1), LO))
 
 
 def count_ids(ids, n_hi):
@@ -482,7 +477,7 @@
     def got(self, kind, k, block):
         remote(block, block, self.pair(kind, k), self.at.to_x).wait_recv()
 
-    def begin(self):
+    def begin(self, _=None):
         own = self.slot(self.col[0])
         pltpu.make_async_copy(self.mine, own, self.sems.at[0, OWN, 0]).start()
         for k, other in enumerate(self.at.others):
@@ -511,7 +506,7 @@
             self.got(kind, k, block.at[half])
         self.send(CD, k, block, block, self.at.to_core)
 
-    def end(self):
+    def end(self, _=None):
         for k in STOPS:
             for kind, far in zip((C, CX, CY, CD), self.far):
                 self.got(kind, k, self.slot(far[k]))
@@ -583,12 +578,12 @@
 
 
 def last_kernel(r_in, ss, wp, cls_t, prev, *refs):
-    early, (sums, out, r, s, w, three, pay, copies, sems_1, sems_0, sems_f1, sems_f0), bufs = refs[:2], refs[2:14], refs[14:]
+    early, (sums, out, r, s, w, three, pay, loads, sems_1, sems_0, sems_f, *bufs) = refs[:3], refs[3:]
     n_hot = COLD_AT - HOT_AT
     n = pay.shape[1]
-    loads = [pltpu.make_async_copy(src, dst, copies.at[i]) for i, (src, dst) in enumerate(((r_in, r), (ss.at[0], s), (wp.at[0], w)))]
-    for load in loads:
-        load.start()
+    copies = [pltpu.make_async_copy(src, dst, loads.at[i]) for i, (src, dst) in enumerate(((r_in, r), (ss.at[0], s), (wp.at[0], w)))]
+    for c in copies:
+        c.start()
     at = Place()
     at.meet()
 
@@ -600,46 +595,35 @@
                 for j, t in enumerate(totals):
                     pay[i, pl.ds(n_hot + RUN * j, RUN), :] = t[z * RUN:(z + 1) * RUN, :]
 
-    fold_1 = Fold(at, prev.at[pl.ds(0, FREQ)], bufs[:6], sems_f1)
-    fold_0 = Fold(at, sums.at[pl.ds(0, FREQ)], bufs[6:], sems_f0)
-    all_1 = Spread(at, pay.at[0], lambda d: out.at[d, pl.ds(0, n)], sems_1)
-    all_0 = Spread(at, pay.at[1], lambda d: out.at[d, pl.ds(n, n)], sems_0)
-    fold_1.begin()
-    fill(0, prev[pl.ds(HOT_AT, n_hot), :], [t[...] for t in early])
+    fold = Fold(at, sums.at[pl.ds(0, FREQ)], bufs, sems_f)
+    all_1, all_0 = [Spread(at, pay.at[i], lambda d, i=i: out.at[d, pl.ds(STRIDE * i, n)], sems) for i, sems in enumerate((sems_1, sems_0))]
+    fill(0, prev[pl.ds(HOT_AT, n_hot), :], [t[...] for t in early[:2]])
     all_1.begin()
-    for load in loads:
-        load.wait()
+    for c in copies:
+        c.wait()
     for m in chunks(len(r), ROWS_B):
         a = dot_nt(r[m, :].astype(BF), w[...])
         rows = gelu(s[m, :].astype(F32)).astype(BF).astype(F32) * a
         for i, part in enumerate(split3(rows)):
             three[i, m, :] = part
-    fold_1.step(0)
+    all_1.onward(0)
     class_sums(cls_t, three, sums)
-    fold_0.begin()
+    fold.begin()
     all_1.column(1)
-    all_1.onward(0)
-    fold_1.step(1)
-    fold_0.step(0)
-    all_1.column(2)
-    all_1.onward(1)
-    fold_1.step(2)
-    fold_0.step(1)
-    all_1.column(3)
-    all_1.onward(2)
-    total_1 = fold_1.total()
-    fold_0.step(2)
+    for k in REST:
+        fold.step(k - 1)
+        all_1.onward(k)
+        if k < REST[-1]:
+            all_1.column(k + 1)
     all_1.across(0)
-    all_1.onward(3)
-    fill(1, sums[pl.ds(HOT_AT, n_hot), :], [total_1, fold_0.total()])
+    fill(1, sums[pl.ds(HOT_AT, n_hot), :], [early[2][...], fold.total()])
     all_0.begin()
     for k in REST:
         all_1.across(k)
-    for k in REST:
+        all_0.onward(k - 1)
         all_0.column(k)
-        all_0.onward(k - 1)
     all_0.across(0)
-    all_0.onward(3)
+    all_0.onward(REST[-1])
     for k in REST:
         all_0.across(k)
     all_1.end()
@@ -652,21 +636,24 @@
     sums[...] = hi + (mid + lo)
 
 
-def last(r_in, ss, w_proj, cls_t, prev, tot_3, tot_2, n_dev):
+STRIDE = 80
+
+
+def last(r_in, ss, w_proj, cls_t, prev, tots, n_dev):
     n_tok, dim = r_in.shape
     n_c, emb = prev.shape
     n = COLD_AT - HOT_AT + 2 * RUN
     vmem = pl.BlockSpec(memory_space=pltpu.VMEM)
     return pl.pallas_call(
         last_kernel,
-        in_specs=[ANY, ANY, ANY] + [vmem] * 4, out_specs=[vmem, ANY],
-        out_shape=[out_of((n_c, emb)), out_of((n_dev, 2 * n, emb))],
+        in_specs=[ANY] * 3 + [vmem] * (2 + len(tots)), out_specs=[vmem, ANY],
+        out_shape=[out_of((n_c, emb)), out_of((n_dev, 2 * STRIDE, emb))],
         scratch_shapes=[pltpu.VMEM((n_tok, dim), F32), pltpu.VMEM((n_tok, emb), BF), pltpu.VMEM((emb, dim), BF),
                         pltpu.VMEM((3, n_tok, emb), BF), pltpu.VMEM((2, n, emb), F32), pltpu.SemaphoreType.DMA((3,)),
-                        SPREAD_SEMS, SPREAD_SEMS, FOLD_SEMS, FOLD_SEMS] + fold_bufs(emb) * 2,
-        compiler_params=params(collective_id=2, has_side_effects=True),
+                        SPREAD_SEMS, SPREAD_SEMS, FOLD_SEMS] + fold_bufs(emb),
+        compiler_params=params(collective_id=0, has_side_effects=True),
         cost_estimate=cost(n_tok * dim * 4 * emb, 1), name="last",
-    )(r_in, ss, w_proj, cls_t, prev, tot_3, tot_2)
+    )(r_in, ss, w_proj, cls_t, prev, *tots)
 
 
 ORDER = [(b & 3) * 8 + (b >> 2 & 1) * 4 + (b >> 3 & 1) * 2 + (b >> 4) for b in range(FREQ // RUN)]
@@ -692,9 +679,9 @@
         out[0] += dot32(sel, parts[0]) + (dot32(sel, parts[1]) + dot32(sel, parts[2]))
 
 
-def hot_out(first, n_l, gathered, stride, freq_from, freq_at, skip, code, into):
+def hot_out(first, n_l, gathered, freq_from, freq_at, skip, code, into):
     n_dev, _, emb = gathered.shape
-    n_r = 2 * RUN
+    n_r = 4 * RUN
     width = n_r * n_dev
     blocks = into.shape[1] // width
     code = code.reshape(blocks, width, 1)
@@ -703,8 +690,8 @@
         grid_spec=pltpu.PrefetchScalarGridSpec(
             num_scalar_prefetch=1, grid=(n_l, blocks),
             in_specs=[
-                pl.BlockSpec((n_dev, n_r, emb), lambda i, b, _: (0, i * stride + b, 0)),
-                spec((n_dev, n_r, emb), 0, freq_at, 0, pipeline_mode=ONCE),
+                pl.BlockSpec((n_dev, n_r, emb), lambda i, b, _: (0, i * (STRIDE // n_r) + b, 0)),
+                spec((n_dev, 2 * RUN, emb), 0, freq_at, 0, pipeline_mode=ONCE),
                 pl.BlockSpec((1, width, 1), lambda i, b, _: (b, 0, 0)),
                 ANY,
             ],
@@ -737,14 +724,13 @@
 
     @pl.when(cold_row >= 0)
     def _():
-        n = freq.shape[1] // 2
         for j in range(2):
-            c = pltpu.make_async_copy(freq.at[cold_no // RUN * 8 + 7, pl.ds(j * n + n - 8, 8)], got.at[j], sem)
+            c = pltpu.make_async_copy(freq.at[len(freq) - 1, pl.ds(j * STRIDE + COLD_AT - HOT_AT, 8)], got.at[j], sem)
             c.start()
             c.wait()
         for l in range(n_l):
             i = n_l - 1 - l
-            stage[COLD_MAX, pl.ds(l, 1), :] = got[i // 2, pl.ds(i % 2 * RUN + cold_no % RUN, 1), :]
+            stage[COLD_MAX, pl.ds(l, 1), :] = got[i // 2, pl.ds(i % 2 * RUN + cold_no, 1), :]
         put(COLD_MAX, cold_row).start()
         put(0, 0).wait()
 
@@ -900,20 +886,20 @@
             cls_row = cls.reshape(1, n_loc)
             xs, hs, ss, es, x_last, zeros = forward(x_moved, cls.reshape(n_loc, 1), table, w_up, w_down, w_gate, w_proj, rows_dev)
             x_back = exchange(x_last)
-            kept = (cls_row, es, xs, hs, ss, w_up, w_down, w_gate, w_proj)
-            sums_3, r = backward(3, d_moved, *kept)
-            sums_2, r, all_3, tot_3 = backward(2, r, *kept, sums_3, n_dev)
+            kept = (cls_row, es, xs, hs, ss, w_up, w_down, w_gate, w_proj, n_dev)
+            sums_3, r, tot_3 = backward(3, d_moved, *kept)
+            sums_2, r, tot_2, all_3 = backward(2, r, *kept, sums_3)
             r, x_back = lax.optimization_barrier((r, x_back))
-            sums_1, r, all_2, tot_2 = backward(1, r, *kept, sums_2, n_dev)
-            sums_0, all_b = last(r, ss, w_proj, cls_row, sums_1, tot_3, tot_2, n_dev)
+            sums_1, r, tot_1, all_2 = backward(1, r, *kept, sums_2)
+            sums_0, all_b = last(r, ss, w_proj, cls_row, sums_1, (tot_3, tot_2, tot_1), n_dev)
             x_out = dot32((col(slot) == iota((n_loc, n_loc), 1)).astype(BF), x_back).astype(BF)
             numbers = jnp.stack([n_used, my_row, jnp.sum(my_cold * jnp.arange(FREQ_COLD, dtype=I32))])
             d_table = put_rows(numbers, row_of, [sums_0, sums_1, sums_2, sums_3], all_b, zeros)
-            at_freq = hot_dev // (2 * RUN)
+            freq_at = hot_dev // (2 * RUN)
             into = empty((layers, n_hot, emb_dim))
-            into = hot_out(3, 1, all_3, 0, all_b, at_freq, 0, code, into)
-            into = hot_out(2, 1, all_2, 0, all_b, at_freq, 1, code, into)
-            into = hot_out(1, 2, all_b, at_freq + 1, all_b, 2 * at_freq + 1, 0, code, into)
+            into = hot_out(3, 1, all_3, all_b, freq_at, 0, code, into)
+            into = hot_out(2, 1, all_2, all_b, freq_at, 1, code, into)
+            into = hot_out(1, 2, all_b, all_b, freq_at + STRIDE // (2 * RUN), 0, code, into)
             return x_out, d_table.transpose(1, 0, 2), into
 
         def slow(*_):

time: 644 us -> 647 us (level)
  the two profiles are of different devices: /device:TPU:0 before, /device:TPU:21 now
where the time goes in v3:
time: 647 us; the launch traced here: 637 us
  Pallas kernels  472 us (73%)
  matrix products  44.2 us (7%)
  starting transfers between devices  37.2 us (6%)
  other arithmetic  23.9 us (4%)
  local copies, waits for them, and re-layouts  21.1 us (3%)
  between operations  18.9 us (3%)
  waiting for transfers between devices  10.4 us (2%)
  loops' own time  9.81 us (2%)
    pallas_call x3, Pallas kernels, backward(): pl.pallas_call(kernel, grid=(n_f,), in_specs=[ANY] * 6 + [spec((1, n_tok)...  180 us
    pallas_call x1, Pallas kernels, forward(): pl.pallas_call(functools.partial(forward_kernel, n_l, n_f), grid=(n_l, n_...  123 us
    pallas_call x1, Pallas kernels, last(): pl.pallas_call(last_kernel, in_specs=[ANY] * 3 + [vmem] * (2 + len(tots))...  105 us
    dot_general x19, matrix products, dot32(): return jnp.dot(a, b, preferred_element_type=F32)  44.2 us
    pallas_call x3, Pallas kernels, hot_out(): pl.pallas_call(functools.partial(hot_kernel, skip), grid_spec=pltpu.Prefe...  37.8 us
    all_to_all x6, starting transfers between devices, swap(): return lax.all_to_all(v, 'emb', 0, 0, tiled=True)  37.2 us
  transfers between devices with their start and end apart: 6, of which 2 were waited for; matrix products, arithmetic and copies ran while one was open for 8% of the time, Pallas kernels for 39%

profile of v3, /device:TPU:21, one launch (start us, length us, event | category | flops | bytes accessed | tf_op | source)
XLA Modules:
  0.0 637.1 jit_solution(17360095935905623930)
XLA Ops:
  7.2 3.1 copy.233
  11.0 6.2 all-to-all-start.5
  17.3 1.3 fusion.207
  18.6 1.2 fusion.204
  20.8 1.7 all-to-all-done.5
  23.2 12.6 %count_ids.1 = f32[200,256]{1,0:T(8,128)} custom-call(s32[32,1024]{1,0:T(8,128)} %bitcast.312), custom_call_target="tpu_custom_call" | custom-call | tf_op jit(solution)/shard_map/count_ids/pallas_call | solution.py:407
  35.8 1.8 broadcast_select_fusion.2
  37.6 1.4 convert_reduce_fusion
  39.7 1.4 convert_reduce_fusion.2
  48.5 5.5 all-to-all-start.6
  55.3 0.9 fusion.215
  56.2 1.2 fusion.214
  59.4 3.7 fusion.210
  63.7 5.8 all-to-all-start.7
  69.6 5.4 fusion.211
  77.7 4.9 fusion.228
  82.6 5.1 fusion.225
  87.7 5.1 fusion.222
  92.8 5.9 all-to-all-start.8
  98.7 4.9 fusion.219
  105.2 1.7 select_reduce_fusion.1
  108.5 1.1 select_reduce_fusion.3.row_of
  109.6 7.0 %pack_rows.1 = bf16[256,4,1024]{2,1,0:T(4,128)(2,1)} custom-call(s32[256]{0:T(256)S(1)} %select_reduce_fusion.3.row_of, bf16[1572,4,1024]{2,1,0:T(4,128)(2,1)} %bitcast.303), custom_call_target="tpu_custom_call" | custom-call | tf_op jit(solution)/shard_map/pack_rows/pallas_call | solution.py:420
  116.7 7.9 %fusion.328 = (bf16[256,1,1024]{2,1,0:T(2,128)(2,1)S(1)}, bf16[256,1,1024]{2,1,0:T(2,128)(2,1)S(1)}, bf16[256,1,1024]{2,1,0:T(2,128)(2,1)S(1)}, bf16[256,1,1024]{2,1,0:T(2,128)(2,1)S(1)}) fusion(bf16[256,4,1024]{2,1,0:T(4,128)(2,1)} %pack_rows.1), kind=kLoop, calls=%fused_computation.455 | loop fusion | bytes 4194304 | tf_op jit(solution)/shard_map/slice | solution.py:823
  126.6 1.0 convolution_convert_fusion.2
  127.6 1.0 maximum_bitcast_fusion.3
  128.6 1.0 convolution_convert_fusion.3
  129.7 1.0 maximum_bitcast_fusion.2
  130.6 1.0 convolution_convert_fusion.4
  131.8 1.0 convolution_convert_fusion.5
  132.9 2.1 pad_maximum_fusion
  135.0 8.7 %all-to-all-done.8 = bf16[32,32,1024]{2,1,0:T(8,128)(2,1)} async-done(((bf16[32,32,1024]{2,1,0:T(8,128)(2,1)}), bf16[32,32,1024]{2,1,0:T(8,128)(2,1)}, u32[]{:S(2)}, u32[]{:S(2)}) %all-to-all-start.8) | async-done | bytes 2097184 | tf_op jit(solution)/shard_map/all_to_all | solution.py:38
  143.7 486.3 %conditional.1 = (bf16[1024,1024]{1,0:T(8,128)(2,1)}, f32[4,1572,1024]{2,0,1:T(4,128)}, f32[4,2048,1024]{2,1,0:T(8,128)}) conditional(s32[]{:T(128)} %convert_element_type.451, (s32[1024]{0:T(1024)S(1)}, s32[2048]{0:T(1024)S(1)}, s32[]{:T(128)}, bf16[4,1024,4096]{2,1,0:T(8,128)(2,1)}, bf16[4,4096,1024]{2,1,0:T(8,128)(2,1)}, ...), branch_computations={%region_29.45_spmd, %region_45.48_spmd} | conditional | flops 180793376768 | bytes 561294080 | solution.py:908
  153.2 7.9 %all-to-all-start = ((bf16[32,32,1024]{2,1,0:T(8,128)(2,1)}), bf16[32,32,1024]{2,1,0:T(8,128)(2,1)}, u32[]{:S(2)}, u32[]{:S(2)}) async-start(bf16[32,32,1024]{2,1,0:T(8,128)(2,1)} %bitcast.308), calls=%async_computation | async-start | bytes 4194304 | tf_op jit(solution)/shard_map/cond/branch_1_fun/all_to_all | solution.py:38
  161.1 1.0 copy.131.cls
  162.2 122.9 %forward.1 = (bf16[4,1024,1024]{2,1,0:T(8,128)(2,1)}, bf16[4,1024,4096]{2,1,0:T(8,128)(2,1)}, bf16[4,1024,1024]{2,1,0:T(8,128)(2,1)}, bf16[4,1024,1024]{2,1,0:T(...) custom-call(bf16[1024,1024]{1,0:T(8,128)(2,1)} %get-tuple-element.470.x0, s32[1024,1]{1,0:T(8,128)} %copy.131.cls, ...), custom_call_target="tpu_custom_call" | custom-call | flops 89657442304 | bytes 160000000 | tf_op jit(solution)/shard_map/cond/branch_1_fun/forward/pallas_call | solution.py:243
  285.1 1.8 reshape.471.code
  288.3 1.2 pad_add_fusion.numbers
  289.5 5.9 all-to-all-start.1
  295.4 54.3 %backward.3 = (f32[448,1024]{1,0:T(8,128)}, f32[1024,1024]{1,0:T(8,128)}, f32[16,1024]{1,0:T(8,128)}) custom-call(bf16[1024,1024]{1,0:T(8,128)(2,1)} %bitcast.5.r_in, bf16[4,1024,1024]{2,1,0:T(8,128)(2,1)} %get-tuple-element.477.ss, bf16[4,1024,1024]{2,1,0:T(8,128)(2,1)} %get-tuple-element.476.wp, bf16[4,1024,1024]{2,1,0:T(8,128)(2,1)} %get-tuple-element.478.es, ...), custom_call_target="tpu_custom_call" | custom-call | flops 24293408768 | bytes 40000000 | tf_op jit(solution)/shard_map/cond/branch_1_fun/backward/pallas_call | solution.py:376
  349.6 64.3 %backward.4 = (f32[448,1024]{1,0:T(8,128)}, f32[1024,1024]{1,0:T(8,128)}, f32[16,1024]{1,0:T(8,128)}, f32[32,64,1024]{2,1,0:T(8,128)}) custom-call(f32[1024,1024]{1,0:T(8,128)} %get-tuple-element.481.r_in, bf16[4,1024,1024]{2,1,0:T(8,128)(2,1)} %get-tuple-element.477.ss, bf16[4,1024,1024]{2,1,0:T(8,128)(2,1)} %get-tuple-element.476.wp, ...), custom_call_target="tpu_custom_call" | custom-call | flops 24293408768 | bytes 40000000 | tf_op jit(solution)/shard_map/cond/branch_1_fun/backward/pallas_call | solution.py:376
  413.9 61.6 %backward.5 = (f32[448,1024]{1,0:T(8,128)}, f32[1024,1024]{1,0:T(8,128)}, f32[16,1024]{1,0:T(8,128)}, f32[32,64,1024]{2,1,0:T(8,128)}) custom-call(f32[1024,1024]{1,0:T(8,128)} %get-tuple-element.490.r_in, bf16[4,1024,1024]{2,1,0:T(8,128)(2,1)} %get-tuple-element.477.ss, bf16[4,1024,1024]{2,1,0:T(8,128)(2,1)} %get-tuple-element.476.wp, ...), custom_call_target="tpu_custom_call" | custom-call | flops 24293408768 | bytes 40000000 | tf_op jit(solution)/shard_map/cond/branch_1_fun/backward/pallas_call | solution.py:376
  475.6 105.0 %last.1 = (f32[448,1024]{1,0:T(8,128)}, f32[32,160,1024]{2,1,0:T(8,128)}) custom-call(f32[1024,1024]{1,0:T(8,128)} %get-tuple-element.492.r_in, bf16[4,1024,1024]{2,1,0:T(8,128)(2,1)} %get-tuple-element.477.ss, bf16[4,1024,1024]{2,1,0:T(8,128)(2,1)} %get-tuple-element.476.wp, s32[1,1024]{1,0:T(1,128)S(1)} %bitcast.321, ...), custom_call_target="tpu_custom_call" | custom-call | flops 8589934592 | bytes 40000000 | tf_op jit(solution)/shard_map/cond/branch_1_fun/last/pallas_call | solution.py:647
  580.5 9.9 %hot_out.3.into = f32[4,2048,1024]{2,1,0:T(8,128)} custom-call(s32[4]{0:T(128)} %convert_element_type.377.any_freq, f32[32,64,1024]{2,1,0:T(8,128)} %get-tuple-element.502.raw, f32[32,160,1024]{2,1,0:T(8,128)} %get-tuple-element.498.refs_4_.freq.raw, s32[4,512,1]{2,1,0:T(8,128)} %reshape.471.code, ...), custom_call_target="tpu_custom_call", output_to_operand_aliasing={{}: (4, {})} | custom-call | flops 1073741824 | bytes 40000000 | tf_op jit(solution)/shard_map/cond/branch_1_fun/hot_out/pallas_call | solution.py:688
  590.4 9.6 %hot_out.4.into = f32[4,2048,1024]{2,1,0:T(8,128)} custom-call(s32[4]{0:T(128)} %convert_element_type.377.any_freq, f32[32,64,1024]{2,1,0:T(8,128)} %get-tuple-element.501.raw, f32[32,160,1024]{2,1,0:T(8,128)} %get-tuple-element.498.refs_4_.freq.raw, s32[4,512,1]{2,1,0:T(8,128)} %reshape.471.code, ...), custom_call_target="tpu_custom_call", output_to_operand_aliasing={{}: (4, {})} | custom-call | flops 1073741824 | bytes 40000000 | tf_op jit(solution)/shard_map/cond/branch_1_fun/hot_out/pallas_call | solution.py:688
  600.0 18.3 %hot_out.5 = f32[4,2048,1024]{2,1,0:T(8,128)} custom-call(s32[4]{0:T(128)} %convert_element_type.377.any_freq, f32[32,160,1024]{2,1,0:T(8,128)} %get-tuple-element.498.refs_4_.freq.raw, f32[32,160,1024]{2,1,0:T(8,128)} %get-tuple-element.498.refs_4_.freq.raw, s32[4,512,1]{2,1,0:T(8,128)} %reshape.471.code, ...), custom_call_target="tpu_custom_call", output_to_operand_aliasing={{}: (4, {})} | custom-call | flops 5368709120 | bytes 80000000 | tf_op jit(solution)/shard_map/cond/branch_1_fun/hot_out/pallas_call | solution.py:688
  618.3 5.3 fusion.6
  623.6 6.1 put_rows.1
  (111 shorter events, 19.6 us)
Async XLA Ops:
  7.2 3.1 copy-start.13
  7.2 10.1 %copy-start.22 = (s32[2048]{0:T(1024)S(1)}, s32[2048]{0:T(1024)}, u32[]{:S(2)}) copy-start(s32[2048]{0:T(1024)} %param.19) | copy-start | bytes 24580
  11.0 11.5 %all-to-all-start.5 = ((s32[32,1,1024]{2,1,0:T(1,128)}), s32[32,1,1024]{2,1,0:T(1,128)S(1)}, u32[]{:S(2)}, u32[]{:S(2)}) async-start(s32[32,1,1024]{2,1,0:T(1,128)} %broadcast_in_dim.279), calls=%async_computation.5 | async-start | bytes 262144 | tf_op jit(solution)/shard_map/all_to_all | solution.py:38
  18.6 19.0 %copy-start.23 = (f32[27]{0:T(128)S(1)}, f32[27]{0:T(128)}, u32[]{:S(2)}) copy-start(f32[27]{0:T(128)} %constant.380.clone) | copy-start | bytes 328
  39.7 3.5 copy-start.8
  48.5 14.6 %all-to-all-start.6 = ((bf16[32,4,1024]{2,1,0:T(4,128)(2,1)}), bf16[32,4,1024]{2,1,0:T(4,128)(2,1)S(1)}, u32[]{:S(2)}, u32[]{:S(2)}) async-start(bf16[32,4,1024]{2,1,0:T(4,128)(2,1)} %broadcast_in_dim.294), calls=%async_computation.6 | async-start | bytes 524288 | tf_op jit(solution)/shard_map/all_to_all | solution.py:38
  54.1 15.4 %copy-start.18 = (s32[1024]{0:T(1024)}, s32[1024]{0:T(1024)S(1)}, u32[]{:S(2)}) copy-start(s32[1024]{0:T(1024)S(1)} %fusion.284) | copy-start | bytes 12292
  56.2 3.2 copy-start
  63.7 12.1 %all-to-all-start.7 = ((s32[32,1,32]{2,1,0:T(1,128)}), s32[32,1,32]{2,1,0:T(1,128)S(1)}, u32[]{:S(2)}, u32[]{:S(2)}) async-start(s32[32,1,32]{2,1,0:T(1,128)} %all_to_all.45), calls=%async_computation.7 | async-start | bytes 32768 | tf_op jit(solution)/shard_map/all_to_all | solution.py:38
  69.6 7.6 %copy-start.6 = (bf16[2048,200]{1,0:T(8,128)(2,1)S(1)}, bf16[2048,200]{1,0:T(8,128)(2,1)}, u32[]{:S(2)}) copy-start(bf16[2048,200]{1,0:T(8,128)(2,1)} %fusion.207) | copy-start | bytes 2457604
  69.6 7.6 %copy-start.7 = (bf16[2048,256]{0,1:T(8,128)(2,1)S(1)}, bf16[2048,256]{0,1:T(8,128)(2,1)}, u32[]{:S(2)}) copy-start(bf16[2048,256]{0,1:T(8,128)(2,1)} %fusion.204) | copy-start | bytes 3145732
  82.6 21.8 %copy-start.5 = (bf16[188,1024]{1,0:T(8,128)(2,1)}, bf16[188,1024]{1,0:T(8,128)(2,1)S(1)}, u32[]{:S(2)}) copy-start(bf16[188,1024]{1,0:T(8,128)(2,1)S(1)} %fusion.228) | copy-start | bytes 1155076
  87.7 17.4 %copy-start.4 = (bf16[188,1024]{1,0:T(8,128)(2,1)}, bf16[188,1024]{1,0:T(8,128)(2,1)S(1)}, u32[]{:S(2)}) copy-start(bf16[188,1024]{1,0:T(8,128)(2,1)S(1)} %fusion.225) | copy-start | bytes 1155076
  92.8 12.3 %copy-start.3 = (bf16[188,1024]{1,0:T(8,128)(2,1)}, bf16[188,1024]{1,0:T(8,128)(2,1)S(1)}, u32[]{:S(2)}) copy-start(bf16[188,1024]{1,0:T(8,128)(2,1)S(1)} %fusion.222) | copy-start | bytes 1155076
  92.8 50.9 %all-to-all-start.8 = ((bf16[32,32,1024]{2,1,0:T(8,128)(2,1)}), bf16[32,32,1024]{2,1,0:T(8,128)(2,1)}, u32[]{:S(2)}, u32[]{:S(2)}) async-start(bf16[32,32,1024]{2,1,0:T(8,128)(2,1)} %bitcast.16), calls=%async_computation.8 | async-start | bytes 4194304 | tf_op jit(solution)/shard_map/all_to_all | solution.py:38
  103.6 13.0 %copy-start.2 = (bf16[188,1024]{1,0:T(8,128)(2,1)}, bf16[188,1024]{1,0:T(8,128)(2,1)S(1)}, u32[]{:S(2)}) copy-start(bf16[188,1024]{1,0:T(8,128)(2,1)S(1)} %fusion.219) | copy-start | bytes 1155076
  109.6 7.1 %copy-start.20 = (s32[256]{0:T(256)}, s32[256]{0:T(256)S(1)}, u32[]{:S(2)}) copy-start(s32[256]{0:T(256)S(1)} %select_reduce_fusion.3.row_of) | copy-start | bytes 3076
  124.6 3.1 slice-start.3
  124.6 5.1 slice-start.2
  124.8 6.9 %slice-start.1 = ((bf16[188,1024]{1,0:T(8,128)(2,1)}), bf16[124,1024]{1,0:T(8,128)(2,1)S(1)}, s32[]{:S(2)}) async-start(bf16[188,1024]{1,0:T(8,128)(2,1)} %copy-done.3), calls=%async_computation.11 | async-start | bytes 524288 | tf_op jit(solution)/shard_map/slice | solution.py:822
  125.0 7.8 %slice-start = ((bf16[188,1024]{1,0:T(8,128)(2,1)}), bf16[124,1024]{1,0:T(8,128)(2,1)S(1)}, s32[]{:S(2)}) async-start(bf16[188,1024]{1,0:T(8,128)(2,1)} %copy-done.2), calls=%async_computation.10 | async-start | bytes 524288 | tf_op jit(solution)/shard_map/slice | solution.py:822
  153.2 136.3 %all-to-all-start = ((bf16[32,32,1024]{2,1,0:T(8,128)(2,1)}), bf16[32,32,1024]{2,1,0:T(8,128)(2,1)}, u32[]{:S(2)}, u32[]{:S(2)}) async-start(bf16[32,32,1024]{2,1,0:T(8,128)(2,1)} %bitcast.308), calls=%async_computation | async-start | bytes 4194304 | tf_op jit(solution)/shard_map/cond/branch_1_fun/all_to_all | solution.py:38
  289.5 124.4 %all-to-all-start.1 = ((bf16[32,32,1024]{2,1,0:T(8,128)(2,1)}), bf16[32,32,1024]{2,1,0:T(8,128)(2,1)}, u32[]{:S(2)}, u32[]{:S(2)}) async-start(bf16[32,32,1024]{2,1,0:T(8,128)(2,1)} %bitcast.8), calls=%async_computation.1 | async-start | bytes 4194304 | tf_op jit(solution)/shard_map/cond/branch_1_fun/all_to_all | solution.py:38
  600.0 18.3 %copy-start.19 = (s32[1024]{0:T(1024)S(1)}, s32[1024]{0:T(1024)}, u32[]{:S(2)}) copy-start(s32[1024]{0:T(1024)} %get-tuple-element.468) | copy-start | bytes 12292 | tf_op jit(solution)/shard_map/cond
  618.3 5.3 copy-start.21

commit v4 on v3

--- a/solution.py
+++ b/solution.py
@@ -289,104 +289,160 @@
     return jax.ShapeDtypeStruct(shape, dtype)
 
 
-def backward_kernel(n_f, r_in, ss, wp, es, wg, xs, cls_t, hs, wu, wd, *refs):
-    prev, refs = (refs[0], refs[1:]) if len(refs) > 20 else (None, refs)
-    sums, r, tot, out, refs = (*refs[:3], refs[3], refs[4:]) if prev is not None else (*refs[:3], None, refs[3:])
-    c_now, acc, three, s_now, p_now, e_now, g_now, x_now, loads, sems, sems_f, *bufs = refs
-    f = pl.program_id(0)
+def backward_kernel(n_l, n_f, r_in, ss, wp, es, wg, xs, cls_t, hs, wu, wd, sums_out, out,
+                    r, c_now, acc, three, s_now, p_now, e_now, g_now, x_now, sums, totals, loads, sems, sems_few, sems_f, *bufs):
+    step = pl.program_id(0)
+    f, n_full = step % n_f, (n_l - 1) * n_f
     n_tok = len(c_now)
+    parts = chunks(n_tok, ROWS_B)
+    n_hot, n_tot = COLD_AT - HOT_AT, n_l * RUN
     at = Place()
-    gather = None if prev is None else Spread(at, prev.at[pl.ds(HOT_AT, COLD_AT - HOT_AT)], lambda d: out.at[d], sems)
-    fold = Fold(at, sums.at[pl.ds(0, FREQ)], bufs, sems_f)
-    rounded = r_in.dtype == BF
-    srcs = (wp, p_now), (r_in, c_now if rounded else r), (ss, s_now), (es, e_now), (wg, g_now), (xs, x_now)
-    copies = [pltpu.make_async_copy(src, dst, loads.at[i]) for i, (src, dst) in enumerate(srcs)]
-
-    def talk(*steps):
-        if gather is not None:
-            for name, k in steps:
-                getattr(gather, name)(k)
-
-    @pl.when(f == 0)
-    def _():
-        for c in copies:
+    folds = [Fold(at, sums.at[i, pl.ds(0, FREQ)], bufs[i * len(bufs) // n_l:(i + 1) * len(bufs) // n_l], sems_f.at[i]) for i in range(n_l)]
+    alls = [Spread(at, sums.at[i, pl.ds(HOT_AT, n_hot)], lambda d, i=i: out.at[d, pl.ds(n_hot * i, n_hot)], sems.at[i]) for i in range(n_l)]
+    few = Spread(at, totals, lambda d: out.at[d, pl.ds(n_hot * n_l, n_tot)], sems_few)
+
+    def total(i):
+        t = folds[i].total()
+        for z in STOPS:
+            @pl.when(at.z == z)
+            def _(z=z):
+                totals[pl.ds(i * RUN, RUN), :] = t[z * RUN:(z + 1) * RUN, :]
+
+    def load(layer, which):
+        srcs = (wp, p_now), (ss, s_now), (es, e_now), (wg, g_now), (xs, x_now)
+        return [pltpu.make_async_copy(srcs[i][0].at[layer], srcs[i][1], loads.at[i]) for i in which]
+
+    early, late = range(4), range(4, 5)
+    layer = n_l - 1 - step // n_f
+    first = pltpu.make_async_copy(r_in, c_now, loads.at[5])
+
+    plan = {}
+    for i in range(n_l):
+        steps = [(1, folds[i].begin, ()), (2, folds[i].step, (0,)), (2, alls[i].begin, ()), (4, folds[i].step, (1,)), (5, alls[i].onward, (0,)),
+                 (6, alls[i].column, (1,)), (6, folds[i].step, (2,)), (8, alls[i].column, (2,)), (8, alls[i].onward, (1,)),
+                 (9, total, (i,)), (9, alls[i].column, (3,)), (10, alls[i].onward, (2,)), (11, alls[i].across, (0,)), (11, alls[i].onward, (3,)),
+                 (13, alls[i].across, (1,)), (14, alls[i].across, (2,)), (15, alls[i].across, (3,))]
+        for when, what, args in steps:
+            plan.setdefault(10 * i + when, []).append((what, args))
+    few_steps = [few.begin], *[[few.column, few.onward]] * 3, [few.onward], [few.across] * 4
+    for k, steps in enumerate(few_steps):
+        for j, what in enumerate(steps):
+            args = () if not k else (k - j,) if k < 4 else (3,) if k == 4 else (j,)
+            plan.setdefault(10 * n_l + k - 0.5, []).append((what, args))
+
+    def point(k, now, layers):
+        for i in range(layers):
+            if 10 * i + k in plan:
+                @pl.when(step == i * n_f + now)
+                def _(i=i):
+                    for what, args in plan.pop(10 * i + k):
+                        what(*args)
+
+    @pl.when(step == 0)
+    def _():
+        first.start()
+        for c in load(layer, early):
             c.start()
         at.meet()
-        talk(("begin", 0))
-        for c in copies[:-1]:
+        first.wait()
+        r[...] = c_now[...].astype(F32)
+
+    @pl.when(f == 0)
+    def _():
+        for c in load(layer, early):
             c.wait()
-        for m in chunks(n_tok, ROWS_B):
-            if rounded:
-                r[m, :] = c_now[m, :].astype(F32)
-            else:
-                c_now[m, :] = r[m, :].astype(BF)
-            a = dot_nt(c_now[m, :], p_now[...])
+        for c in load(layer, late):
+            c.start()
+        for m in parts:
+            c = r[m, :].astype(BF)
+            c_now[m, :] = c
+            a = dot_nt(c, p_now[...])
             s = s_now[m, :].astype(F32)
             rows = gelu(s).astype(BF).astype(F32) * a
             for j, part in enumerate(split3(rows)):
                 three[j, m, :] = part
-            ds = (gelu_slope(s) * (a * e_now[m, :].astype(F32))).astype(BF)
-            acc[m, :] = dot_nt(ds, g_now[...])
-        talk(("onward", 0))
-        class_sums(cls_t, three, sums)
-        fold.begin()
-        talk(("column", 1))
-
-    plan = {(0, 1): (("onward", 1), ("column", 2)), (1, 0): (("column", 3),), (1, 1): (("onward", 2),),
-            (2, 0): (("across", 0), ("onward", 3)), (2, 1): (("across", 1),), (3, 0): (("across", 2),)}
-    for i, m in enumerate(chunks(n_tok, ROWS_B)):
-        d_act = dot_nt(c_now[m, :], wd[...])
-        dh = (gelu_slope(hs[m, :].astype(F32)) * d_act).astype(BF)
-        acc[m, :] += dot_nt(dh, wu[...])
-        for k in range(n_f):
-            @pl.when(f == k)
-            def _(k=k, i=i):
-                if i and k < 3:
-                    fold.step(k)
-                talk(*plan.get((k, i), ()))
-
-    @pl.when(f == n_f - 1)
-    def _():
-        copies[-1].wait()
+            e_now[m, :] = (gelu_slope(s) * (a * e_now[m, :].astype(F32))).astype(BF)
+        point(0, 0, n_l)
+        class_sums(cls_t, three, sums.at[step // n_f])
+        point(1, 0, n_l)
+
+    @pl.when((f == 0) & (step < n_full))
+    def _():
+        for m in parts:
+            acc[m, :] = dot_nt(e_now[m, :], g_now[...])
+
+    @pl.when((f == 1) & (step < n_full))
+    def _():
+        for c in load(layer - 1, early):
+            c.start()
+
+    @pl.when(step < n_full)
+    def _():
+        for i, m in enumerate(parts):
+            d_act = dot_nt(c_now[m, :], wd[...])
+            dh = (gelu_slope(hs[m, :].astype(F32)) * d_act).astype(BF)
+            acc[m, :] += dot_nt(dh, wu[...])
+            for k in range(n_f):
+                point(2 + 2 * k + i, k, n_l - 1)
+
+    @pl.when((f == n_f - 1) & (step < n_full))
+    def _():
+        for c in load(layer, late):
+            c.wait()
         for m in chunks(n_tok, ROWS_A):
             x = x_now[m, :].astype(F32)
             k = lax.rsqrt(jnp.mean(x * x, axis=-1, keepdims=True) + NORM_EPS)
             du = acc[m, :]
             inner = jnp.mean(du * x, axis=-1, keepdims=True)
             r[m, :] = r[m, :] + k * du - x * (k * k * k) * inner
-        tot[...] = fold.total()
-        talk(("across", 3), ("end", 0))
-
-
-def backward(layer, r_in, cls_t, es, xs, hs, ss, w_up, w_down, w_gate, w_proj, n_dev, prev=None):
+
+    @pl.when(step == n_full)
+    def _():
+        for c in load(layer, late):
+            c.wait()
+        keep = pltpu.make_async_copy(sums, sums_out, loads.at[5])
+        keep.start()
+        for k in sorted(plan):
+            for what, args in plan[k]:
+                what(*args)
+        for v in (*alls, few):
+            v.end()
+        keep.wait()
+
+
+def backward(r_in, cls_t, es, xs, hs, ss, w_up, w_down, w_gate, w_proj, n_dev):
     n_tok, dim = r_in.shape
-    ff = w_up.shape[2]
+    n_l, _, ff = w_up.shape
     emb = w_gate.shape[2]
     n_c = COLD_AT + COLD_MAX
     n_f = 4
     tile = ff // n_f
-    more = prev is not None
+    n_full = (n_l - 1) * n_f
+    n_out = n_l * (COLD_AT - HOT_AT + RUN)
+
+    def at_layer(t):
+        t = jnp.minimum(t, n_full - 1)
+        return n_l - 1 - t // n_f, t % n_f
 
     def cols(n):
-        return pl.BlockSpec((None, n, tile), lambda t: (layer, 0, t))
-
-    def kernel(r_in, ss, wp, es, wg, xs, *refs):
-        backward_kernel(n_f, r_in, *[v.at[layer] for v in (ss, wp, es, wg, xs)], *refs)
+        return pl.BlockSpec((None, n, tile), lambda t: (at_layer(t)[0], 0, at_layer(t)[1]))
 
     return pl.pallas_call(
-        kernel,
-        grid=(n_f,),
-        in_specs=[ANY] * 6 + [spec((1, n_tok)), cols(n_tok), cols(dim), pl.BlockSpec((None, tile, dim), lambda t: (layer, t, 0))]
-        + [spec((n_c, emb), pipeline_mode=ONCE)] * more,
-        out_specs=[spec((n_c, emb)), spec((n_tok, dim)), spec((16, emb))] + [ANY] * more,
-        out_shape=[out_of((n_c, emb)), out_of((n_tok, dim)), out_of((16, emb))] + [out_of((n_dev, COLD_AT - HOT_AT, emb))] * more,
-        scratch_shapes=[pltpu.VMEM((n_tok, dim), BF), pltpu.VMEM((n_tok, dim), F32), pltpu.VMEM((3, n_tok, emb), BF)]
+        functools.partial(backward_kernel, n_l, n_f),
+        grid=(n_full + 1,),
+        in_specs=[ANY] * 6 + [spec((1, n_tok), pipeline_mode=ONCE), cols(n_tok), cols(dim),
+                              pl.BlockSpec((None, tile, dim), lambda t: (*at_layer(t), 0))],
+        out_specs=[ANY] * 2,
+        out_shape=[out_of((n_l, n_c, emb)), out_of((n_dev, n_out, emb))],
+        scratch_shapes=[pltpu.VMEM((n_tok, dim), F32), pltpu.VMEM((n_tok, dim), BF), pltpu.VMEM((n_tok, dim), F32), pltpu.VMEM((3, n_tok, emb), BF)]
         + [pltpu.VMEM(v, BF) for v in ((n_tok, emb), (emb, dim), (n_tok, emb), (dim, emb), (n_tok, dim))]
-        + [pltpu.SemaphoreType.DMA((6,)), SPREAD_SEMS, FOLD_SEMS] + fold_bufs(emb),
-        compiler_params=params("arbitrary", collective_id=layer, has_side_effects=True),
-        cost_estimate=cost(n_tok * dim * (2 * ff + 2 * emb + 3 * n_c), 1),
+        + [pltpu.VMEM((n_l, n_c, emb), F32), pltpu.VMEM((n_l * RUN, emb), F32), pltpu.SemaphoreType.DMA((6,)),
+           pltpu.SemaphoreType.DMA((n_l, *SPREAD_SEMS)), pltpu.SemaphoreType.DMA(SPREAD_SEMS), pltpu.SemaphoreType.DMA((n_l, *FOLD_SEMS))]
+        + fold_bufs(emb) * n_l,
+        compiler_params=params("arbitrary", collective_id=0, has_side_effects=True),
+        cost_estimate=cost(n_l * n_tok * dim * (2 * ff + 2 * emb + 3 * n_c), n_l),
         name="backward",
-    )(r_in, ss, w_proj, es, w_gate, xs, cls_t, hs, w_up, w_down, *([prev] if more else []))
+    )(r_in, ss, w_proj, es, w_gate, xs, cls_t, hs, w_up, w_down)
 
 
 def count_kernel(ids, out):
@@ -477,7 +533,7 @@
     def got(self, kind, k, block):
         remote(block, block, self.pair(kind, k), self.at.to_x).wait_recv()
 
-    def begin(self, _=None):
+    def begin(self):
         own = self.slot(self.col[0])
         pltpu.make_async_copy(self.mine, own, self.sems.at[0, OWN, 0]).start()
         for k, other in enumerate(self.at.others):
@@ -506,7 +562,7 @@
             self.got(kind, k, block.at[half])
         self.send(CD, k, block, block, self.at.to_core)
 
-    def end(self, _=None):
+    def end(self):
         for k in STOPS:
             for kind, far in zip((C, CX, CY, CD), self.far):
                 self.got(kind, k, self.slot(far[k]))
@@ -570,167 +626,86 @@
     return [pltpu.VMEM((n, emb), F32) for n in (64, 32, 16, 64, 32)] + [pltpu.VMEM((4, 16, emb), F32)]
 
 
-SPREAD_SEMS = pltpu.SemaphoreType.DMA((2, 10, 4))
+SPREAD_SEMS = (2, 10, 4)
 STOPS = range(4)
 REST = STOPS[1:]
-FOLD_SEMS = pltpu.SemaphoreType.DMA((2, 4, 4))
+FOLD_SEMS = (2, 4, 4)
 HOT_AT, COLD_AT = FREQ, FREQ + 64
 
 
-def last_kernel(r_in, ss, wp, cls_t, prev, *refs):
-    early, (sums, out, r, s, w, three, pay, loads, sems_1, sems_0, sems_f, *bufs) = refs[:3], refs[3:]
-    n_hot = COLD_AT - HOT_AT
-    n = pay.shape[1]
-    copies = [pltpu.make_async_copy(src, dst, loads.at[i]) for i, (src, dst) in enumerate(((r_in, r), (ss.at[0], s), (wp.at[0], w)))]
-    for c in copies:
-        c.start()
-    at = Place()
-    at.meet()
-
-    def fill(i, hot, totals):
-        pay[i, pl.ds(0, n_hot), :] = hot
-        for z in STOPS:
-            @pl.when(at.z == z)
-            def _(z=z):
-                for j, t in enumerate(totals):
-                    pay[i, pl.ds(n_hot + RUN * j, RUN), :] = t[z * RUN:(z + 1) * RUN, :]
-
-    fold = Fold(at, sums.at[pl.ds(0, FREQ)], bufs, sems_f)
-    all_1, all_0 = [Spread(at, pay.at[i], lambda d, i=i: out.at[d, pl.ds(STRIDE * i, n)], sems) for i, sems in enumerate((sems_1, sems_0))]
-    fill(0, prev[pl.ds(HOT_AT, n_hot), :], [t[...] for t in early[:2]])
-    all_1.begin()
-    for c in copies:
-        c.wait()
-    for m in chunks(len(r), ROWS_B):
-        a = dot_nt(r[m, :].astype(BF), w[...])
-        rows = gelu(s[m, :].astype(F32)).astype(BF).astype(F32) * a
-        for i, part in enumerate(split3(rows)):
-            three[i, m, :] = part
-    all_1.onward(0)
-    class_sums(cls_t, three, sums)
-    fold.begin()
-    all_1.column(1)
-    for k in REST:
-        fold.step(k - 1)
-        all_1.onward(k)
-        if k < REST[-1]:
-            all_1.column(k + 1)
-    all_1.across(0)
-    fill(1, sums[pl.ds(HOT_AT, n_hot), :], [early[2][...], fold.total()])
-    all_0.begin()
-    for k in REST:
-        all_1.across(k)
-        all_0.onward(k - 1)
-        all_0.column(k)
-    all_0.across(0)
-    all_0.onward(REST[-1])
-    for k in REST:
-        all_0.across(k)
-    all_1.end()
-    all_0.end()
-
-
 def class_sums(cls_t, three, sums):
-    pick_t = (cls_t[...] == iota((len(sums), cls_t.shape[1]), 0)).astype(BF)
+    pick_t = (cls_t[...] == iota((sums.shape[0], cls_t.shape[1]), 0)).astype(BF)
     hi, mid, lo = [dot32(pick_t, three[i]) for i in range(3)]
     sums[...] = hi + (mid + lo)
 
 
-STRIDE = 80
-
-
-def last(r_in, ss, w_proj, cls_t, prev, tots, n_dev):
-    n_tok, dim = r_in.shape
-    n_c, emb = prev.shape
-    n = COLD_AT - HOT_AT + 2 * RUN
-    vmem = pl.BlockSpec(memory_space=pltpu.VMEM)
-    return pl.pallas_call(
-        last_kernel,
-        in_specs=[ANY] * 3 + [vmem] * (2 + len(tots)), out_specs=[vmem, ANY],
-        out_shape=[out_of((n_c, emb)), out_of((n_dev, 2 * STRIDE, emb))],
-        scratch_shapes=[pltpu.VMEM((n_tok, dim), F32), pltpu.VMEM((n_tok, emb), BF), pltpu.VMEM((emb, dim), BF),
-                        pltpu.VMEM((3, n_tok, emb), BF), pltpu.VMEM((2, n, emb), F32), pltpu.SemaphoreType.DMA((3,)),
-                        SPREAD_SEMS, SPREAD_SEMS, FOLD_SEMS] + fold_bufs(emb),
-        compiler_params=params(collective_id=0, has_side_effects=True),
-        cost_estimate=cost(n_tok * dim * 4 * emb, 1), name="last",
-    )(r_in, ss, w_proj, cls_t, prev, *tots)
-
-
 ORDER = [(b & 3) * 8 + (b >> 2 & 1) * 4 + (b >> 3 & 1) * 2 + (b >> 4) for b in range(FREQ // RUN)]
 
 
-def hot_kernel(skip, any_freq, raw, freq, code, into, out, parts):
+def hot_kernel(any_freq, raw, freq, code, out, parts):
     n_dev, n_r, _ = raw.shape
     layer, block = pl.program_id(0), pl.program_id(1)
     n = RUN * n_dev
     for g in range(n_r // RUN):
         for o in range(n_dev):
-            out[0, pl.ds(g * n + o * RUN, RUN), :] = raw[o, pl.ds(g * RUN, RUN), :]
+            out[pl.ds(g * n + o * RUN, RUN), :] = raw[o, pl.ds(g * RUN, RUN), :]
 
     @pl.when(any_freq[block] > 0)
     def _():
-        for j in range(2):
-            @pl.when(layer + skip == j)
+        for j in range(freq.shape[1] // RUN):
+            @pl.when(layer == j)
             def _(j=j):
                 rows = jnp.concatenate([freq[o, j * RUN:(j + 1) * RUN, :] for o in ORDER])
                 for i, part in enumerate(split3(rows)):
                     parts[i] = part
-        sel = (code[0] == iota((n_r * n_dev, FREQ), 1)).astype(BF)
-        out[0] += dot32(sel, parts[0]) + (dot32(sel, parts[1]) + dot32(sel, parts[2]))
-
-
-def hot_out(first, n_l, gathered, freq_from, freq_at, skip, code, into):
-    n_dev, _, emb = gathered.shape
+        sel = (code[...] == iota((n_r * n_dev, FREQ), 1)).astype(BF)
+        out[...] += dot32(sel, parts[0]) + (dot32(sel, parts[1]) + dot32(sel, parts[2]))
+
+
+def hot_out(gathered, code, n_l):
+    n_dev, n_rows, emb = gathered.shape
     n_r = 4 * RUN
     width = n_r * n_dev
-    blocks = into.shape[1] // width
-    code = code.reshape(blocks, width, 1)
+    blocks = len(code) // width
     return pl.pallas_call(
-        functools.partial(hot_kernel, skip),
+        hot_kernel,
         grid_spec=pltpu.PrefetchScalarGridSpec(
             num_scalar_prefetch=1, grid=(n_l, blocks),
             in_specs=[
-                pl.BlockSpec((n_dev, n_r, emb), lambda i, b, _: (0, i * (STRIDE // n_r) + b, 0)),
-                spec((n_dev, 2 * RUN, emb), 0, freq_at, 0, pipeline_mode=ONCE),
-                pl.BlockSpec((1, width, 1), lambda i, b, _: (b, 0, 0)),
-                ANY,
+                pl.BlockSpec((n_dev, n_r, emb), lambda i, b, _: (0, i * blocks + b, 0)),
+                spec((n_dev, n_l * RUN, emb), 0, n_rows // (n_l * RUN) - 1, 0, pipeline_mode=ONCE),
+                pl.BlockSpec((width, 1), lambda i, b, _: (b, 0)),
             ],
-            out_specs=pl.BlockSpec((1, width, emb), lambda i, b, _: (first - i, b, 0)),
+            out_specs=pl.BlockSpec((None, width, emb), lambda i, b, _: (n_l - 1 - i, b, 0)),
             scratch_shapes=[pltpu.VMEM((3, FREQ, emb), BF)]),
-        out_shape=out_of(into.shape),
-        input_output_aliases={4: 0},
+        out_shape=out_of((n_l, len(code), emb)),
         compiler_params=params("arbitrary", "arbitrary"),
-        cost_estimate=cost(n_l * gathered.size * LO, n_l), name="hot_out",
-    )((code[:, :, 0] >= 0).any(axis=1).astype(I32), gathered, freq_from, code, into)
-
-
-def empty(shape):
-    return pl.pallas_call(lambda out: None, out_specs=ANY, out_shape=out_of(shape), name="empty")()
-
-
-def rows_kernel(numbers, row_of, *refs):
-    srcs, (freq, into, out, stage, got, sem) = refs[:-6], refs[-6:]
+        cost_estimate=cost(gathered.size * LO, n_l), name="hot_out",
+    )((code.reshape(blocks, width) >= 0).any(axis=1).astype(I32), gathered, gathered, code.reshape(-1, 1))
+
+
+def rows_kernel(numbers, row_of, sums, freq, into, out, stage, got, sem):
     n_used, cold_row, cold_no = [numbers[i] for i in range(3)]
-    n_l = len(srcs)
+    n_l = len(sums)
 
     def put(k, row):
         return pltpu.make_async_copy(stage.at[pl.ds(k, 1)], out.at[pl.ds(row, 1)], sem)
 
+    def fill(k, src, at):
+        for i in range(n_l):
+            stage[k, pl.ds(n_l - 1 - i, 1), :] = src(i, at)
+
     @pl.loop(0, n_used)
     def _(k):
-        for l, src in enumerate(srcs):
-            stage[k, pl.ds(l, 1), :] = src[pl.ds(COLD_AT + k, 1), :]
+        fill(k, lambda i, at: sums[i, pl.ds(at, 1), :], COLD_AT + k)
         put(k, row_of[k]).start()
 
     @pl.when(cold_row >= 0)
     def _():
-        for j in range(2):
-            c = pltpu.make_async_copy(freq.at[len(freq) - 1, pl.ds(j * STRIDE + COLD_AT - HOT_AT, 8)], got.at[j], sem)
-            c.start()
-            c.wait()
-        for l in range(n_l):
-            i = n_l - 1 - l
-            stage[COLD_MAX, pl.ds(l, 1), :] = got[i // 2, pl.ds(i % 2 * RUN + cold_no, 1), :]
+        c = pltpu.make_async_copy(freq.at[len(freq) - 1, pl.ds(n_l * (COLD_AT - HOT_AT), n_l * RUN)], got, sem)
+        c.start()
+        c.wait()
+        fill(COLD_MAX, lambda i, at: got[pl.ds(i * RUN + at, 1), :], cold_no)
         put(COLD_MAX, cold_row).start()
         put(0, 0).wait()
 
@@ -739,19 +714,17 @@
         put(0, 0).wait()
 
 
-def put_rows(numbers, row_of, srcs, freq, into):
-    n_l = len(srcs)
-    shape = srcs[0].shape
-    emb = shape[-1]
+def put_rows(numbers, row_of, sums, freq, into):
+    n_l, _, emb = sums.shape
     return pl.pallas_call(
         rows_kernel,
         grid_spec=pltpu.PrefetchScalarGridSpec(
             num_scalar_prefetch=2, grid=(1,),
-            in_specs=[spec(shape)] * n_l + [ANY, ANY], out_specs=ANY,
-            scratch_shapes=[pltpu.VMEM((COLD_MAX + 1, n_l, emb), F32), pltpu.VMEM((2, 8, emb), F32), pltpu.SemaphoreType.DMA(())]),
-        out_shape=out_of(into.shape), input_output_aliases={n_l + 3: 0},
+            in_specs=[spec(sums.shape), ANY, ANY], out_specs=ANY,
+            scratch_shapes=[pltpu.VMEM((COLD_MAX + 1, n_l, emb), F32), pltpu.VMEM((n_l * RUN, emb), F32), pltpu.SemaphoreType.DMA(())]),
+        out_shape=out_of(into.shape), input_output_aliases={4: 0},
         compiler_params=params("arbitrary"), name="put_rows",
-    )(numbers, row_of, *srcs, freq, into)
+    )(numbers, row_of, sums, freq, into)
 
 
 def down_sum(v):
@@ -885,22 +858,14 @@
             d_moved = exchange(d_placed)
             cls_row = cls.reshape(1, n_loc)
             xs, hs, ss, es, x_last, zeros = forward(x_moved, cls.reshape(n_loc, 1), table, w_up, w_down, w_gate, w_proj, rows_dev)
+            sums, gathered = backward(d_moved, cls_row, es, xs, hs, ss, w_up, w_down, w_gate, w_proj, n_dev)
+            x_last, gathered = lax.optimization_barrier((x_last, gathered))
             x_back = exchange(x_last)
-            kept = (cls_row, es, xs, hs, ss, w_up, w_down, w_gate, w_proj, n_dev)
-            sums_3, r, tot_3 = backward(3, d_moved, *kept)
-            sums_2, r, tot_2, all_3 = backward(2, r, *kept, sums_3)
-            r, x_back = lax.optimization_barrier((r, x_back))
-            sums_1, r, tot_1, all_2 = backward(1, r, *kept, sums_2)
-            sums_0, all_b = last(r, ss, w_proj, cls_row, sums_1, (tot_3, tot_2, tot_1), n_dev)
+            numbers = jnp.stack([n_used, my_row, jnp.sum(my_cold * jnp.arange(FREQ_COLD, dtype=I32))])
+            d_table = put_rows(numbers, row_of, sums, gathered, zeros)
+            d_hot = hot_out(gathered, code, layers)
             x_out = dot32((col(slot) == iota((n_loc, n_loc), 1)).astype(BF), x_back).astype(BF)
-            numbers = jnp.stack([n_used, my_row, jnp.sum(my_cold * jnp.arange(FREQ_COLD, dtype=I32))])
-            d_table = put_rows(numbers, row_of, [sums_0, sums_1, sums_2, sums_3], all_b, zeros)
-            freq_at = hot_dev // (2 * RUN)
-            into = empty((layers, n_hot, emb_dim))
-            into = hot_out(3, 1, all_3, all_b, freq_at, 0, code, into)
-            into = hot_out(2, 1, all_2, all_b, freq_at, 1, code, into)
-            into = hot_out(1, 2, all_b, all_b, freq_at + STRIDE // (2 * RUN), 0, code, into)
-            return x_out, d_table.transpose(1, 0, 2), into
+            return x_out, d_table.transpose(1, 0, 2), d_hot
 
         def slow(*_):
             return general_path(n_dev, me, token_ids, hot_ids, x_in, d_out, emb_table, hot_table, w_up, w_down, w_gate, w_proj)

time: 647 us -> 584 us (0.903)
  the two profiles are of different devices: /device:TPU:21 before, /device:TPU:0 now
where the time goes in v4:
time: 584 us; the launch traced here: 574 us
  Pallas kernels  399 us (68%)
  matrix products  42.1 us (7%)
  starting transfers between devices  32.7 us (6%)
  waiting for transfers between devices  27.6 us (5%)
  other arithmetic  24.5 us (4%)
  local copies, waits for them, and re-layouts  20.2 us (3%)
  between operations  19 us (3%)
  loops' own time  9.26 us (2%)
    pallas_call x1, Pallas kernels, backward(): pl.pallas_call(functools.partial(backward_kernel, n_l, n_f), grid=(n_full...  215 us
    pallas_call x1, Pallas kernels, forward(): pl.pallas_call(functools.partial(forward_kernel, n_l, n_f), grid=(n_l, n_...  123 us
    dot_general x19, matrix products, dot32(): return jnp.dot(a, b, preferred_element_type=F32)  42.1 us
    pallas_call x1, Pallas kernels, hot_out(): pl.pallas_call(hot_kernel, grid_spec=pltpu.PrefetchScalarGridSpec(num_sca...  35.3 us
    all_to_all x6, starting transfers between devices, swap(): return lax.all_to_all(v, 'emb', 0, 0, tiled=True)  32.7 us
    all_to_all x6, waiting for transfers between devices, swap(): return lax.all_to_all(v, 'emb', 0, 0, tiled=True)  27.6 us
    pallas_call x1, Pallas kernels, count_ids(): pl.pallas_call(count_kernel, out_shape=out_of((n_hi, LO)), compiler_param...  12.6 us
  transfers between devices with their start and end apart: 6, of which 4 were waited for; matrix products, arithmetic and copies ran while one was open for 8% of the time, Pallas kernels for 30%

profile of v4, /device:TPU:0, one launch (start us, length us, event | category | flops | bytes accessed | tf_op | source)
XLA Modules:
  0.0 574.4 jit_solution(10900258640285820028)
XLA Ops:
  7.2 3.1 copy.215
  10.3 0.7 broadcast_in_dim.279
  11.0 7.3 %all-to-all-start.5 = ((s32[32,1,1024]{2,1,0:T(1,128)}), s32[32,1,1024]{2,1,0:T(1,128)S(1)}, u32[]{:S(2)}, u32[]{:S(2)}) async-start(s32[32,1,1024]{2,1,0:T(1,128)} %broadcast_in_dim.279), calls=%async_computation.5 | async-start | bytes 262144 | tf_op jit(solution)/shard_map/all_to_all | solution.py:38
  19.0 1.3 fusion.207
  20.3 1.2 fusion.204
  21.5 0.9 convolution_convert_fusion
  22.5 4.0 all-to-all-done.5
  27.2 12.6 %count_ids.1 = f32[200,256]{1,0:T(8,128)} custom-call(s32[32,1024]{1,0:T(8,128)} %bitcast.316), custom_call_target="tpu_custom_call" | custom-call | tf_op jit(solution)/shard_map/count_ids/pallas_call | solution.py:463
  39.9 0.9 compare_convert_fusion.4
  40.8 1.8 broadcast_select_fusion.2
  42.6 1.4 convert_reduce_fusion
  44.6 1.4 convert_reduce_fusion.2
  46.6 0.8 fusion.255
  49.0 1.1 fusion.325
  51.5 0.8 broadcast_in_dim.294
  52.3 2.6 all-to-all-start.6
  58.1 0.9 fusion.215
  58.9 1.2 fusion.214
  61.6 5.4 fusion.211
  67.7 5.8 %all-to-all-start.7 = ((s32[32,1,32]{2,1,0:T(1,128)}), s32[32,1,32]{2,1,0:T(1,128)S(1)}, u32[]{:S(2)}, u32[]{:S(2)}) async-start(s32[32,1,32]{2,1,0:T(1,128)} %all_to_all.45), calls=%async_computation.7 | async-start | bytes 32768 | tf_op jit(solution)/shard_map/all_to_all | solution.py:38
  73.6 3.7 fusion.210
  77.2 0.8 copy.130
  78.0 2.7 all-to-all-done.7
  82.1 1.7 fusion.218
  84.4 4.9 fusion.228
  89.3 5.1 fusion.225
  94.4 5.1 fusion.222
  99.5 3.5 all-to-all-start.8
  103.0 4.9 fusion.219
  108.0 0.7 slice.148
  110.2 1.7 select_reduce_fusion.1
  113.5 1.1 select_reduce_fusion.3.row_of
  114.6 8.0 %pack_rows.1 = bf16[256,4,1024]{2,1,0:T(4,128)(2,1)} custom-call(s32[256]{0:T(256)S(1)} %select_reduce_fusion.3.row_of, bf16[1572,4,1024]{2,1,0:T(4,128)(2,1)} %bitcast.306), custom_call_target="tpu_custom_call" | custom-call | tf_op jit(solution)/shard_map/pack_rows/pallas_call | solution.py:476
  122.6 7.9 %fusion.328 = (bf16[256,1,1024]{2,1,0:T(2,128)(2,1)S(1)}, bf16[256,1,1024]{2,1,0:T(2,128)(2,1)S(1)}, bf16[256,1,1024]{2,1,0:T(2,128)(2,1)S(1)}, bf16[256,1,1024]{2,1,0:T(2,128)(2,1)S(1)}) fusion(bf16[256,4,1024]{2,1,0:T(4,128)(2,1)} %pack_rows.1), kind=kLoop, calls=%fused_computation.455 | loop fusion | bytes 4194304 | tf_op jit(solution)/shard_map/slice | solution.py:796
  132.6 2.1 pad_maximum_fusion
  134.7 17.1 %all-to-all-done.8 = bf16[32,32,1024]{2,1,0:T(8,128)(2,1)} async-done(((bf16[32,32,1024]{2,1,0:T(8,128)(2,1)}), bf16[32,32,1024]{2,1,0:T(8,128)(2,1)}, u32[]{:S(2)}, u32[]{:S(2)}) %all-to-all-start.8) | async-done | bytes 2097184 | tf_op jit(solution)/shard_map/all_to_all | solution.py:38
  151.8 415.2 %conditional.1 = (bf16[1024,1024]{1,0:T(8,128)(2,1)}, f32[4,1572,1024]{2,0,1:T(4,128)}, f32[4,2048,1024]{2,1,0:T(8,128)}) conditional(s32[]{:T(128)} %convert_element_type.449, (s32[1024]{0:T(1024)S(1)}, s32[2048]{0:T(1024)S(1)}, s32[]{:T(128)}, bf16[4,1024,4096]{2,1,0:T(8,128)(2,1)}, bf16[4,4096,1024]{2,1,0:T(8,128)(2,1)}, ...), branch_computations={%region_29.45_spmd, %region_45.48_spmd} | conditional | flops 193544060928 | bytes 561294080 | solution.py:873
  160.7 4.1 all-to-all-start
  164.8 1.0 copy.118.cls
  165.8 122.9 %forward.1 = (bf16[4,1024,1024]{2,1,0:T(8,128)(2,1)}, bf16[4,1024,4096]{2,1,0:T(8,128)(2,1)}, bf16[4,1024,1024]{2,1,0:T(8,128)(2,1)}, bf16[4,1024,1024]{2,1,0:T(...) custom-call(bf16[1024,1024]{1,0:T(8,128)(2,1)} %get-tuple-element.469.x0, s32[1024,1]{1,0:T(8,128)} %copy.118.cls, ...), custom_call_target="tpu_custom_call" | custom-call | flops 89657442304 | bytes 160000000 | tf_op jit(solution)/shard_map/cond/branch_1_fun/forward/pallas_call | solution.py:243
  288.8 214.6 %backward.1 = (f32[4,448,1024]{2,1,0:T(8,128)}, f32[32,272,1024]{2,1,0:T(8,128)}) custom-call(bf16[1024,1024]{1,0:T(8,128)(2,1)} %bitcast.6.r_in, bf16[4,1024,1024]{2,1,0:T(8,128)(2,1)} %get-tuple-element.478.ss, bf16[4,1024,1024]{2,1,0:T(8,128)(2,1)} %get-tuple-element.475.wp, bf16[4,1024,1024]{2,1,0:T(8,128)(2,1)} %get-tuple-element.479.es, ...), custom_call_target="tpu_custom_call" | custom-call | flops 97173635072 | bytes 160000000 | tf_op jit(solution)/shard_map/cond/branch_1_fun/backward/pallas_call | solution.py:430
  503.4 9.4 %all-to-all-start.1 = ((bf16[32,32,1024]{2,1,0:T(8,128)(2,1)}), bf16[32,32,1024]{2,1,0:T(8,128)(2,1)}, u32[]{:S(2)}, u32[]{:S(2)}) async-start(bf16[32,32,1024]{2,1,0:T(8,128)(2,1)} %bitcast.312), calls=%async_computation.1 | async-start | bytes 4194304 | tf_op jit(solution)/shard_map/cond/branch_1_fun/all_to_all | solution.py:38
  513.4 1.4 copy.119.code
  515.5 1.3 pad_add_fusion.numbers
  516.8 5.6 put_rows.1
  522.4 35.3 %hot_out.1 = f32[4,2048,1024]{2,1,0:T(8,128)} custom-call(s32[4]{0:T(128)} %convert_element_type.375.any_freq, f32[32,272,1024]{2,1,0:T(8,128)} %get-tuple-element.489.freq.raw, f32[32,272,1024]{2,1,0:T(8,128)} %get-tuple-element.489.freq.raw, s32[2048,1]{1,0:T(8,128)} %copy.119.code), custom_call_target="tpu_custom_call" | custom-call | flops 4563402752 | bytes 160000000 | tf_op jit(solution)/shard_map/cond/branch_1_fun/hot_out/pallas_call | solution.py:670
  557.7 3.8 all-to-all-done.1
  561.5 5.3 fusion.6
  (115 shorter events, 15.2 us)
Async XLA Ops:
  7.2 3.1 copy-start.13
  7.2 11.8 %copy-start.23 = (s32[2048]{0:T(1024)S(1)}, s32[2048]{0:T(1024)}, u32[]{:S(2)}) copy-start(s32[2048]{0:T(1024)} %param.19) | copy-start | bytes 24580
  11.0 15.5 %all-to-all-start.5 = ((s32[32,1,1024]{2,1,0:T(1,128)}), s32[32,1,1024]{2,1,0:T(1,128)S(1)}, u32[]{:S(2)}, u32[]{:S(2)}) async-start(s32[32,1,1024]{2,1,0:T(1,128)} %broadcast_in_dim.279), calls=%async_computation.5 | async-start | bytes 262144 | tf_op jit(solution)/shard_map/all_to_all | solution.py:38
  20.3 22.2 %copy-start.24 = (f32[27]{0:T(128)S(1)}, f32[27]{0:T(128)}, u32[]{:S(2)}) copy-start(f32[27]{0:T(128)} %constant.380.clone) | copy-start | bytes 328
  46.6 10.8 %copy-start.27 = (s32[32]{0:T(128)S(1)}, s32[32]{0:T(128)}, u32[]{:S(2)}) copy-start(s32[32]{0:T(128)} %iota_multiply_fusion.1) | copy-start | bytes 388
  49.0 5.9 %copy-start.25 = (s32[4]{0:T(128)}, s32[4]{0:T(128)S(1)}, u32[]{:S(2)}) copy-start(s32[4]{0:T(128)S(1)} %get-tuple-element.518) | copy-start | bytes 52
  52.3 14.8 %all-to-all-start.6 = ((bf16[32,4,1024]{2,1,0:T(4,128)(2,1)}), bf16[32,4,1024]{2,1,0:T(4,128)(2,1)S(1)}, u32[]{:S(2)}, u32[]{:S(2)}) async-start(bf16[32,4,1024]{2,1,0:T(4,128)(2,1)} %broadcast_in_dim.294), calls=%async_computation.6 | async-start | bytes 524288 | tf_op jit(solution)/shard_map/all_to_all | solution.py:38
  57.5 16.0 %copy-start.19 = (s32[1024]{0:T(1024)}, s32[1024]{0:T(1024)S(1)}, u32[]{:S(2)}) copy-start(s32[1024]{0:T(1024)S(1)} %fusion.284) | copy-start | bytes 12292
  61.6 12.0 %copy-start = (bf16[1024,1024]{1,0:T(8,128)(2,1)S(1)}, bf16[1024,1024]{1,0:T(8,128)(2,1)}, u32[]{:S(2)}) copy-start(bf16[1024,1024]{1,0:T(8,128)(2,1)} %copy.215) | copy-start | bytes 6291460
  67.7 13.0 %all-to-all-start.7 = ((s32[32,1,32]{2,1,0:T(1,128)}), s32[32,1,32]{2,1,0:T(1,128)S(1)}, u32[]{:S(2)}, u32[]{:S(2)}) async-start(s32[32,1,32]{2,1,0:T(1,128)} %all_to_all.45), calls=%async_computation.7 | async-start | bytes 32768 | tf_op jit(solution)/shard_map/all_to_all | solution.py:38
  73.6 8.5 %copy-start.6 = (bf16[2048,200]{1,0:T(8,128)(2,1)S(1)}, bf16[2048,200]{1,0:T(8,128)(2,1)}, u32[]{:S(2)}) copy-start(bf16[2048,200]{1,0:T(8,128)(2,1)} %fusion.207) | copy-start | bytes 2457604
  89.3 19.4 %copy-start.4 = (bf16[188,1024]{1,0:T(8,128)(2,1)}, bf16[188,1024]{1,0:T(8,128)(2,1)S(1)}, u32[]{:S(2)}) copy-start(bf16[188,1024]{1,0:T(8,128)(2,1)S(1)} %fusion.228) | copy-start | bytes 1155076
  94.4 14.3 %copy-start.3 = (bf16[188,1024]{1,0:T(8,128)(2,1)}, bf16[188,1024]{1,0:T(8,128)(2,1)S(1)}, u32[]{:S(2)}) copy-start(bf16[188,1024]{1,0:T(8,128)(2,1)S(1)} %fusion.225) | copy-start | bytes 1155076
  99.5 9.3 %copy-start.2 = (bf16[188,1024]{1,0:T(8,128)(2,1)}, bf16[188,1024]{1,0:T(8,128)(2,1)S(1)}, u32[]{:S(2)}) copy-start(bf16[188,1024]{1,0:T(8,128)(2,1)S(1)} %fusion.222) | copy-start | bytes 1155076
  99.5 52.3 %all-to-all-start.8 = ((bf16[32,32,1024]{2,1,0:T(8,128)(2,1)}), bf16[32,32,1024]{2,1,0:T(8,128)(2,1)}, u32[]{:S(2)}, u32[]{:S(2)}) async-start(bf16[32,32,1024]{2,1,0:T(8,128)(2,1)} %bitcast.17), calls=%async_computation.8 | async-start | bytes 4194304 | tf_op jit(solution)/shard_map/all_to_all | solution.py:38
  108.0 0.9 copy-start.5
  114.6 8.1 %copy-start.21 = (s32[256]{0:T(256)}, s32[256]{0:T(256)S(1)}, u32[]{:S(2)}) copy-start(s32[256]{0:T(256)S(1)} %select_reduce_fusion.3.row_of) | copy-start | bytes 3076
  130.5 1.0 copy-start.12
  130.5 0.9 copy-start.26
  130.6 1.1 slice-start.3
  130.6 1.4 slice-start.2
  130.6 1.4 copy-start.7
  130.8 1.5 slice-start.1
  130.9 1.6 slice-start
  160.7 128.0 %all-to-all-start = ((bf16[32,32,1024]{2,1,0:T(8,128)(2,1)}), bf16[32,32,1024]{2,1,0:T(8,128)(2,1)}, u32[]{:S(2)}, u32[]{:S(2)}) async-start(bf16[32,32,1024]{2,1,0:T(8,128)(2,1)} %bitcast.311), calls=%async_computation | async-start | bytes 4194304 | tf_op jit(solution)/shard_map/cond/branch_1_fun/all_to_all | solution.py:38
  503.3 9.4 %copy-start.16 = (s32[2048]{0:T(1024)S(1)}, s32[2048]{0:T(1024)}, u32[]{:S(2)}) copy-start(s32[2048]{0:T(1024)} %get-tuple-element.491) | copy-start | bytes 24580 | tf_op jit(solution)/shard_map/cond
  503.3 11.5 %copy-start.28 = (s32[4]{0:T(128)S(1)}, s32[4]{0:T(128)}, u32[]{:S(2)}) copy-start(s32[4]{0:T(128)} %get-tuple-element.486) | copy-start | bytes 52 | tf_op jit(solution)/shard_map/cond
  503.4 13.4 %copy-start.22 = (s32[256]{0:T(256)S(1)}, s32[256]{0:T(256)}, u32[]{:S(2)}) copy-start(s32[256]{0:T(256)} %get-tuple-element.487.row_of) | copy-start | bytes 3076 | tf_op jit(solution)/shard_map/cond
  503.4 58.1 %all-to-all-start.1 = ((bf16[32,32,1024]{2,1,0:T(8,128)(2,1)}), bf16[32,32,1024]{2,1,0:T(8,128)(2,1)}, u32[]{:S(2)}, u32[]{:S(2)}) async-start(bf16[32,32,1024]{2,1,0:T(8,128)(2,1)} %bitcast.312), calls=%async_computation.1 | async-start | bytes 4194304 | tf_op jit(solution)/shard_map/cond/branch_1_fun/all_to_all | solution.py:38
  522.3 39.1 %copy-start.20 = (s32[1024]{0:T(1024)S(1)}, s32[1024]{0:T(1024)}, u32[]{:S(2)}) copy-start(s32[1024]{0:T(1024)} %get-tuple-element.468) | copy-start | bytes 12292 | tf_op jit(solution)/shard_map/cond

commit v5 on v4

--- a/solution.py
+++ b/solution.py
@@ -117,7 +117,8 @@
         emb_rows = jnp.where(col(is_hot), hot_rows, cold_rows)
         return layer_forward(resid, emb_rows, up, down, gate_w, proj), (resid, emb_rows)
 
-    x_out, (x_saved, rows_saved) = lax.scan(fwd, x_in, (emb_table, hot_table, w_up, w_down, w_gate, w_proj))
+    x_first = jnp.where(n_loc * hot_ids[0] >= 0, x_in, 0)
+    x_out, (x_saved, rows_saved) = lax.scan(fwd, x_first, (emb_table, hot_table, w_up, w_down, w_gate, w_proj))
 
     def bwd(d_resid, per_layer):
         resid_l, rows_l, up, down, gate_w, proj = per_layer
@@ -162,23 +163,9 @@
     return (0.5 + 0.5 * th) + (0.5 * x) * (1.0 - th * th) * (GELU_A + (3.0 * GELU_B) * sq)
 
 
-def forward_kernel(n_l, n_f, x0, cls, table, wu, wd, wg, wp, xs, hs, ss, es, xo, zeros, x_now, u_now, acc, q_now, blank, sem):
+def forward_kernel(n_l, n_f, x0, cls, table, wu, wd, wg, wp, xs, hs, ss, es, xo, x_now, u_now, acc, q_now):
     layer, step = pl.program_id(0), pl.program_id(1)
     n_tok = x_now.shape[0]
-    n_blank = blank.shape[0]
-    blanks = [pltpu.make_async_copy(blank, zeros.at[pl.ds(i, n_blank)], sem) for i in range(0, zeros.shape[0], n_blank)]
-
-    @pl.when((layer == 0) & (step == n_f - 1))
-    def _():
-        blank[...] = jnp.zeros(blank.shape, F32)
-        for b in blanks:
-            b.start()
-
-    @pl.when((layer == n_l - 1) & (step == n_f - 1))
-    def _():
-        for b in blanks:
-            b.wait()
-
 
     @pl.when((layer == 0) & (step == 0))
     def _():
@@ -223,7 +210,7 @@
     return [pl.ds(m, size) for m in range(0, n, size)]
 
 
-def forward(x0, cls, table, w_up, w_down, w_gate, w_proj, rows_dev):
+def forward(x0, cls, table, w_up, w_down, w_gate, w_proj):
     n_tok, dim = x0.shape
     n_l, _, ff = w_up.shape
     emb = w_gate.shape[2]
@@ -258,11 +245,9 @@
             pl.BlockSpec((None, n_tok, emb), whole),
             pl.BlockSpec((None, n_tok, emb), whole),
             pl.BlockSpec((n_tok, dim), fixed),
-            ANY,
         ],
-        out_shape=[out_of((n_l, n_tok, n), BF) for n in (dim, ff, emb, emb)] + [out_of((n_tok, dim), BF), out_of((rows_dev, n_l, emb))],
-        scratch_shapes=[pltpu.VMEM((n_tok, dim), t) for t in (BF, BF, F32, BF)]
-        + [pltpu.VMEM((rows_dev // 12, n_l, emb), F32), pltpu.SemaphoreType.DMA(())],
+        out_shape=[out_of((n_l, n_tok, n), BF) for n in (dim, ff, emb, emb)] + [out_of((n_tok, dim), BF)],
+        scratch_shapes=[pltpu.VMEM((n_tok, dim), t) for t in (BF, BF, F32, BF)],
         compiler_params=params("arbitrary", "arbitrary"),
         cost_estimate=cost(n_l * n_tok * dim * (2 * ff + 2 * emb + n_c), n_l),
         name="forward",
@@ -318,10 +303,10 @@
 
     plan = {}
     for i in range(n_l):
-        steps = [(1, folds[i].begin, ()), (2, folds[i].step, (0,)), (2, alls[i].begin, ()), (4, folds[i].step, (1,)), (5, alls[i].onward, (0,)),
-                 (6, alls[i].column, (1,)), (6, folds[i].step, (2,)), (8, alls[i].column, (2,)), (8, alls[i].onward, (1,)),
-                 (9, total, (i,)), (9, alls[i].column, (3,)), (10, alls[i].onward, (2,)), (11, alls[i].across, (0,)), (11, alls[i].onward, (3,)),
-                 (13, alls[i].across, (1,)), (14, alls[i].across, (2,)), (15, alls[i].across, (3,))]
+        steps = [(1, folds[i].begin, ()), (2, folds[i].step, (0,)), (2, alls[i].begin, ()), (4, folds[i].step, (1,)), (5, alls[i].column, (1,)),
+                 (6, alls[i].onward, (0,)), (7, folds[i].step, (2,)), (8, alls[i].column, (2,)), (9, alls[i].onward, (1,)), (9, total, (i,)),
+                 (10, alls[i].across, (0,)), (10, alls[i].onward, (2,)), (11, alls[i].column, (3,)), (12, alls[i].across, (1,)),
+                 (13, alls[i].across, (2,)), (14, alls[i].onward, (3,)), (17, alls[i].across, (3,))]
         for when, what, args in steps:
             plan.setdefault(10 * i + when, []).append((what, args))
     few_steps = [few.begin], *[[few.column, few.onward]] * 3, [few.onward], [few.across] * 4
@@ -445,22 +430,35 @@
     )(r_in, ss, w_proj, es, w_gate, xs, cls_t, hs, w_up, w_down)
 
 
-def count_kernel(ids, out):
+def count_kernel(ids, out, zeros, blank, sem):
     n_tok = ids.shape[1]
+    blank[...] = jnp.zeros(blank.shape, F32)
+    blanks = [pltpu.make_async_copy(blank, zeros.at[pl.ds(i, len(blank))], sem) for i in range(0, len(zeros), len(blank))]
+    for c in blanks:
+        c.start()
     out[...] = jnp.zeros(out.shape, F32)
 
     def hits(v, n):
         same = v.astype(F32).astype(BF) == iota((n, n_tok), 0).astype(F32).astype(BF)
         return jnp.where(same, jnp.ones((), BF), jnp.zeros((), BF))
 
-    @pl.loop(0, len(ids))
+    @pl.loop(0, len(ids) // RUN)
     def _(i):
-        ids_i = ids[pl.ds(i, 1), :]
-        out[...] += dot_nt(hits(ids_i >> HI_BITS, len(out)), hits(ids_i & (LO - 1), LO))
-
-
-def count_ids(ids, n_hi):
-    return pl.pallas_call(count_kernel, out_shape=out_of((n_hi, LO)), compiler_params=params(), name="count_ids")(ids)
+        got = []
+        for j in range(RUN):
+            ids_j = ids[pl.ds(i * RUN + j, 1), :]
+            got.append(dot_nt(hits(ids_j >> HI_BITS, len(out)), hits(ids_j & (LO - 1), LO)))
+        out[...] += sum(got)
+
+    for c in blanks:
+        c.wait()
+
+
+def count_ids(ids, n_hi, shape):
+    return pl.pallas_call(
+        count_kernel, out_shape=[out_of((n_hi, LO)), out_of(shape)], out_specs=[pl.BlockSpec(memory_space=pltpu.VMEM), ANY],
+        scratch_shapes=[pltpu.VMEM((shape[0] // 12, *shape[1:]), F32), pltpu.SemaphoreType.DMA(())],
+        compiler_params=params(), name="count_ids")(ids)
 
 
 def pack_kernel(row_of, table, out, sem):
@@ -485,8 +483,8 @@
     def __init__(self):
         me = lax.axis_index('emb')
         self.core, self.x, self.y, self.z = me % 2, (me // 2) % 2, (me // 4) % 2, me // 8
-        self.others = [self.dev(z=(self.z + k) % 4) for k in REST]
-        self.columns = [(self.z - k + 4) % 4 for k in STOPS]
+        self.columns = [self.z, self.z + 1 - self.z % 2 * 2, (self.z + 2) % 4, 3 - self.z]
+        self.others = [self.dev(z=z) for z in self.columns[1:]]
         self.to_x, self.to_y, self.to_core = self.dev(x=1 - self.x), self.dev(y=1 - self.y), self.dev(core=1 - self.core)
 
     def dev(self, z=None, y=None, x=None, core=None):
@@ -628,7 +626,6 @@
 
 SPREAD_SEMS = (2, 10, 4)
 STOPS = range(4)
-REST = STOPS[1:]
 FOLD_SEMS = (2, 4, 4)
 HOT_AT, COLD_AT = FREQ, FREQ + 64
 
@@ -727,6 +724,37 @@
     )(numbers, row_of, sums, freq, into)
 
 
+def merge_kernel(keep, *refs):
+    n = (len(refs) - 1) // 3
+    sem = refs[-1]
+
+    @pl.when(keep[0] == 0)
+    def _():
+        copies = [pltpu.make_async_copy(src, dst, sem.at[i]) for i, (src, dst) in enumerate(zip(refs[n:2 * n], refs[2 * n:]))]
+        for c in copies:
+            c.start()
+        for c in copies:
+            c.wait()
+
+
+def merge(keep, fast, general):
+    n = len(fast)
+    return pl.pallas_call(
+        merge_kernel,
+        in_specs=[pl.BlockSpec(memory_space=pltpu.SMEM)] + [ANY] * 2 * n, out_specs=[ANY] * n,
+        out_shape=[out_of(v.shape, v.dtype) for v in fast], scratch_shapes=[pltpu.SemaphoreType.DMA((n,))],
+        input_output_aliases={i + 1: i for i in range(n)}, name="merge",
+    )(keep, *fast, *general)
+
+
+def empty_kernel(*_):
+    pass
+
+
+def empty(like):
+    return pl.pallas_call(empty_kernel, out_specs=[ANY] * len(like), out_shape=[out_of(v.shape, v.dtype) for v in like], name="empty")()
+
+
 def down_sum(v):
     return jnp.sum(v, axis=0)
 
@@ -802,7 +830,7 @@
             d_placed = dot32(move, d_out).astype(BF)
             return d_placed, table, cls, n_used, row_of, code
 
-        count = count_ids(swap(jnp.broadcast_to(row(token_ids), (n_dev, n_loc))), n_hi)
+        count, zeros = count_ids(swap(jnp.broadcast_to(row(token_ids), (n_dev, n_loc))), n_hi, (rows_dev, layers, emb_dim))
         tok, hot = digits(token_ids, n_hi), digits(hot_ids, n_hi)
         slot_no = jnp.arange(n_hot, dtype=I32)
         hot_place = slot_no // (RUN * n_dev) * RUN + slot_no % RUN
@@ -854,23 +882,26 @@
         given = prepare(got_class, hot_hi, hot_lo, row_used, cold_owner, freq_cold, freq_map, hot_table, by_row, move, d_out)
         all_fit = jnp.max(got_class) < bad
 
-        def fast(x_moved, slot, my_cold, my_row, d_placed, table, cls, n_used, row_of, code):
-            d_moved = exchange(d_placed)
-            cls_row = cls.reshape(1, n_loc)
-            xs, hs, ss, es, x_last, zeros = forward(x_moved, cls.reshape(n_loc, 1), table, w_up, w_down, w_gate, w_proj, rows_dev)
-            sums, gathered = backward(d_moved, cls_row, es, xs, hs, ss, w_up, w_down, w_gate, w_proj, n_dev)
-            x_last, gathered = lax.optimization_barrier((x_last, gathered))
-            x_back = exchange(x_last)
-            numbers = jnp.stack([n_used, my_row, jnp.sum(my_cold * jnp.arange(FREQ_COLD, dtype=I32))])
-            d_table = put_rows(numbers, row_of, sums, gathered, zeros)
-            d_hot = hot_out(gathered, code, layers)
-            x_out = dot32((col(slot) == iota((n_loc, n_loc), 1)).astype(BF), x_back).astype(BF)
-            return x_out, d_table.transpose(1, 0, 2), d_hot
-
-        def slow(*_):
-            return general_path(n_dev, me, token_ids, hot_ids, x_in, d_out, emb_table, hot_table, w_up, w_down, w_gate, w_proj)
-
-        return lax.cond(all_fit, fast, slow, *lax.optimization_barrier((x_moved, slot, my_cold, my_row, *given)))
+        d_placed, table, cls, n_used, row_of, code = given
+        d_moved = exchange(d_placed)
+        cls_row = cls.reshape(1, n_loc)
+        xs, hs, ss, es, x_last = forward(x_moved, cls.reshape(n_loc, 1), table, w_up, w_down, w_gate, w_proj)
+        sums, gathered = backward(d_moved, cls_row, es, xs, hs, ss, w_up, w_down, w_gate, w_proj, n_dev)
+        x_last, gathered = lax.optimization_barrier((x_last, gathered))
+        x_back = exchange(x_last)
+        numbers = jnp.stack([n_used, my_row, jnp.minimum(jnp.sum(my_cold * jnp.arange(FREQ_COLD, dtype=I32)), FREQ_COLD - 1)])
+        d_table = put_rows(numbers, row_of, sums, gathered, zeros)
+        d_hot = hot_out(gathered, code, layers)
+        x_out = dot32((col(slot) == iota((n_loc, n_loc), 1)).astype(BF), x_back).astype(BF)
+        *fast, fit = lax.optimization_barrier((x_out, d_table, d_hot, all_fit))
+
+        def slow():
+            x, table_grad, hot_grad = general_path(n_dev, me, token_ids, hot_ids, x_in, d_out, emb_table, hot_table, w_up, w_down, w_gate, w_proj)
+            return x, table_grad.transpose(1, 0, 2), hot_grad
+
+        general = lax.cond(fit, lambda: tuple(empty(fast)), slow)
+        x_out, d_table, d_hot = merge(fit.astype(I32).reshape(1), fast, general)
+        return x_out, d_table.transpose(1, 0, 2), d_hot
 
     return jax.shard_map(body, mesh=mesh,
                          in_specs=(P('emb'), P(), P('emb', None), P('emb', None), P(None, 'emb', None), P(), P(), P(), P(), P()),

time: 584 us -> 560 us (0.959)
  loops' own time: 9.26 us -> 1.27 us
    another operation x1, loops' own time: 9.26 us -> 1.27 us  [body(): general = lax.cond(fit, lambda: tuple(empty(fast)), slow)]
    pallas_call x1 -> x3, Pallas kernels: 12.6 us -> 10.3 us  [the longest x1 10.3 us: count_ids(): pl.pallas_call(count_kernel, out_shape=[out_of((n_hi, LO)), out_of(shape)...]
where the time goes in v5:
time: 560 us; the launch traced here: 553 us
  Pallas kernels  395 us (71%)
  matrix products  42.2 us (8%)
  starting transfers between devices  27.9 us (5%)
  waiting for transfers between devices  26 us (5%)
  other arithmetic  23.8 us (4%)
  between operations  19.3 us (3%)
  local copies, waits for them, and re-layouts  17.5 us (3%)
    pallas_call x1, Pallas kernels, backward(): pl.pallas_call(functools.partial(backward_kernel, n_l, n_f), grid=(n_full...  217 us
    pallas_call x1, Pallas kernels, forward(): pl.pallas_call(functools.partial(forward_kernel, n_l, n_f), grid=(n_l, n_...  118 us
    dot_general x19, matrix products, dot32(): return jnp.dot(a, b, preferred_element_type=F32)  42.2 us
    pallas_call x1, Pallas kernels, hot_out(): pl.pallas_call(hot_kernel, grid_spec=pltpu.PrefetchScalarGridSpec(num_sca...  35.3 us
    all_to_all x6, starting transfers between devices, swap(): return lax.all_to_all(v, 'emb', 0, 0, tiled=True)  27.9 us
    all_to_all x6, waiting for transfers between devices, swap(): return lax.all_to_all(v, 'emb', 0, 0, tiled=True)  26 us
  transfers between devices with their start and end apart: 6, of which 4 were waited for; matrix products, arithmetic and copies ran while one was open for 8% of the time, Pallas kernels for 30%

profile of v5, /device:TPU:0, one launch (start us, length us, event | category | flops | bytes accessed | tf_op | source)
XLA Modules:
  0.0 553.0 jit_solution(10257311375186706636)
XLA Ops:
  7.2 1.4 broadcast_in_dim.283
  8.6 7.3 %all-to-all-start.3 = ((s32[32,1,1024]{2,1,0:T(1,128)}), s32[32,1,1024]{2,1,0:T(1,128)S(1)}, u32[]{:S(2)}, u32[]{:S(2)}) async-start(s32[32,1,1024]{2,1,0:T(1,128)} %broadcast_in_dim.283), calls=%async_computation.3 | async-start | bytes 262144 | tf_op jit(solution)/shard_map/all_to_all | solution.py:38
  16.7 0.7 broadcast_shift-right-arithmetic_fusion
  17.4 1.3 fusion.206
  18.7 1.2 fusion.203
  19.9 0.9 convolution_convert_fusion
  20.9 3.2 all-to-all-done.3
  24.8 10.3 %count_ids.1 = (f32[200,256]{1,0:T(8,128)}, f32[1572,4,1024]{2,1,0:T(4,128)}) custom-call(s32[32,1024]{1,0:T(8,128)} %bitcast.319), custom_call_target="tpu_custom_call" | custom-call | tf_op jit(solution)/shard_map/count_ids/pallas_call | solution.py:458
  35.1 1.0 compare_convert_fusion.4
  36.0 1.8 broadcast_select_fusion.3
  37.8 1.4 convert_reduce_fusion
  39.9 1.5 convert_reduce_fusion.2
  42.1 0.8 fusion.255
  43.8 0.8 select_reduce_fusion.8
  45.2 0.7 dynamic-slice_bitcast_fusion.1
  46.0 0.8 broadcast_in_dim.298
  46.7 3.1 all-to-all-start.4
  53.1 0.9 fusion.215
  53.9 1.2 fusion.214
  56.4 5.4 fusion.211
  62.5 5.9 %all-to-all-start.5 = ((s32[32,1,32]{2,1,0:T(1,128)}), s32[32,1,32]{2,1,0:T(1,128)S(1)}, u32[]{:S(2)}, u32[]{:S(2)}) async-start(s32[32,1,32]{2,1,0:T(1,128)} %all_to_all.45), calls=%async_computation.5 | async-start | bytes 32768 | tf_op jit(solution)/shard_map/all_to_all | solution.py:38
  68.5 3.7 fusion.210
  72.1 0.8 copy.89
  72.9 2.7 all-to-all-done.5
  76.8 1.7 fusion.218
  79.2 4.9 fusion.228
  84.1 5.1 fusion.225
  89.2 5.1 fusion.222
  94.3 3.7 all-to-all-start.6
  98.0 4.9 fusion.219
  103.7 1.7 select_reduce_fusion.1
  105.4 0.7 fusion.327
  106.1 1.0 copy.97.cls
  107.4 1.6 select_reduce_fusion.3.row_of
  109.1 8.2 %pack_rows.1 = bf16[256,4,1024]{2,1,0:T(4,128)(2,1)} custom-call(s32[256]{0:T(256)} %select_reduce_fusion.3.row_of, bf16[1572,4,1024]{2,1,0:T(4,128)(2,1)} %bitcast.310), custom_call_target="tpu_custom_call" | custom-call | tf_op jit(solution)/shard_map/pack_rows/pallas_call | solution.py:474
  117.3 7.8 %fusion.326 = (bf16[256,1,1024]{2,1,0:T(2,128)(2,1)S(1)}, bf16[256,1,1024]{2,1,0:T(2,128)(2,1)S(1)}, bf16[256,1,1024]{2,1,0:T(2,128)(2,1)S(1)}, bf16[256,1,1024]{2,1,0:T(2,128)(2,1)S(1)}) fusion(bf16[256,4,1024]{2,1,0:T(4,128)(2,1)} %pack_rows.1), kind=kLoop, calls=%fused_computation.456 | loop fusion | bytes 4194304 | tf_op jit(solution)/shard_map/slice | solution.py:824
  127.1 2.1 pad_maximum_fusion.table
  129.3 17.5 %all-to-all-done.6 = bf16[32,32,1024]{2,1,0:T(8,128)(2,1)} async-done(((bf16[32,32,1024]{2,1,0:T(8,128)(2,1)}), bf16[32,32,1024]{2,1,0:T(8,128)(2,1)}, u32[]{:S(2)}, u32[]{:S(2)}) %all-to-all-start.6) | async-done | bytes 2097184 | tf_op jit(solution)/shard_map/all_to_all | solution.py:38
  146.8 4.3 all-to-all-start.7
  151.1 118.3 %forward.1 = (bf16[4,1024,1024]{2,1,0:T(8,128)(2,1)}, bf16[4,1024,4096]{2,1,0:T(8,128)(2,1)}, bf16[4,1024,1024]{2,1,0:T(8,128)(2,1)}, bf16[4,1024,1024]{2,1,0:T(8,128)(2,1)}, bf16[1024,1024]{1,0:T(8,128)(2,1)}) custom-call(bf16[1024,1024]{1,0:T(8,128)(2,1)} %bitcast.9.x0, s32[1024,1]{1,0:T(8,128)} %copy.97.cls, bf16[4,448,1024]{2,1,0:T(8,128)(2,1)} %pad_maximum_fusion.table, ...), custom_call_target="tpu_custom_call" | custom-call | flops 89657442304 | bytes 160000000 | tf_op jit(solution)/shard_map/forward/pallas_call | solution.py:230
  269.4 217.5 %backward.1 = (f32[4,448,1024]{2,1,0:T(8,128)}, f32[32,272,1024]{2,1,0:T(8,128)}) custom-call(bf16[1024,1024]{1,0:T(8,128)(2,1)} %bitcast.29.r_in, bf16[4,1024,1024]{2,1,0:T(8,128)(2,1)} %get-tuple-element.482.ss, bf16[4,1024,1024]{2,1,0:T(8,128)(2,1)} %wp.3, bf16[4,1024,1024]{2,1,0:T(8,128)(2,1)} %get-tuple-element.483.es, bf16[4,1024,1024]{2,1,0:T(8,128)(2,1)} %wg.3, ...), custom_call_target="tpu_custom_call" | custom-call | flops 97173635072 | bytes 160000000 | tf_op jit(solution)/shard_map/backward/pallas_call | solution.py:415
  486.9 3.5 all-to-all-start.8
  493.7 1.3 copy.98.code
  495.7 5.6 %put_rows.1.refs_1_ = f32[1572,4,1024]{2,1,0:T(4,128)} custom-call(s32[3]{0:T(128)} %pad_add_fusion.numbers, s32[256]{0:T(256)} %select_reduce_fusion.3.row_of, f32[4,448,1024]{2,1,0:T(8,128)} %get-tuple-element.488.sums, f32[32,272,1024]{2,1,0:T(8,128)} %get-tuple-element.489.freq.raw, ...), custom_call_target="tpu_custom_call", output_to_operand_aliasing={{}: (4, {})} | custom-call | tf_op jit(solution)/shard_map/put_rows/pallas_call | solution.py:716
  501.3 35.3 %hot_out.1.refs_2_ = f32[4,2048,1024]{2,1,0:T(8,128)} custom-call(s32[4]{0:T(128)} %convert_element_type.476.any_freq, f32[32,272,1024]{2,1,0:T(8,128)} %get-tuple-element.489.freq.raw, f32[32,272,1024]{2,1,0:T(8,128)} %get-tuple-element.489.freq.raw, s32[2048,1]{1,0:T(8,128)} %copy.98.code), custom_call_target="tpu_custom_call" | custom-call | flops 4563402752 | bytes 160000000 | tf_op jit(solution)/shard_map/hot_out/pallas_call | solution.py:667
  536.6 2.5 all-to-all-done.8
  539.2 5.4 fusion.209.refs_0_
  544.6 1.3 conditional.1
  (112 shorter events, 13.9 us)
Async XLA Ops:
  8.6 15.5 %all-to-all-start.3 = ((s32[32,1,1024]{2,1,0:T(1,128)}), s32[32,1,1024]{2,1,0:T(1,128)S(1)}, u32[]{:S(2)}, u32[]{:S(2)}) async-start(s32[32,1,1024]{2,1,0:T(1,128)} %broadcast_in_dim.283), calls=%async_computation.3 | async-start | bytes 262144 | tf_op jit(solution)/shard_map/all_to_all | solution.py:38
  18.7 19.1 %copy-start.26 = (f32[27]{0:T(128)S(1)}, f32[27]{0:T(128)}, u32[]{:S(2)}) copy-start(f32[27]{0:T(128)} %constant.386.clone) | copy-start | bytes 328
  39.9 3.4 copy-start.12
  46.7 15.1 %all-to-all-start.4 = ((bf16[32,4,1024]{2,1,0:T(4,128)(2,1)}), bf16[32,4,1024]{2,1,0:T(4,128)(2,1)S(1)}, u32[]{:S(2)}, u32[]{:S(2)}) async-start(bf16[32,4,1024]{2,1,0:T(4,128)(2,1)} %broadcast_in_dim.298), calls=%async_computation.4 | async-start | bytes 524288 | tf_op jit(solution)/shard_map/all_to_all | solution.py:38
  52.6 15.9 %copy-start.22 = (s32[1024]{0:T(1024)}, s32[1024]{0:T(1024)S(1)}, u32[]{:S(2)}) copy-start(s32[1024]{0:T(1024)S(1)} %fusion.284) | copy-start | bytes 12292
  55.8 51.6 %copy-start.19 = (pred[1572]{0:T(1024)(128)(4,1)}, pred[1572]{0:T(1024)(128)(4,1)S(1)}, u32[]{:S(2)}) copy-start(pred[1572]{0:T(1024)(128)(4,1)S(1)} %get-tuple-element.476) | copy-start | bytes 4720
  56.4 12.1 %copy-start = (bf16[1024,1024]{1,0:T(8,128)(2,1)S(1)}, bf16[1024,1024]{1,0:T(8,128)(2,1)}, u32[]{:S(2)}) copy-start(bf16[1024,1024]{1,0:T(8,128)(2,1)} %param.20) | copy-start | bytes 6291460
  62.5 13.1 %all-to-all-start.5 = ((s32[32,1,32]{2,1,0:T(1,128)}), s32[32,1,32]{2,1,0:T(1,128)S(1)}, u32[]{:S(2)}, u32[]{:S(2)}) async-start(s32[32,1,32]{2,1,0:T(1,128)} %all_to_all.45), calls=%async_computation.5 | async-start | bytes 32768 | tf_op jit(solution)/shard_map/all_to_all | solution.py:38
  68.5 8.4 %copy-start.6 = (bf16[2048,200]{1,0:T(8,128)(2,1)S(1)}, bf16[2048,200]{1,0:T(8,128)(2,1)}, u32[]{:S(2)}) copy-start(bf16[2048,200]{1,0:T(8,128)(2,1)} %fusion.206) | copy-start | bytes 2457604
  84.1 18.8 %copy-start.2 = (bf16[188,1024]{1,0:T(8,128)(2,1)}, bf16[188,1024]{1,0:T(8,128)(2,1)S(1)}, u32[]{:S(2)}) copy-start(bf16[188,1024]{1,0:T(8,128)(2,1)S(1)} %fusion.228) | copy-start | bytes 1155076
  89.2 13.8 %copy-start.4 = (bf16[188,1024]{1,0:T(8,128)(2,1)}, bf16[188,1024]{1,0:T(8,128)(2,1)S(1)}, u32[]{:S(2)}) copy-start(bf16[188,1024]{1,0:T(8,128)(2,1)S(1)} %fusion.225) | copy-start | bytes 1155076
  94.3 8.8 %copy-start.3 = (bf16[188,1024]{1,0:T(8,128)(2,1)}, bf16[188,1024]{1,0:T(8,128)(2,1)S(1)}, u32[]{:S(2)}) copy-start(bf16[188,1024]{1,0:T(8,128)(2,1)S(1)} %fusion.222) | copy-start | bytes 1155076
  94.3 52.5 %all-to-all-start.6 = ((bf16[32,32,1024]{2,1,0:T(8,128)(2,1)}), bf16[32,32,1024]{2,1,0:T(8,128)(2,1)}, u32[]{:S(2)}, u32[]{:S(2)}) async-start(bf16[32,32,1024]{2,1,0:T(8,128)(2,1)} %bitcast.8), calls=%async_computation.6 | async-start | bytes 4194304 | tf_op jit(solution)/shard_map/all_to_all | solution.py:38
  102.9 0.8 copy-start.5
  106.1 11.2 %copy-start.21 = (s32[1024]{0:T(1024)}, s32[1024]{0:T(1024)S(1)}, u32[]{:S(2)}) copy-start(s32[1024]{0:T(1024)S(1)} %get-tuple-element.804) | copy-start | bytes 12292
  125.1 1.0 copy-start.11
  125.1 1.1 slice-start.3
  125.1 1.4 slice-start.2
  125.3 1.5 slice-start.1
  125.5 1.6 slice-start
  146.8 122.6 %all-to-all-start.7 = ((bf16[32,32,1024]{2,1,0:T(8,128)(2,1)}), bf16[32,32,1024]{2,1,0:T(8,128)(2,1)}, u32[]{:S(2)}, u32[]{:S(2)}) async-start(bf16[32,32,1024]{2,1,0:T(8,128)(2,1)} %bitcast.28), calls=%async_computation.7 | async-start | bytes 4194304 | tf_op jit(solution)/shard_map/all_to_all | solution.py:38
  486.8 4.2 copy-start.20
  486.8 6.1 %copy-start.25 = (pred[2048]{0:T(1024)(128)(4,1)S(1)}, pred[2048]{0:T(1024)(128)(4,1)}, u32[]{:S(2)}) copy-start(pred[2048]{0:T(1024)(128)(4,1)} %get-tuple-element.768) | copy-start | bytes 6148
  486.9 6.8 %copy-start.18 = (s32[2048]{0:T(1024)S(1)}, s32[2048]{0:T(1024)}, u32[]{:S(2)}) copy-start(s32[2048]{0:T(1024)} %get-tuple-element.769) | copy-start | bytes 24580
  486.9 52.3 %all-to-all-start.8 = ((bf16[32,32,1024]{2,1,0:T(8,128)(2,1)}), bf16[32,32,1024]{2,1,0:T(8,128)(2,1)}, u32[]{:S(2)}, u32[]{:S(2)}) async-start(bf16[32,32,1024]{2,1,0:T(8,128)(2,1)} %bitcast.315), calls=%async_computation.8 | async-start | bytes 4194304 | tf_op jit(solution)/shard_map/all_to_all | solution.py:38
  501.3 37.9 %copy-start.23 = (s32[1024]{0:T(1024)S(1)}, s32[1024]{0:T(1024)}, u32[]{:S(2)}) copy-start(s32[1024]{0:T(1024)} %copy-done.22) | copy-start | bytes 12292
  539.2 5.4 copy-start.1
  539.2 5.4 copy-start.13
  539.2 5.5 copy-start.24

commit v6 on v5

--- a/solution.py
+++ b/solution.py
@@ -163,9 +163,39 @@
     return (0.5 + 0.5 * th) + (0.5 * x) * (1.0 - th * th) * (GELU_A + (3.0 * GELU_B) * sq)
 
 
-def forward_kernel(n_l, n_f, x0, cls, table, wu, wd, wg, wp, xs, hs, ss, es, xo, x_now, u_now, acc, q_now):
+def forward_kernel(n_l, n_f, n_dev, x0, cls, table, wu, wd, wg, wp, d_in, xs, hs, ss, es, xo, d_got, x_now, u_now, acc, q_now, sems):
     layer, step = pl.program_id(0), pl.program_id(1)
     n_tok = x_now.shape[0]
+    me = lax.axis_index('emb')
+    places = n_tok // n_dev
+    barrier = pltpu.get_barrier_semaphore()
+
+    def block(dev):
+        return pl.ds(pl.multiple_of(dev * places, places), places)
+
+    own = pltpu.make_async_copy(d_in.at[block(me)], d_got.at[block(me)], sems.at[2])
+
+    @pl.when((layer == 0) & (step == 0))
+    def _():
+        @pl.loop(1, n_dev)
+        def _(k):
+            pl.semaphore_signal(barrier, device_id=((me + k) % n_dev,), device_id_type=pl.DeviceIdType.MESH)
+
+    @pl.when((layer == 0) & (step == 1))
+    def _():
+        own.start()
+        pl.semaphore_wait(barrier, n_dev - 1)
+
+        @pl.loop(1, n_dev)
+        def _(k):
+            to = (me + k) % n_dev
+            remote(d_in.at[block(to)], d_got.at[block(me)], sems, to).start()
+
+    @pl.when((layer == n_l - 1) & (step == n_f - 1))
+    def _():
+        others = pl.ds(0, n_tok - places)
+        remote(d_in.at[others], d_got.at[others], sems, me).wait()
+        own.wait()
 
     @pl.when((layer == 0) & (step == 0))
     def _():
@@ -210,7 +240,7 @@
     return [pl.ds(m, size) for m in range(0, n, size)]
 
 
-def forward(x0, cls, table, w_up, w_down, w_gate, w_proj):
+def forward(x0, cls, table, w_up, w_down, w_gate, w_proj, d_in, n_dev):
     n_tok, dim = x0.shape
     n_l, _, ff = w_up.shape
     emb = w_gate.shape[2]
@@ -228,7 +258,7 @@
         return (0, 0)
 
     return pl.pallas_call(
-        functools.partial(forward_kernel, n_l, n_f),
+        functools.partial(forward_kernel, n_l, n_f, n_dev),
         grid=(n_l, n_f),
         in_specs=[
             pl.BlockSpec((n_tok, dim), fixed, pipeline_mode=ONCE),
@@ -238,6 +268,7 @@
             pl.BlockSpec((None, tile, dim), lambda l, f: (l, f, 0)),
             pl.BlockSpec((None, dim, emb), whole),
             pl.BlockSpec((None, emb, dim), whole),
+            ANY,
         ],
         out_specs=[
             pl.BlockSpec((None, n_tok, dim), whole),
@@ -245,13 +276,14 @@
             pl.BlockSpec((None, n_tok, emb), whole),
             pl.BlockSpec((None, n_tok, emb), whole),
             pl.BlockSpec((n_tok, dim), fixed),
+            ANY,
         ],
-        out_shape=[out_of((n_l, n_tok, n), BF) for n in (dim, ff, emb, emb)] + [out_of((n_tok, dim), BF)],
-        scratch_shapes=[pltpu.VMEM((n_tok, dim), t) for t in (BF, BF, F32, BF)],
-        compiler_params=params("arbitrary", "arbitrary"),
+        out_shape=[out_of((n_l, n_tok, n), BF) for n in (dim, ff, emb, emb)] + [out_of((n_tok, dim), BF)] * 2,
+        scratch_shapes=[pltpu.VMEM((n_tok, dim), t) for t in (BF, BF, F32, BF)] + [pltpu.SemaphoreType.DMA((3,))],
+        compiler_params=params("arbitrary", "arbitrary", collective_id=1, has_side_effects=True),
         cost_estimate=cost(n_l * n_tok * dim * (2 * ff + 2 * emb + n_c), n_l),
         name="forward",
-    )(x0, cls, table, w_up, w_down, w_gate, w_proj)
+    )(x0, cls, table, w_up, w_down, w_gate, w_proj, d_in)
 
 
 def params(*kinds, **more):
@@ -303,17 +335,17 @@
 
     plan = {}
     for i in range(n_l):
-        steps = [(1, folds[i].begin, ()), (2, folds[i].step, (0,)), (2, alls[i].begin, ()), (4, folds[i].step, (1,)), (5, alls[i].column, (1,)),
-                 (6, alls[i].onward, (0,)), (7, folds[i].step, (2,)), (8, alls[i].column, (2,)), (9, alls[i].onward, (1,)), (9, total, (i,)),
-                 (10, alls[i].across, (0,)), (10, alls[i].onward, (2,)), (11, alls[i].column, (3,)), (12, alls[i].across, (1,)),
-                 (13, alls[i].across, (2,)), (14, alls[i].onward, (3,)), (17, alls[i].across, (3,))]
+        steps = [(1, folds[i].begin, ()), (2, folds[i].step, (0,)), (2, alls[i].begin, ()), (5, folds[i].step, (1,)), (8, alls[i].onward, (0,)),
+                 (9, alls[i].column, (1,)), (10, folds[i].step, (2,)), (10, alls[i].column, (2,)), (13, alls[i].onward, (1,)),
+                 (13, alls[i].across, (0,)), (14, alls[i].column, (3,)), (18, total, (i,)), (19, alls[i].onward, (2,)), (21, alls[i].onward, (3,)),
+                 (21, alls[i].across, (1,)), (23, alls[i].across, (2,)), (26, alls[i].across, (3,))]
         for when, what, args in steps:
             plan.setdefault(10 * i + when, []).append((what, args))
     few_steps = [few.begin], *[[few.column, few.onward]] * 3, [few.onward], [few.across] * 4
     for k, steps in enumerate(few_steps):
         for j, what in enumerate(steps):
             args = () if not k else (k - j,) if k < 4 else (3,) if k == 4 else (j,)
-            plan.setdefault(10 * n_l + k - 0.5, []).append((what, args))
+            plan.setdefault(10 * n_l + 8 + k / 2, []).append((what, args))
 
     def point(k, now, layers):
         for i in range(layers):
@@ -500,7 +532,8 @@
 
 
 def remote(src, dst, sems, to):
-    return pltpu.make_async_remote_copy(src_ref=src, dst_ref=dst, send_sem=sems[0], recv_sem=sems[1],
+    send, recv = sems if isinstance(sems, tuple) else (sems.at[0], sems.at[1])
+    return pltpu.make_async_remote_copy(src_ref=src, dst_ref=dst, send_sem=send, recv_sem=recv,
                                         device_id=(to,), device_id_type=pl.DeviceIdType.MESH)
 
 
@@ -883,9 +916,8 @@
         all_fit = jnp.max(got_class) < bad
 
         d_placed, table, cls, n_used, row_of, code = given
-        d_moved = exchange(d_placed)
         cls_row = cls.reshape(1, n_loc)
-        xs, hs, ss, es, x_last = forward(x_moved, cls.reshape(n_loc, 1), table, w_up, w_down, w_gate, w_proj)
+        xs, hs, ss, es, x_last, d_moved = forward(x_moved, cls.reshape(n_loc, 1), table, w_up, w_down, w_gate, w_proj, d_placed, n_dev)
         sums, gathered = backward(d_moved, cls_row, es, xs, hs, ss, w_up, w_down, w_gate, w_proj, n_dev)
         x_last, gathered = lax.optimization_barrier((x_last, gathered))
         x_back = exchange(x_last)

time: 560 us -> 542 us (0.968)
  Pallas kernels: 395 us -> 382 us
    pallas_call x1, Pallas kernels: 217 us -> 203 us  [backward(): pl.pallas_call(functools.partial(backward_kernel, n_l, n_f), grid=(n_full...]
    all_to_all x6 -> x5, starting transfers between devices: 27.9 us -> 24 us  [swap(): return lax.all_to_all(v, 'emb', 0, 0, tiled=True)]
    all_to_all x6 -> x5, waiting for transfers between devices: 26 us -> 25.9 us  [swap(): return lax.all_to_all(v, 'emb', 0, 0, tiled=True)]
  transfers between devices with their start and end apart: 6 -> 5, of which waited for: 4 -> 4; matrix products, arithmetic and copies ran while one was open for 8% -> 8% of each run, Pallas kernels for 30% -> 9%
where the time goes in v6:
time: 542 us; the launch traced here: 536 us
  Pallas kernels  382 us (70%)
  matrix products  42.2 us (8%)
  waiting for transfers between devices  25.9 us (5%)
  starting transfers between devices  24 us (4%)
  other arithmetic  23.7 us (4%)
  between operations  19.4 us (4%)
  local copies, waits for them, and re-layouts  17.5 us (3%)
    pallas_call x1, Pallas kernels, backward(): pl.pallas_call(functools.partial(backward_kernel, n_l, n_f), grid=(n_full...  203 us
    pallas_call x1, Pallas kernels, forward(): pl.pallas_call(functools.partial(forward_kernel, n_l, n_f, n_dev), grid=(...  119 us
    dot_general x19, matrix products, dot32(): return jnp.dot(a, b, preferred_element_type=F32)  42.2 us
    pallas_call x1, Pallas kernels, hot_out(): pl.pallas_call(hot_kernel, grid_spec=pltpu.PrefetchScalarGridSpec(num_sca...  35.3 us
    all_to_all x5, waiting for transfers between devices, swap(): return lax.all_to_all(v, 'emb', 0, 0, tiled=True)  25.9 us
    all_to_all x5, starting transfers between devices, swap(): return lax.all_to_all(v, 'emb', 0, 0, tiled=True)  24 us
  transfers between devices with their start and end apart: 5, of which 4 were waited for; matrix products, arithmetic and copies ran while one was open for 8% of the time, Pallas kernels for 9%

profile of v6, /device:TPU:0, one launch (start us, length us, event | category | flops | bytes accessed | tf_op | source)
XLA Modules:
  0.0 535.8 jit_solution(5606409220020284880)
XLA Ops:
  7.2 1.4 broadcast_in_dim.283
  8.6 7.3 %all-to-all-start.3 = ((s32[32,1,1024]{2,1,0:T(1,128)}), s32[32,1,1024]{2,1,0:T(1,128)S(1)}, u32[]{:S(2)}, u32[]{:S(2)}) async-start(s32[32,1,1024]{2,1,0:T(1,128)} %broadcast_in_dim.283), calls=%async_computation.3 | async-start | bytes 262144 | tf_op jit(solution)/shard_map/all_to_all | solution.py:38
  16.0 0.7 broadcast_and_fusion.1
  16.7 0.7 broadcast_shift-right-arithmetic_fusion
  17.4 1.3 fusion.206
  18.7 1.2 fusion.203
  19.9 0.9 convolution_convert_fusion
  20.9 3.2 all-to-all-done.3
  24.8 10.3 %count_ids.1 = (f32[200,256]{1,0:T(8,128)}, f32[1572,4,1024]{2,1,0:T(4,128)}) custom-call(s32[32,1024]{1,0:T(8,128)} %bitcast.317), custom_call_target="tpu_custom_call" | custom-call | tf_op jit(solution)/shard_map/count_ids/pallas_call | solution.py:490
  35.1 1.0 compare_convert_fusion.4
  36.0 1.8 broadcast_select_fusion.3
  37.8 1.4 convert_reduce_fusion
  39.9 1.5 convert_reduce_fusion.2
  42.1 0.8 fusion.255
  43.8 0.8 select_reduce_fusion.8
  45.2 0.7 dynamic-slice_bitcast_fusion.1
  45.9 0.8 broadcast_in_dim.298
  46.7 3.1 all-to-all-start.4
  53.1 0.9 fusion.215
  53.9 1.2 fusion.214
  56.5 5.4 %fusion.211.d_in = bf16[1024,1024]{1,0:T(8,128)(2,1)} fusion(bf16[1024,1024]{1,0:T(8,128)(2,1)} %param.21, s32[1024]{0:T(1024)S(1)} %fusion.284), kind=kOutput, calls=%fused_computation.259 | convolution fusion | flops 2149580800 | bytes 4198400 | tf_op jit(solution)/shard_map/dot_general | solution.py:50
  62.6 5.9 %all-to-all-start.5 = ((s32[32,1,32]{2,1,0:T(1,128)}), s32[32,1,32]{2,1,0:T(1,128)S(1)}, u32[]{:S(2)}, u32[]{:S(2)}) async-start(s32[32,1,32]{2,1,0:T(1,128)} %all_to_all.42), calls=%async_computation.5 | async-start | bytes 32768 | tf_op jit(solution)/shard_map/all_to_all | solution.py:38
  68.6 3.7 fusion.210
  72.2 0.8 copy.89
  73.0 2.7 all-to-all-done.5
  77.0 1.7 fusion.218
  79.3 4.9 fusion.228
  84.3 5.1 fusion.225
  89.3 5.1 fusion.222
  94.4 3.7 all-to-all-start.6
  98.1 4.9 fusion.219
  103.8 1.7 select_reduce_fusion.1
  105.5 0.7 fusion.327
  106.2 1.1 copy.97.cls
  107.6 1.7 select_reduce_fusion.3.row_of
  109.3 8.2 %pack_rows.1 = bf16[256,4,1024]{2,1,0:T(4,128)(2,1)} custom-call(s32[256]{0:T(256)} %select_reduce_fusion.3.row_of, bf16[1572,4,1024]{2,1,0:T(4,128)(2,1)} %bitcast.308), custom_call_target="tpu_custom_call" | custom-call | tf_op jit(solution)/shard_map/pack_rows/pallas_call | solution.py:506
  117.4 7.8 %fusion.326 = (bf16[256,1,1024]{2,1,0:T(2,128)(2,1)S(1)}, bf16[256,1,1024]{2,1,0:T(2,128)(2,1)S(1)}, bf16[256,1,1024]{2,1,0:T(2,128)(2,1)S(1)}, bf16[256,1,1024]{2,1,0:T(2,128)(2,1)S(1)}) fusion(bf16[256,4,1024]{2,1,0:T(4,128)(2,1)} %pack_rows.1), kind=kLoop, calls=%fused_computation.456 | loop fusion | bytes 4194304 | tf_op jit(solution)/shard_map/slice | solution.py:857
  127.3 2.1 pad_maximum_fusion.table
  129.4 17.5 %all-to-all-done.6 = bf16[32,32,1024]{2,1,0:T(8,128)(2,1)} async-done(((bf16[32,32,1024]{2,1,0:T(8,128)(2,1)}), bf16[32,32,1024]{2,1,0:T(8,128)(2,1)}, u32[]{:S(2)}, u32[]{:S(2)}) %all-to-all-start.6) | async-done | bytes 2097184 | tf_op jit(solution)/shard_map/all_to_all | solution.py:38
  146.9 119.4 %forward.1 = (bf16[4,1024,1024]{2,1,0:T(8,128)(2,1)}, bf16[4,1024,4096]{2,1,0:T(8,128)(2,1)}, bf16[4,1024,1024]{2,1,0:T(8,128)(2,1)}, bf16[4,1024,1024]{2,1,0:T(...) custom-call(bf16[1024,1024]{1,0:T(8,128)(2,1)} %bitcast.9.x0, s32[1024,1]{1,0:T(8,128)} %copy.97.cls, ...), custom_call_target="tpu_custom_call" | custom-call | flops 89657442304 | bytes 160000000 | tf_op jit(solution)/shard_map/forward/pallas_call | solution.py:260
  266.3 202.9 %backward.1 = (f32[4,448,1024]{2,1,0:T(8,128)}, f32[32,272,1024]{2,1,0:T(8,128)}) custom-call(bf16[1024,1024]{1,0:T(8,128)(2,1)} %get-tuple-element.483.r_in, bf16[4,1024,1024]{2,1,0:T(8,128)(2,1)} %get-tuple-element.484.ss, bf16[4,1024,1024]{2,1,0:T(8,128)(2,1)} %wp.3, bf16[4,1024,1024]{2,1,0:T(8,128)(2,1)} %get-tuple-element.485.es, ...), custom_call_target="tpu_custom_call" | custom-call | flops 97173635072 | bytes 160000000 | tf_op jit(solution)/shard_map/backward/pallas_call | solution.py:447
  469.3 4.0 all-to-all-start.7
  476.6 1.3 copy.98.code
  478.6 5.6 %put_rows.1.refs_1_ = f32[1572,4,1024]{2,1,0:T(4,128)} custom-call(s32[3]{0:T(128)} %pad_add_fusion.numbers, s32[256]{0:T(256)} %select_reduce_fusion.3.row_of, f32[4,448,1024]{2,1,0:T(8,128)} %get-tuple-element.490.sums, f32[32,272,1024]{2,1,0:T(8,128)} %get-tuple-element.491.freq.raw, ...), custom_call_target="tpu_custom_call", output_to_operand_aliasing={{}: (4, {})} | custom-call | tf_op jit(solution)/shard_map/put_rows/pallas_call | solution.py:749
  484.2 35.3 %hot_out.1.refs_2_ = f32[4,2048,1024]{2,1,0:T(8,128)} custom-call(s32[4]{0:T(128)} %convert_element_type.476.any_freq, f32[32,272,1024]{2,1,0:T(8,128)} %get-tuple-element.491.freq.raw, f32[32,272,1024]{2,1,0:T(8,128)} %get-tuple-element.491.freq.raw, s32[2048,1]{1,0:T(8,128)} %copy.98.code), custom_call_target="tpu_custom_call" | custom-call | flops 4563402752 | bytes 160000000 | tf_op jit(solution)/shard_map/hot_out/pallas_call | solution.py:700
  519.5 2.4 all-to-all-done.7
  522.0 5.4 %fusion.209.refs_0_ = bf16[1024,1024]{1,0:T(8,128)(2,1)} fusion(bf16[1024,1024]{1,0:T(8,128)(2,1)} %bitcast.30, s32[1024]{0:T(1024)S(1)} %copy-done.23), kind=kOutput, calls=%fused_computation.257 | convolution fusion | flops 2149580800 | bytes 4198400 | tf_op jit(solution)/shard_map/dot_general | solution.py:50
  527.4 1.3 conditional.1
  (110 shorter events, 13.2 us)
Async XLA Ops:
  8.6 15.5 %all-to-all-start.3 = ((s32[32,1,1024]{2,1,0:T(1,128)}), s32[32,1,1024]{2,1,0:T(1,128)S(1)}, u32[]{:S(2)}, u32[]{:S(2)}) async-start(s32[32,1,1024]{2,1,0:T(1,128)} %broadcast_in_dim.283), calls=%async_computation.3 | async-start | bytes 262144 | tf_op jit(solution)/shard_map/all_to_all | solution.py:38
  18.7 19.1 %copy-start.26 = (f32[27]{0:T(128)S(1)}, f32[27]{0:T(128)}, u32[]{:S(2)}) copy-start(f32[27]{0:T(128)} %constant.386.clone) | copy-start | bytes 328
  39.9 3.4 copy-start.12
  46.7 15.2 %all-to-all-start.4 = ((bf16[32,4,1024]{2,1,0:T(4,128)(2,1)}), bf16[32,4,1024]{2,1,0:T(4,128)(2,1)S(1)}, u32[]{:S(2)}, u32[]{:S(2)}) async-start(bf16[32,4,1024]{2,1,0:T(4,128)(2,1)} %broadcast_in_dim.298), calls=%async_computation.4 | async-start | bytes 524288 | tf_op jit(solution)/shard_map/all_to_all | solution.py:38
  52.5 16.0 %copy-start.22 = (s32[1024]{0:T(1024)}, s32[1024]{0:T(1024)S(1)}, u32[]{:S(2)}) copy-start(s32[1024]{0:T(1024)S(1)} %fusion.284) | copy-start | bytes 12292
  55.8 51.8 %copy-start.19 = (pred[1572]{0:T(1024)(128)(4,1)}, pred[1572]{0:T(1024)(128)(4,1)S(1)}, u32[]{:S(2)}) copy-start(pred[1572]{0:T(1024)(128)(4,1)S(1)} %get-tuple-element.477) | copy-start | bytes 4720
  56.5 12.1 %copy-start = (bf16[1024,1024]{1,0:T(8,128)(2,1)S(1)}, bf16[1024,1024]{1,0:T(8,128)(2,1)}, u32[]{:S(2)}) copy-start(bf16[1024,1024]{1,0:T(8,128)(2,1)} %param.20) | copy-start | bytes 6291460
  62.6 13.1 %all-to-all-start.5 = ((s32[32,1,32]{2,1,0:T(1,128)}), s32[32,1,32]{2,1,0:T(1,128)S(1)}, u32[]{:S(2)}, u32[]{:S(2)}) async-start(s32[32,1,32]{2,1,0:T(1,128)} %all_to_all.42), calls=%async_computation.5 | async-start | bytes 32768 | tf_op jit(solution)/shard_map/all_to_all | solution.py:38
  68.5 8.4 %copy-start.6 = (bf16[2048,200]{1,0:T(8,128)(2,1)S(1)}, bf16[2048,200]{1,0:T(8,128)(2,1)}, u32[]{:S(2)}) copy-start(bf16[2048,200]{1,0:T(8,128)(2,1)} %fusion.206) | copy-start | bytes 2457604
  84.3 18.8 %copy-start.2 = (bf16[188,1024]{1,0:T(8,128)(2,1)}, bf16[188,1024]{1,0:T(8,128)(2,1)S(1)}, u32[]{:S(2)}) copy-start(bf16[188,1024]{1,0:T(8,128)(2,1)S(1)} %fusion.228) | copy-start | bytes 1155076
  89.3 13.8 %copy-start.4 = (bf16[188,1024]{1,0:T(8,128)(2,1)}, bf16[188,1024]{1,0:T(8,128)(2,1)S(1)}, u32[]{:S(2)}) copy-start(bf16[188,1024]{1,0:T(8,128)(2,1)S(1)} %fusion.225) | copy-start | bytes 1155076
  94.4 8.8 %copy-start.3 = (bf16[188,1024]{1,0:T(8,128)(2,1)}, bf16[188,1024]{1,0:T(8,128)(2,1)S(1)}, u32[]{:S(2)}) copy-start(bf16[188,1024]{1,0:T(8,128)(2,1)S(1)} %fusion.222) | copy-start | bytes 1155076
  94.4 52.5 %all-to-all-start.6 = ((bf16[32,32,1024]{2,1,0:T(8,128)(2,1)}), bf16[32,32,1024]{2,1,0:T(8,128)(2,1)}, u32[]{:S(2)}, u32[]{:S(2)}) async-start(bf16[32,32,1024]{2,1,0:T(8,128)(2,1)} %bitcast.8), calls=%async_computation.6 | async-start | bytes 4194304 | tf_op jit(solution)/shard_map/all_to_all | solution.py:38
  103.0 0.8 copy-start.5
  106.2 11.2 %copy-start.21 = (s32[1024]{0:T(1024)}, s32[1024]{0:T(1024)S(1)}, u32[]{:S(2)}) copy-start(s32[1024]{0:T(1024)S(1)} %get-tuple-element.806) | copy-start | bytes 12292
  125.3 1.0 copy-start.11
  125.3 1.1 slice-start.3
  125.3 1.4 slice-start.2
  125.5 1.5 slice-start.1
  125.7 1.6 slice-start
  469.3 4.6 copy-start.20
  469.3 6.6 %copy-start.25 = (pred[2048]{0:T(1024)(128)(4,1)S(1)}, pred[2048]{0:T(1024)(128)(4,1)}, u32[]{:S(2)}) copy-start(pred[2048]{0:T(1024)(128)(4,1)} %get-tuple-element.770) | copy-start | bytes 6148
  469.3 7.3 %copy-start.18 = (s32[2048]{0:T(1024)S(1)}, s32[2048]{0:T(1024)}, u32[]{:S(2)}) copy-start(s32[2048]{0:T(1024)} %get-tuple-element.771) | copy-start | bytes 24580
  469.3 52.7 %all-to-all-start.7 = ((bf16[32,32,1024]{2,1,0:T(8,128)(2,1)}), bf16[32,32,1024]{2,1,0:T(8,128)(2,1)}, u32[]{:S(2)}, u32[]{:S(2)}) async-start(bf16[32,32,1024]{2,1,0:T(8,128)(2,1)} %bitcast.313), calls=%async_computation.7 | async-start | bytes 4194304 | tf_op jit(solution)/shard_map/all_to_all | solution.py:38
  484.2 37.8 %copy-start.23 = (s32[1024]{0:T(1024)S(1)}, s32[1024]{0:T(1024)}, u32[]{:S(2)}) copy-start(s32[1024]{0:T(1024)} %copy-done.22) | copy-start | bytes 12292
  522.0 5.5 %copy-start.1 = (bf16[1024,1024]{1,0:T(8,128)(2,1)S(1)}, bf16[1024,1024]{1,0:T(8,128)(2,1)}, u32[]{:S(2)}) copy-start(bf16[1024,1024]{1,0:T(8,128)(2,1)} %param.20) | copy-start | bytes 6291460
  522.0 5.5 %copy-start.13 = (s32[1024]{0:T(1024)S(1)}, s32[1024]{0:T(1024)}, u32[]{:S(2)}) copy-start(s32[1024]{0:T(1024)} %param.18) | copy-start | bytes 12292
  522.0 5.5 %copy-start.24 = (s32[2048]{0:T(1024)S(1)}, s32[2048]{0:T(1024)}, u32[]{:S(2)}) copy-start(s32[2048]{0:T(1024)} %param.19) | copy-start | bytes 24580

commit v7 on v6

--- a/solution.py
+++ b/solution.py
@@ -366,7 +366,7 @@
 
     @pl.when(f == 0)
     def _():
-        for c in load(layer, early):
+        for c in load(layer, early[:3]):
             c.wait()
         for c in load(layer, late):
             c.start()
@@ -382,6 +382,11 @@
         point(0, 0, n_l)
         class_sums(cls_t, three, sums.at[step // n_f])
         point(1, 0, n_l)
+
+    @pl.when(f == 0)
+    def _():
+        for c in load(layer, early[3:]):
+            c.wait()
 
     @pl.when((f == 0) & (step < n_full))
     def _():
@@ -672,6 +677,21 @@
 ORDER = [(b & 3) * 8 + (b >> 2 & 1) * 4 + (b >> 3 & 1) * 2 + (b >> 4) for b in range(FREQ // RUN)]
 
 
+def pick_kernel(pick, table, out):
+    out[...] = dot32(pick[...], table[...]).astype(BF)
+
+
+def pick_rows(pick, table):
+    n_l, n, emb = table.shape
+    return pl.pallas_call(
+        pick_kernel, grid=(n_l,),
+        in_specs=[spec(pick.shape, pipeline_mode=ONCE), pl.BlockSpec((None, n, emb), lambda l: (l, 0, 0))],
+        out_specs=pl.BlockSpec((None, len(pick), emb), lambda l: (l, 0, 0)),
+        out_shape=out_of((n_l, len(pick), emb), BF), compiler_params=params("arbitrary"),
+        cost_estimate=cost(len(pick) * table.size, n_l), name="pick_rows",
+    )(pick, table)
+
+
 def hot_kernel(any_freq, raw, freq, code, out, parts):
     n_dev, n_r, _ = raw.shape
     layer, block = pl.program_id(0), pl.program_id(1)
@@ -692,10 +712,10 @@
         out[...] += dot32(sel, parts[0]) + (dot32(sel, parts[1]) + dot32(sel, parts[2]))
 
 
-def hot_out(gathered, code, n_l):
+def hot_out(gathered, code, any_freq, n_l):
     n_dev, n_rows, emb = gathered.shape
-    n_r = 4 * RUN
-    width = n_r * n_dev
+    width = len(code) // len(any_freq)
+    n_r = width // n_dev
     blocks = len(code) // width
     return pl.pallas_call(
         hot_kernel,
@@ -711,7 +731,7 @@
         out_shape=out_of((n_l, len(code), emb)),
         compiler_params=params("arbitrary", "arbitrary"),
         cost_estimate=cost(gathered.size * LO, n_l), name="hot_out",
-    )((code.reshape(blocks, width) >= 0).any(axis=1).astype(I32), gathered, gathered, code.reshape(-1, 1))
+    )(any_freq, gathered, gathered, code)
 
 
 def rows_kernel(numbers, row_of, sums, freq, into, out, stage, got, sem):
@@ -850,18 +870,20 @@
             row_of = row_sum(jnp.where(at_rank, iota((COLD_MAX, rows_dev), 1), 0))
             packed = pack_rows(row_of, by_row)
             mine_no = jnp.where(hot_owner == me, FREQ_HOT + hot_place, -1)
-            hot_pick = (one_hot(hot_f - 1, FREQ_HOT + hot_dev) * col((hot_f <= FREQ_HOT).astype(BF)) + one_hot(mine_no, FREQ_HOT + hot_dev)).T
-            hot_rows = [dot32(hot_pick, hot_table[i]).astype(BF) for i in range(layers)]
+            wanted = jnp.where(hot_f <= FREQ_HOT, hot_f - 1, -1)
+            pick_no = iota((FREQ + hot_dev, n_hot), 0)
+            hot_rows = pick_rows(((row(wanted) == pick_no) | (row(mine_no) == pick_no)).astype(BF), hot_table)
             table = jnp.stack([jnp.concatenate([
-                hot_rows[i][:FREQ_HOT], dot32(one_hot(cold_owner, n_dev), freq_cold[:, i]).astype(BF),
-                hot_rows[i][FREQ_HOT:], packed[:, i]]) for i in range(layers)])
+                hot_rows[i, :FREQ_HOT], dot32(one_hot(cold_owner, n_dev), freq_cold[:, i]).astype(BF),
+                hot_rows[i, FREQ_HOT:FREQ_HOT + hot_dev], packed[:, i]]) for i in range(layers)])
             n_used = jnp.minimum(jnp.sum(row_used.astype(I32)), COLD_MAX)
             row_no = got_class - cold_at
             used_before = row_sum(jnp.where(row(row_used) & (iota((n_loc, rows_dev), 1) < col(row_no)), 1, 0))
             cls = jnp.where(row_no >= 0, cold_at + used_before, got_class)
-            code = jnp.where(hot_f <= FREQ_HOT, hot_f - 1, -1)
+            any_freq = (wanted.reshape(-1, 4 * RUN * n_dev) >= 0).any(axis=1).astype(I32)
+            numbers = jnp.stack([n_used, my_row, jnp.minimum(jnp.sum(my_cold * jnp.arange(FREQ_COLD, dtype=I32)), FREQ_COLD - 1)])
             d_placed = dot32(move, d_out).astype(BF)
-            return d_placed, table, cls, n_used, row_of, code
+            return d_placed, table, cls, numbers, row_of, wanted.reshape(-1, 1), any_freq
 
         count, zeros = count_ids(swap(jnp.broadcast_to(row(token_ids), (n_dev, n_loc))), n_hi, (rows_dev, layers, emb_dim))
         tok, hot = digits(token_ids, n_hi), digits(hot_ids, n_hi)
@@ -915,15 +937,14 @@
         given = prepare(got_class, hot_hi, hot_lo, row_used, cold_owner, freq_cold, freq_map, hot_table, by_row, move, d_out)
         all_fit = jnp.max(got_class) < bad
 
-        d_placed, table, cls, n_used, row_of, code = given
+        x_moved, d_placed, table, cls, numbers, row_of, code, any_freq = lax.optimization_barrier((x_moved, *given))
         cls_row = cls.reshape(1, n_loc)
         xs, hs, ss, es, x_last, d_moved = forward(x_moved, cls.reshape(n_loc, 1), table, w_up, w_down, w_gate, w_proj, d_placed, n_dev)
         sums, gathered = backward(d_moved, cls_row, es, xs, hs, ss, w_up, w_down, w_gate, w_proj, n_dev)
         x_last, gathered = lax.optimization_barrier((x_last, gathered))
         x_back = exchange(x_last)
-        numbers = jnp.stack([n_used, my_row, jnp.minimum(jnp.sum(my_cold * jnp.arange(FREQ_COLD, dtype=I32)), FREQ_COLD - 1)])
         d_table = put_rows(numbers, row_of, sums, gathered, zeros)
-        d_hot = hot_out(gathered, code, layers)
+        d_hot = hot_out(gathered, code, any_freq, layers)
         x_out = dot32((col(slot) == iota((n_loc, n_loc), 1)).astype(BF), x_back).astype(BF)
         *fast, fit = lax.optimization_barrier((x_out, d_table, d_hot, all_fit))
 

time: 542 us -> 531 us (0.980)
  matrix products: 42.2 us -> 22.2 us
  waiting for transfers between devices: 25.9 us -> 17.6 us
  Pallas kernels: 382 us -> 390 us
  local copies, waits for them, and re-layouts: 17.5 us -> 23.7 us
    dot_general x19 -> x15, matrix products: 42.2 us -> 22.2 us  [dot32(): return jnp.dot(a, b, preferred_element_type=F32)]
    pallas_call x0 -> x1, Pallas kernels: none -> 9.06 us  [pick_rows(): pl.pallas_call(pick_kernel, grid=(n_l,), in_specs=[spec(pick.shape, pipel...]
    all_to_all x5, waiting for transfers between devices: 25.9 us -> 17.6 us  [swap(): return lax.all_to_all(v, 'emb', 0, 0, tiled=True)]
  transfers between devices with their start and end apart: 5 -> 5, of which waited for: 4 -> 4; matrix products, arithmetic and copies ran while one was open for 8% -> 9% of each run, Pallas kernels for 9% -> 11%
where the time goes in v7:
time: 531 us; the launch traced here: 524 us
  Pallas kernels  390 us (73%)
  other arithmetic  25.5 us (5%)
  starting transfers between devices  24.5 us (5%)
  local copies, waits for them, and re-layouts  23.7 us (4%)
  matrix products  22.2 us (4%)
  between operations  19.1 us (4%)
  waiting for transfers between devices  17.6 us (3%)
    pallas_call x1, Pallas kernels, backward(): pl.pallas_call(functools.partial(backward_kernel, n_l, n_f), grid=(n_full...  202 us
    pallas_call x1, Pallas kernels, forward(): pl.pallas_call(functools.partial(forward_kernel, n_l, n_f, n_dev), grid=(...  119 us
    pallas_call x1, Pallas kernels, hot_out(): pl.pallas_call(hot_kernel, grid_spec=pltpu.PrefetchScalarGridSpec(num_sca...  35.3 us
    all_to_all x5, starting transfers between devices, swap(): return lax.all_to_all(v, 'emb', 0, 0, tiled=True)  24.5 us
    dot_general x15, matrix products, dot32(): return jnp.dot(a, b, preferred_element_type=F32)  22.2 us
    all_to_all x5, waiting for transfers between devices, swap(): return lax.all_to_all(v, 'emb', 0, 0, tiled=True)  17.6 us
  transfers between devices with their start and end apart: 5, of which 4 were waited for; matrix products, arithmetic and copies ran while one was open for 9% of the time, Pallas kernels for 11%

profile of v7, /device:TPU:0, one launch (start us, length us, event | category | flops | bytes accessed | tf_op | source)
XLA Modules:
  0.0 524.2 jit_solution(10269201409977879908)
XLA Ops:
  7.2 1.4 broadcast_in_dim.282
  8.6 7.3 %all-to-all-start.3 = ((s32[32,1,1024]{2,1,0:T(1,128)}), s32[32,1,1024]{2,1,0:T(1,128)S(1)}, u32[]{:S(2)}, u32[]{:S(2)}) async-start(s32[32,1,1024]{2,1,0:T(1,128)} %broadcast_in_dim.282), calls=%async_computation.3 | async-start | bytes 262144 | tf_op jit(solution)/shard_map/all_to_all | solution.py:38
  17.4 1.3 fusion.194
  18.7 1.2 fusion.191
  19.9 0.9 convolution_convert_fusion
  20.9 3.2 all-to-all-done.3
  24.8 10.3 %count_ids.1 = (f32[200,256]{1,0:T(8,128)}, f32[1572,4,1024]{2,1,0:T(4,128)}) custom-call(s32[32,1024]{1,0:T(8,128)} %bitcast.314), custom_call_target="tpu_custom_call" | custom-call | tf_op jit(solution)/shard_map/count_ids/pallas_call | solution.py:495
  35.1 1.0 compare_convert_fusion.4
  36.0 1.8 broadcast_select_fusion.3
  37.8 1.4 convert_reduce_fusion
  39.9 1.5 convert_reduce_fusion.2
  42.1 0.8 fusion.218
  45.8 0.8 broadcast_in_dim.297
  46.6 3.1 all-to-all-start.4
  53.0 0.9 fusion.201
  53.9 1.2 fusion.200
  56.3 5.4 %fusion.197.d_in = bf16[1024,1024]{1,0:T(8,128)(2,1)} fusion(bf16[1024,1024]{1,0:T(8,128)(2,1)} %param.21, s32[1024]{0:T(1024)S(1)} %fusion.239), kind=kOutput, calls=%fused_computation.243 | convolution fusion | flops 2149580800 | bytes 4198400 | tf_op jit(solution)/shard_map/dot_general | solution.py:50
  62.4 5.9 %all-to-all-start.5 = ((s32[32,1,32]{2,1,0:T(1,128)}), s32[32,1,32]{2,1,0:T(1,128)S(1)}, u32[]{:S(2)}, u32[]{:S(2)}) async-start(s32[32,1,32]{2,1,0:T(1,128)} %all_to_all.42), calls=%async_computation.5 | async-start | bytes 32768 | tf_op jit(solution)/shard_map/all_to_all | solution.py:38
  68.4 3.7 fusion.196
  72.7 0.8 copy.89
  73.5 2.1 all-to-all-done.5
  78.2 1.7 fusion.206
  80.3 1.6 select_reduce_fusion.3.row_of
  81.9 4.1 all-to-all-start.6
  86.0 8.2 %pack_rows.1 = bf16[256,4,1024]{2,1,0:T(4,128)(2,1)} custom-call(s32[256]{0:T(256)} %select_reduce_fusion.3.row_of, bf16[1572,4,1024]{2,1,0:T(4,128)(2,1)} %bitcast.304), custom_call_target="tpu_custom_call" | custom-call | tf_op jit(solution)/shard_map/pack_rows/pallas_call | solution.py:511
  94.2 8.6 %fusion.277 = (bf16[256,1,1024]{2,1,0:T(2,128)(2,1)}, bf16[256,1,1024]{2,1,0:T(2,128)(2,1)S(1)}, bf16[256,1,1024]{2,1,0:T(2,128)(2,1)S(1)}, bf16[256,1,1024]{2,1,0:T(2,128)(2,1)S(1)}) fusion(bf16[256,4,1024]{2,1,0:T(4,128)(2,1)} %pack_rows.1), kind=kLoop, calls=%fused_computation.426 | loop fusion | bytes 4194304 | tf_op jit(solution)/shard_map/slice | solution.py:878
  104.1 2.2 copy.129
  106.3 1.0 copy.127
  107.3 1.0 copy.128
  108.7 1.3 fusion.205.pick
  110.0 9.1 %pick_rows.1 = bf16[4,192,1024]{2,1,0:T(8,128)(2,1)} custom-call(bf16[192,2048]{1,0:T(8,128)(2,1)} %fusion.205.pick, bf16[4,2048,1024]{2,1,0:T(8,128)(2,1)} %table.1), custom_call_target="tpu_custom_call" | custom-call | flops 3221225472 | bytes 160000000 | tf_op jit(solution)/shard_map/pick_rows/pallas_call | solution.py:686
  119.1 1.3 slice_bitcast_fusion.7
  120.4 1.3 slice_bitcast_fusion.3
  121.7 1.1 maximum_bitcast_fusion
  123.7 1.7 select_reduce_fusion.1
  125.4 0.7 fusion.278
  126.1 2.1 pad_maximum_fusion.table
  128.2 6.5 %all-to-all-done.6 = bf16[32,32,1024]{2,1,0:T(8,128)(2,1)} async-done(((bf16[32,32,1024]{2,1,0:T(8,128)(2,1)}), bf16[32,32,1024]{2,1,0:T(8,128)(2,1)}, u32[]{:S(2)}, u32[]{:S(2)}) %all-to-all-start.6) | async-done | bytes 2097184 | tf_op jit(solution)/shard_map/all_to_all | solution.py:38
  134.7 1.0 copy.97.cls
  135.7 119.4 %forward.1 = (bf16[4,1024,1024]{2,1,0:T(8,128)(2,1)}, bf16[4,1024,4096]{2,1,0:T(8,128)(2,1)}, bf16[4,1024,1024]{2,1,0:T(8,128)(2,1)}, bf16[4,1024,1024]{2,1,0:T(...) custom-call(bf16[1024,1024]{1,0:T(8,128)(2,1)} %bitcast.9.x0, s32[1024,1]{1,0:T(8,128)} %copy.97.cls, ...), custom_call_target="tpu_custom_call" | custom-call | flops 89657442304 | bytes 160000000 | tf_op jit(solution)/shard_map/forward/pallas_call | solution.py:260
  255.2 202.4 %backward.1 = (f32[4,448,1024]{2,1,0:T(8,128)}, f32[32,272,1024]{2,1,0:T(8,128)}) custom-call(bf16[1024,1024]{1,0:T(8,128)(2,1)} %get-tuple-element.495.r_in, bf16[4,1024,1024]{2,1,0:T(8,128)(2,1)} %get-tuple-element.496.ss, bf16[4,1024,1024]{2,1,0:T(8,128)(2,1)} %wp.3, bf16[4,1024,1024]{2,1,0:T(8,128)(2,1)} %get-tuple-element.497.es, ...), custom_call_target="tpu_custom_call" | custom-call | flops 97173635072 | bytes 160000000 | tf_op jit(solution)/shard_map/backward/pallas_call | solution.py:452
  457.6 4.0 all-to-all-start.7
  462.4 1.3 copy.98.code
  463.7 5.6 %put_rows.1.refs_1_ = f32[1572,4,1024]{2,1,0:T(4,128)} custom-call(s32[3]{0:T(128)} %pad_add_fusion.numbers, s32[256]{0:T(256)} %select_reduce_fusion.3.row_of, f32[4,448,1024]{2,1,0:T(8,128)} %get-tuple-element.504.sums, f32[32,272,1024]{2,1,0:T(8,128)} %get-tuple-element.505.freq.raw, ...), custom_call_target="tpu_custom_call", output_to_operand_aliasing={{}: (4, {})} | custom-call | tf_op jit(solution)/shard_map/put_rows/pallas_call | solution.py:769
  469.3 35.3 %hot_out.1.refs_2_ = f32[4,2048,1024]{2,1,0:T(8,128)} custom-call(s32[4]{0:T(128)} %convert_element_type.448.any_freq, f32[32,272,1024]{2,1,0:T(8,128)} %get-tuple-element.505.freq.raw, f32[32,272,1024]{2,1,0:T(8,128)} %get-tuple-element.505.freq.raw, s32[2048,1]{1,0:T(8,128)} %copy.98.code), custom_call_target="tpu_custom_call" | custom-call | flops 4563402752 | bytes 160000000 | tf_op jit(solution)/shard_map/hot_out/pallas_call | solution.py:720
  504.7 5.7 %all-to-all-done.7 = bf16[32,32,1024]{2,1,0:T(8,128)(2,1)} async-done(((bf16[32,32,1024]{2,1,0:T(8,128)(2,1)}), bf16[32,32,1024]{2,1,0:T(8,128)(2,1)}, u32[]{:S(2)}, u32[]{:S(2)}) %all-to-all-start.7) | async-done | bytes 2097184 | tf_op jit(solution)/shard_map/all_to_all | solution.py:38
  510.4 5.4 %fusion.195.refs_0_ = bf16[1024,1024]{1,0:T(8,128)(2,1)} fusion(bf16[1024,1024]{1,0:T(8,128)(2,1)} %bitcast.38, s32[1024]{0:T(1024)S(1)} %copy-done.20), kind=kOutput, calls=%fused_computation.241 | convolution fusion | flops 2149580800 | bytes 4198400 | tf_op jit(solution)/shard_map/dot_general | solution.py:50
  515.8 1.3 conditional.1
  (89 shorter events, 14.1 us)
Async XLA Ops:
  8.6 15.5 %all-to-all-start.3 = ((s32[32,1,1024]{2,1,0:T(1,128)}), s32[32,1,1024]{2,1,0:T(1,128)S(1)}, u32[]{:S(2)}, u32[]{:S(2)}) async-start(s32[32,1,1024]{2,1,0:T(1,128)} %broadcast_in_dim.282), calls=%async_computation.3 | async-start | bytes 262144 | tf_op jit(solution)/shard_map/all_to_all | solution.py:38
  18.7 19.1 %copy-start.22 = (f32[27]{0:T(128)S(1)}, f32[27]{0:T(128)}, u32[]{:S(2)}) copy-start(f32[27]{0:T(128)} %constant.390.clone) | copy-start | bytes 328
  39.9 3.4 copy-start.10
  46.6 15.1 %all-to-all-start.4 = ((bf16[32,4,1024]{2,1,0:T(4,128)(2,1)}), bf16[32,4,1024]{2,1,0:T(4,128)(2,1)S(1)}, u32[]{:S(2)}, u32[]{:S(2)}) async-start(bf16[32,4,1024]{2,1,0:T(4,128)(2,1)} %broadcast_in_dim.297), calls=%async_computation.4 | async-start | bytes 524288 | tf_op jit(solution)/shard_map/all_to_all | solution.py:38
  52.5 15.8 %copy-start.19 = (s32[1024]{0:T(1024)}, s32[1024]{0:T(1024)S(1)}, u32[]{:S(2)}) copy-start(s32[1024]{0:T(1024)S(1)} %fusion.239) | copy-start | bytes 12292
  56.3 12.1 %copy-start.2 = (bf16[1024,1024]{1,0:T(8,128)(2,1)S(1)}, bf16[1024,1024]{1,0:T(8,128)(2,1)}, u32[]{:S(2)}) copy-start(bf16[1024,1024]{1,0:T(8,128)(2,1)} %param.20) | copy-start | bytes 6291460
  62.4 13.1 %all-to-all-start.5 = ((s32[32,1,32]{2,1,0:T(1,128)}), s32[32,1,32]{2,1,0:T(1,128)S(1)}, u32[]{:S(2)}, u32[]{:S(2)}) async-start(s32[32,1,32]{2,1,0:T(1,128)} %all_to_all.42), calls=%async_computation.5 | async-start | bytes 32768 | tf_op jit(solution)/shard_map/all_to_all | solution.py:38
  68.4 9.8 %copy-start.4 = (bf16[2048,200]{1,0:T(8,128)(2,1)S(1)}, bf16[2048,200]{1,0:T(8,128)(2,1)}, u32[]{:S(2)}) copy-start(bf16[2048,200]{1,0:T(8,128)(2,1)} %fusion.194) | copy-start | bytes 2457604
  81.9 52.8 %all-to-all-start.6 = ((bf16[32,32,1024]{2,1,0:T(8,128)(2,1)}), bf16[32,32,1024]{2,1,0:T(8,128)(2,1)}, u32[]{:S(2)}, u32[]{:S(2)}) async-start(bf16[32,32,1024]{2,1,0:T(8,128)(2,1)} %bitcast.309), calls=%async_computation.6 | async-start | bytes 4194304 | tf_op jit(solution)/shard_map/all_to_all | solution.py:38
  102.8 5.7 %copy-start.9 = (bf16[32,4,1024]{2,0,1:T(8,128)(2,1)S(1)}, bf16[32,4,1024]{2,0,1:T(8,128)(2,1)}, u32[]{:S(2)}) copy-start(bf16[32,4,1024]{2,0,1:T(8,128)(2,1)} %copy.89) | copy-start | bytes 786436
  108.5 10.6 %copy-start.14 = (s32[2048]{0:T(1024)}, s32[2048]{0:T(1024)S(1)}, u32[]{:S(2)}) copy-start(s32[2048]{0:T(1024)S(1)} %add_select_fusion.6) | copy-start | bytes 24580
  119.1 4.0 copy-start.1
  119.1 4.2 copy-start
  126.1 129.1 %copy-start.18 = (s32[1024]{0:T(1024)}, s32[1024]{0:T(1024)S(1)}, u32[]{:S(2)}) copy-start(s32[1024]{0:T(1024)S(1)} %get-tuple-element.491) | copy-start | bytes 12292
  457.6 4.7 copy-start.15
  457.6 52.8 %all-to-all-start.7 = ((bf16[32,32,1024]{2,1,0:T(8,128)(2,1)}), bf16[32,32,1024]{2,1,0:T(8,128)(2,1)}, u32[]{:S(2)}, u32[]{:S(2)}) async-start(bf16[32,32,1024]{2,1,0:T(8,128)(2,1)} %bitcast.310), calls=%async_computation.7 | async-start | bytes 4194304 | tf_op jit(solution)/shard_map/all_to_all | solution.py:38
  469.3 41.0 %copy-start.20 = (s32[1024]{0:T(1024)S(1)}, s32[1024]{0:T(1024)}, u32[]{:S(2)}) copy-start(s32[1024]{0:T(1024)} %copy-done.19) | copy-start | bytes 12292
  510.4 5.4 %copy-start.3 = (bf16[1024,1024]{1,0:T(8,128)(2,1)S(1)}, bf16[1024,1024]{1,0:T(8,128)(2,1)}, u32[]{:S(2)}) copy-start(bf16[1024,1024]{1,0:T(8,128)(2,1)} %param.20) | copy-start | bytes 6291460
  510.4 5.5 %copy-start.11 = (s32[1024]{0:T(1024)S(1)}, s32[1024]{0:T(1024)}, u32[]{:S(2)}) copy-start(s32[1024]{0:T(1024)} %param.18) | copy-start | bytes 12292
  510.4 5.5 %copy-start.21 = (s32[2048]{0:T(1024)S(1)}, s32[2048]{0:T(1024)}, u32[]{:S(2)}) copy-start(s32[2048]{0:T(1024)} %param.19) | copy-start | bytes 24580
